TPU v7x, 32 devices: a whole 2x2x4 slice. The times are simulated.
32 devices in a mesh: gx: 4 (over z), gy: 4 (over x, core), gz: 2 (over y).
Axes of the slice: x: 2, y: 2, z: 4, core: 2. Of those that a mesh axis runs over, the one named last changes fastest.
Arguments:
- x_a: bfloat16 [32, 8, 64, 256], P(None, 'gx', 'gy', 'gz'), may hold values from -12 to 12
- x_b: bfloat16 [32, 8, 64, 256], P(None, 'gx', 'gy', 'gz'), may hold values from -12 to 12
- w_first: bfloat16 [3, 3, 3, 32, 32], replicated, may hold values from -0.21875 to 0.21875
- w_second: bfloat16 [3, 3, 3, 32, 32], replicated, may hold values from -0.21875 to 0.21875
- gain_first: float32 [32], replicated, may hold values from 0.1 to 1.9
- bias_first: float32 [32], replicated, may hold values from -2 to 2
- gain_second: float32 [32], replicated, may hold values from 0.1 to 1.9
- bias_second: float32 [32], replicated, may hold values from -2 to 2
- grad_out: bfloat16 [32, 8, 64, 256], P(None, 'gx', 'gy', 'gz'), may hold values from -6 to 6
Outputs:
- y_a: bfloat16 [32, 8, 64, 256], P(None, 'gx', 'gy', 'gz')
- dx_b: bfloat16 [32, 8, 64, 256], P(None, 'gx', 'gy', 'gz')
- grad_w_first: float32 [3, 3, 3, 32, 32], replicated
- grad_w_second: float32 [3, 3, 3, 32, 32], replicated
- grad_norm: float32 [4, 32], replicated
All inputs are finite; a program needn't handle non-finite values.
Results may differ from a plain program's by a relative error of at most 0.0063.
Values may be sent and summed in bfloat16 or wider, within the bound.
No kernel may reach another device: no remote copies, remote signals or barrier semaphores. Data moves between devices by JAX's collectives and lax.ppermute only.
A program may use at most 128 MiB of HBM per device.

v0:
```python
import math

import jax
import jax.numpy as jnp
from jax import lax
from jax.sharding import PartitionSpec as P

EPSILON = 1e-05


def extended(block, sides, width):
    for axis, dim in sides:
        count = lax.axis_size(axis)
        forward = [(i, i + 1) for i in range(count - 1)]
        backward = [(target, source) for source, target in forward]
        low = lax.ppermute(
            lax.slice_in_dim(block, block.shape[dim] - width, None, axis=dim), axis, forward
        )
        high = lax.ppermute(lax.slice_in_dim(block, 0, width, axis=dim), axis, backward)
        block = jnp.concatenate([low, block, high], axis=dim)
    return block


def spread(values):
    return values[:, None, None, None]


def silu_slope(value):
    sigma = jax.nn.sigmoid(value)
    return sigma * (1.0 + value * (1.0 - sigma))


def convolve(padded, weight):
    in_chan = padded.shape[0]
    out_chan = weight.shape[3]
    span_x = padded.shape[1] - 2
    span_y = padded.shape[2] - 2
    span_z = padded.shape[3] - 2
    total = jnp.zeros((out_chan, span_x * span_y * span_z), jnp.float32)
    for shift_x in range(3):
        for shift_y in range(3):
            pieces = [
                padded[
                    :,
                    shift_x : shift_x + span_x,
                    shift_y : shift_y + span_y,
                    shift_z : shift_z + span_z,
                ]
                for shift_z in range(3)
            ]
            stacked = jnp.concatenate(pieces, axis=0).reshape(3 * in_chan, -1)
            matrix = weight[shift_x, shift_y].transpose(1, 0, 2).reshape(out_chan, 3 * in_chan)
            total = total + jnp.dot(matrix, stacked, preferred_element_type=jnp.float32)
    return total.reshape(out_chan, span_x, span_y, span_z)


def kernel_grad(padded, upstream):
    in_chan = padded.shape[0]
    out_chan = upstream.shape[0]
    span_x, span_y, span_z = (upstream.shape[1], upstream.shape[2], upstream.shape[3])
    flat = upstream.reshape(out_chan, -1)
    rows = []
    for shift_x in range(3):
        for shift_y in range(3):
            pieces = [
                padded[
                    :,
                    shift_x : shift_x + span_x,
                    shift_y : shift_y + span_y,
                    shift_z : shift_z + span_z,
                ]
                for shift_z in range(3)
            ]
            stacked = jnp.concatenate(pieces, axis=0).reshape(3 * in_chan, -1)
            product = lax.dot_general(
                flat, stacked, (((1,), (1,)), ((), ())), preferred_element_type=jnp.float32
            )
            rows.append(product.reshape(out_chan, 3, in_chan).transpose(1, 0, 2))
    return jnp.stack(rows).reshape(3, 3, 3, out_chan, in_chan)


def flipped(weight):
    return jnp.flip(weight, (0, 1, 2)).transpose(0, 1, 2, 4, 3)


def statistics(blocks, voxels):
    local_sums = jnp.stack([jnp.sum(block, axis=(1, 2, 3)) for block in blocks])
    local_squares = jnp.stack([jnp.sum(jnp.square(block), axis=(1, 2, 3)) for block in blocks])
    sums, squares = lax.psum((local_sums, local_squares), ("gx", "gy", "gz"))
    means = sums / voxels
    variance = squares / voxels - means * means
    return (means, lax.rsqrt(variance + EPSILON))


def normalize(block, means, scales, gain, bias):
    normed = (block - spread(means)) * spread(scales)
    return (normed, spread(gain) * normed + spread(bias))


def backward_layer(upstream, preact, normed, scales, gain, voxels):
    slope = upstream * silu_slope(preact)
    sum_d, sum_dx = lax.psum(
        (jnp.sum(slope, axis=(1, 2, 3)), jnp.sum(slope * normed, axis=(1, 2, 3))),
        ("gx", "gy", "gz"),
    )
    delta = spread(gain * scales) * (
        slope - spread(sum_d / voxels) - normed * spread(sum_dx / voxels)
    )
    return (delta.astype(jnp.bfloat16), sum_d, sum_dx)


def body(x_a, x_b, w_first, w_second, gain_first, bias_first, gain_second, bias_second, grad_out):
    rows_x, rows_y, rows_z = (x_a.shape[1], x_a.shape[2], x_a.shape[3])
    voxels = float(
        rows_x * rows_y * rows_z * lax.axis_size("gx") * lax.axis_size("gy") * lax.axis_size("gz")
    )
    factor = 1.0 / math.sqrt(voxels)
    volumes = jnp.stack([x_a, x_b])
    padded = extended(volumes, (("gx", 2), ("gy", 3), ("gz", 4)), 1)
    first = [convolve(padded[member], w_first) for member in range(2)]
    means, scales = statistics(first, voxels)
    hidden = []
    for member in range(2):
        normed, preact = normalize(
            first[member], means[member], scales[member], gain_first, bias_first
        )
        hidden.append((preact * jax.nn.sigmoid(preact)).astype(jnp.bfloat16))
    hidden_all = extended(jnp.stack(hidden), (("gx", 2), ("gy", 3), ("gz", 4)), 1)
    hidden_pads = [hidden_all[0], hidden_all[1]]
    input_pad_b = padded[1]
    scale_one = scales[1]
    second = [convolve(hidden_pads[member], w_second) for member in range(2)]
    means_two, scales_two = statistics(second, voxels)
    normed_a, preact_a = normalize(second[0], means_two[0], scales_two[0], gain_second, bias_second)
    y_a = (preact_a * jax.nn.sigmoid(preact_a)).astype(jnp.bfloat16)
    norm_two, pre_two = normalize(second[1], means_two[1], scales_two[1], gain_second, bias_second)
    delta_two, sum_d2, sum_x2 = backward_layer(
        grad_out.astype(jnp.float32), pre_two, norm_two, scales_two[1], gain_second, voxels
    )
    local_second = kernel_grad(hidden_pads[1], delta_two) * factor
    grad_w_second = lax.psum(local_second, ("gx", "gy", "gz"))
    delta_pad_two = extended(delta_two, (("gx", 1), ("gy", 2), ("gz", 3)), 1)
    upstream_one = convolve(delta_pad_two, flipped(w_second))
    delta_one, sum_d1, sum_x1 = backward_layer(
        upstream_one, preact, normed, scale_one, gain_first, voxels
    )
    local_first = kernel_grad(input_pad_b, delta_one) * factor
    delta_pad_one = extended(delta_one, (("gx", 1), ("gy", 2), ("gz", 3)), 1)
    dx_b = convolve(delta_pad_one, flipped(w_first)).astype(jnp.bfloat16)
    grad_w_first = lax.psum(local_first, ("gx", "gy", "gz"))
    grad_norm = jnp.stack([sum_x1, sum_d1, sum_x2, sum_d2]) * factor
    return (y_a, dx_b, grad_w_first, grad_w_second, grad_norm)


def solution(mesh):
    placed = (
        P(None, "gx", "gy", "gz"),
        P(None, "gx", "gy", "gz"),
        P(),
        P(),
        P(),
        P(),
        P(),
        P(),
        P(None, "gx", "gy", "gz"),
    )
    return jax.shard_map(
        body,
        mesh=mesh,
        in_specs=placed,
        out_specs=(P(None, "gx", "gy", "gz"), P(None, "gx", "gy", "gz"), P(), P(), P()),
        check_vma=False,
    )
```

profile of v0, /device:TPU:0, one launch (start us, length us, event | category | flops | bytes accessed | tf_op | source)
XLA Modules:
  0.0 585.4 jit_solution(11531565275628670312)
XLA Ops:
  8.4 5.0 collective-permute-start
  15.6 3.3 collective-permute-done
  18.9 4.1 collective-permute-done.1
  23.2 3.7 copy.460
  31.5 3.1 collective-permute-done.3
  34.6 6.2 %pad_maximum_fusion = bf16[2,32,4,18,128]{1,2,4,3,0:T(4,128)(2,1)S(1)} fusion(bf16[2,32,4,1,128]{1,2,4,3,0:T(4,128)(2,1)S(1)} %collective-permute-done.3, bf16[2,32,4,16,128]{1,2,4,3,0:T(4,128)(2,1)} %copy.460, bf16[2,32,4,1,128]{1,2,4,3,0:T(4,128)(2,1)S(1)} %collective-permute-done.2), kind=kLoop, calls=%fused_computation | loop fusion | flops 1179648 | bytes 2359296 | tf_op jit(solution)/shard_map/concatenate | solution.py:20
  40.8 2.1 copy-done
  43.0 4.0 collective-permute-start.4
  54.2 6.3 %copy.464 = bf16[2,32,4,18,128]{4,1,3,2,0:T(8,128)(2,1)S(1)} copy(bf16[2,32,4,18,128]{1,2,4,3,0:T(4,128)(2,1)} %copy-done) | data formatting | bytes 2359296 | tf_op jit(solution)/shard_map/concatenate | solution.py:20
  61.5 1.7 copy.463
  66.0 1.7 fusion.176
  67.7 3.2 fusion.175
  82.2 1.6 pad_maximum_fusion.19
  94.8 44.5 %all-reduce.3 = (f32[2,32]{1,0:T(2,128)S(1)}, f32[2,32]{1,0:T(2,128)S(1)}) all-reduce(f32[2,32]{1,0:T(2,128)S(1)} %pad_maximum_fusion.75, f32[2,32]{1,0:T(2,128)S(1)} %pad_maximum_fusion.74), channel_id=1, replica_groups=mesh['gx'=4,'gy'=4,'gz'=2] {'gx','gy','gz'}, use_global_device_ids=true, to_apply=%region_5.0 | all-reduce | flops 128 | bytes 1024 | tf_op jit(solution)/shard_map/psum | solution.py:89
  141.6 2.2 collective-permute-start.6
  145.9 2.7 collective-permute-done.6
  148.5 4.1 collective-permute-done.7
  153.8 5.6 copy.493
  159.4 2.1 fusion.165
  169.8 6.3 %pad_maximum_fusion.1 = bf16[2,32,4,18,128]{1,2,4,3,0:T(4,128)(2,1)S(1)} fusion(bf16[2,32,4,1,128]{1,2,4,3,0:T(4,128)(2,1)} %collective-permute-done.9, bf16[2,32,4,16,128]{1,2,4,3,0:T(4,128)(2,1)} %copy.493, bf16[2,32,4,1,128]{1,2,4,3,0:T(4,128)(2,1)S(1)} %collective-permute-done.8), kind=kLoop, calls=%fused_computation.1 | loop fusion | flops 1179648 | bytes 2359296 | tf_op jit(solution)/shard_map/concatenate | solution.py:20
  176.1 2.1 copy-done.1
  178.3 3.6 collective-permute-start.10
  185.6 2.2 dot_general.394
  195.3 7.1 %copy.497 = bf16[2,32,4,18,128]{4,1,3,2,0:T(8,128)(2,1)} copy(bf16[2,32,4,18,128]{1,2,4,3,0:T(4,128)(2,1)} %copy-done.1) | data formatting | bytes 2359296 | tf_op jit(solution)/shard_map/concatenate | solution.py:20
  204.4 2.6 pad_maximum_fusion.3
  207.2 1.8 fusion.174
  209.0 3.1 fusion.173
  213.3 3.0 fusion.171
  243.7 2.2 dot_general.408
  249.7 2.2 dot_general.404
  257.3 44.2 %all-reduce.2 = (f32[2,32]{1,0:T(2,128)S(1)}, f32[2,32]{1,0:T(2,128)S(1)}) all-reduce(f32[2,32]{1,0:T(2,128)S(1)} %pad_maximum_fusion.77, f32[2,32]{1,0:T(2,128)S(1)} %pad_maximum_fusion.76), channel_id=1, replica_groups=mesh['gx'=4,'gy'=4,'gz'=2] {'gx','gy','gz'}, use_global_device_ids=true, to_apply=%region_11.0 | all-reduce | flops 128 | bytes 1024 | tf_op jit(solution)/shard_map/psum | solution.py:89
  301.7 1.9 fusion.162
  303.6 38.6 %all-reduce.1 = (f32[32]{0:T(128)S(1)}, f32[32]{0:T(128)S(1)}) all-reduce(f32[32]{0:T(128)S(1)} %get-tuple-element.28, f32[32]{0:T(128)S(1)} %get-tuple-element.27), channel_id=1, replica_groups=mesh['gx'=4,'gy'=4,'gz'=2] {'gx','gy','gz'}, use_global_device_ids=true, to_apply=%region_15.0 | all-reduce | flops 64 | bytes 512 | tf_op jit(solution)/shard_map/psum | solution.py:102
  342.1 1.4 multiply_convert_fusion.1
  345.7 3.7 collective-permute-start.12
  349.4 1.4 collective-permute-start.13
  350.9 1.7 fusion.10
  361.8 2.7 collective-permute-done.15
  368.1 5.1 collective-permute-start.16
  376.8 2.2 maximum_maximum_fusion
  387.8 43.2 %all-reduce = (f32[32]{0:T(128)S(1)}, f32[32]{0:T(128)S(1)}) all-reduce(f32[32]{0:T(128)S(1)} %get-tuple-element.26, f32[32]{0:T(128)S(1)} %get-tuple-element.25), channel_id=1, replica_groups=mesh['gx'=4,'gy'=4,'gz'=2] {'gx','gy','gz'}, use_global_device_ids=true, to_apply=%region_19.20 | all-reduce | flops 64 | bytes 512 | tf_op jit(solution)/shard_map/psum | solution.py:102
  432.1 2.1 collective-permute-start.18
  434.2 1.6 collective-permute-start.19
  445.5 3.7 collective-permute-done.21
  452.2 4.5 collective-permute-start.22
  469.4 105.3 %all-reduce.7.cloned.1.call-done = (f32[3,3,3,32,32]{4,3,2,1,0:T(8,128)}, f32[3,3,3,32,32]{4,3,2,1,0:T(8,128)}) async-done(((f32[3,3,3,32,32]{4,3,2,1,0:T(8,128)}, f32[3,3,3,32,32]{4,3,2,1,0:T(8,128)}), (f32[3,3,3,32,32]{4,3,2,1,0:T(8,128)}, f32[3,3,3,32,32]{4,3,2,1,0:T(8,128)})) %all-reduce.7.cloned.1.call-update) | async-done | bytes 221200 | tf_op jit(solution)/shard_map/psum | solution.py:150
  574.7 1.8 copy.917
  576.5 1.8 copy.918
  (639 shorter events, 157.3 us)
Async XLA Ops:
  7.2 15.9 %copy-start.99 = (bf16[32,2,16,128]{3,2,1,0:T(8,128)(2,1)S(1)}, bf16[32,2,16,128]{3,2,1,0:T(8,128)(2,1)}, u32[]{:S(2)}) copy-start(bf16[32,2,16,128]{3,2,1,0:T(8,128)(2,1)} %param.10) | copy-start | bytes 786436
  7.2 15.9 %copy-start.98 = (bf16[32,2,16,128]{3,2,1,0:T(8,128)(2,1)S(1)}, bf16[32,2,16,128]{3,2,1,0:T(8,128)(2,1)}, u32[]{:S(2)}) copy-start(bf16[32,2,16,128]{3,2,1,0:T(8,128)(2,1)} %param.9) | copy-start | bytes 786436
  7.2 567.6 %all-reduce.7.cloned.1.call-start = ((), (), s32[]{:S(2)}) async-start(), calls=%async_computation | async-start | bytes 1769472 | tf_op jit(solution)/shard_map/psum | solution.py:150
  8.4 10.5 %collective-permute-start = (bf16[2,32,1,16,128]{4,3,2,1,0:T(8,128)(2,1)S(1)}, bf16[2,32,1,16,128]{4,3,2,1,0:T(8,128)(2,1)S(1)}, u32[]{:S(2)}, u32[]{:S(2)}) collective-permute-start(bf16[2,32,1,16,128]{4,3,2,1,0:T(8,128)(2,1)S(1)} %get-tuple-element.227), channel_id=1, source_target_pairs={{0,8},{8,16},{16,24},{1,9},{9,17},{17,25},{2,10},{10,18},{18,26},{... | collective-permute-start | bytes 786440 | tf_op jit(solution)/shard_map/ppermute | solution.py:16
  13.4 9.7 %collective-permute-start.1 = (bf16[2,32,1,16,128]{4,3,2,1,0:T(8,128)(2,1)S(1)}, bf16[2,32,1,16,128]{4,3,2,1,0:T(8,128)(2,1)S(1)}, u32[]{:S(2)}, u32[]{:S(2)}) collective-permute-start(bf16[2,32,1,16,128]{4,3,2,1,0:T(8,128)(2,1)S(1)} %get-tuple-element.228), channel_id=1, source_target_pairs={{8,0},{16,8},{24,16},{9,1},{17,9},{25,17},{10,2},{18,10},{26,18},{... | collective-permute-start | bytes 786440 | tf_op jit(solution)/shard_map/ppermute | solution.py:19
  28.2 3.3 collective-permute-start.2
  29.5 5.1 collective-permute-start.3
  31.5 16.8 %copy-start.100 = (bf16[3,3,3,32,32]{4,3,2,1,0:T(8,128)(2,1)S(1)}, bf16[3,3,3,32,32]{4,3,2,1,0:T(8,128)(2,1)}, u32[]{:S(2)}) copy-start(bf16[3,3,3,32,32]{4,3,2,1,0:T(8,128)(2,1)} %param.11) | copy-start | bytes 165892
  43.0 18.5 %collective-permute-start.4 = (bf16[2,32,4,18,1]{1,2,4,3,0:T(4,128)(2,1)S(1)}, bf16[2,32,4,18,1]{1,2,4,3,0:T(4,128)(2,1)}, u32[]{:S(2)}, u32[]{:S(2)}) collective-permute-start(bf16[2,32,4,18,1]{1,2,4,3,0:T(4,128)(2,1)S(1)} %get-tuple-element.43), channel_id=1, source_target_pairs={{0,1},{2,3},{4,5},{6,7},{8,9},{10,11},{12,13},{14,15},{16,17},{18,... | collective-permute-start | bytes 27656 | tf_op jit(solution)/shard_map/ppermute | solution.py:16
  47.0 13.5 %collective-permute-start.5 = (bf16[2,32,4,18,1]{1,2,4,3,0:T(4,128)(2,1)S(1)}, bf16[2,32,4,18,1]{1,2,4,3,0:T(4,128)(2,1)S(1)}, u32[]{:S(2)}, u32[]{:S(2)}) collective-permute-start(bf16[2,32,4,18,1]{1,2,4,3,0:T(4,128)(2,1)S(1)} %get-tuple-element.44), channel_id=1, source_target_pairs={{1,0},{3,2},{5,4},{7,6},{9,8},{11,10},{13,12},{15,14},{17,16},{19,... | collective-permute-start | bytes 27656 | tf_op jit(solution)/shard_map/ppermute | solution.py:19
  82.2 58.9 %copy-start.21 = (f32[4,8,32,128]{3,2,1,0:T(8,128)}, f32[4,8,32,128]{3,2,1,0:T(8,128)S(1)}, u32[]{:S(2)}) copy-start(f32[4,8,32,128]{3,2,1,0:T(8,128)S(1)} %copy.596) | copy-start | bytes 1572868
  92.2 48.9 %copy-start.147 = (f32[32]{0:T(128)S(1)}, f32[32]{0:T(128)}, u32[]{:S(2)}) copy-start(f32[32]{0:T(128)} %param.14) | copy-start | bytes 388
  92.2 48.9 %copy-start.149 = (f32[32]{0:T(128)S(1)}, f32[32]{0:T(128)}, u32[]{:S(2)}) copy-start(f32[32]{0:T(128)} %param.13) | copy-start | bytes 388
  141.6 6.9 %collective-permute-start.6 = (bf16[2,32,1,16,128]{4,3,2,1,0:T(8,128)(2,1)S(1)}, bf16[2,32,1,16,128]{4,3,2,1,0:T(8,128)(2,1)S(1)}, u32[]{:S(2)}, u32[]{:S(2)}) collective-permute-start(bf16[2,32,1,16,128]{4,3,2,1,0:T(8,128)(2,1)S(1)} %get-tuple-element.225), channel_id=1, source_target_pairs={{0,8},{8,16},{16,24},{1,9},{9,17},{17,25},{2,10},{10,18},{18,26},{... | collective-permute-start | bytes 786440 | tf_op jit(solution)/shard_map/ppermute | solution.py:16
  143.8 8.8 %collective-permute-start.7 = (bf16[2,32,1,16,128]{4,3,2,1,0:T(8,128)(2,1)S(1)}, bf16[2,32,1,16,128]{4,3,2,1,0:T(8,128)(2,1)S(1)}, u32[]{:S(2)}, u32[]{:S(2)}) collective-permute-start(bf16[2,32,1,16,128]{4,3,2,1,0:T(8,128)(2,1)S(1)} %get-tuple-element.226), channel_id=1, source_target_pairs={{8,0},{16,8},{24,16},{9,1},{17,9},{25,17},{10,2},{18,10},{26,18},{... | collective-permute-start | bytes 786440 | tf_op jit(solution)/shard_map/ppermute | solution.py:19
  159.4 9.7 %copy-start.126 = (bf16[32,3,32]{2,0,1:T(8,128)(2,1)S(1)}, bf16[32,3,32]{2,0,1:T(8,128)(2,1)}, u32[]{:S(2)}) copy-start(bf16[32,3,32]{2,0,1:T(8,128)(2,1)} %get-tuple-element.260) | copy-start | bytes 18436
  159.4 9.8 %copy-start.125 = (bf16[32,3,32]{2,0,1:T(8,128)(2,1)S(1)}, bf16[32,3,32]{2,0,1:T(8,128)(2,1)}, u32[]{:S(2)}) copy-start(bf16[32,3,32]{2,0,1:T(8,128)(2,1)} %get-tuple-element.261) | copy-start | bytes 18436
  159.4 9.9 %copy-start.124 = (bf16[32,3,32]{2,0,1:T(8,128)(2,1)S(1)}, bf16[32,3,32]{2,0,1:T(8,128)(2,1)}, u32[]{:S(2)}) copy-start(bf16[32,3,32]{2,0,1:T(8,128)(2,1)} %get-tuple-element.262) | copy-start | bytes 18436
  159.4 10.1 %copy-start.123 = (bf16[32,3,32]{2,0,1:T(8,128)(2,1)S(1)}, bf16[32,3,32]{2,0,1:T(8,128)(2,1)}, u32[]{:S(2)}) copy-start(bf16[32,3,32]{2,0,1:T(8,128)(2,1)} %get-tuple-element.263) | copy-start | bytes 18436
  159.4 10.2 %copy-start.122 = (bf16[32,3,32]{2,0,1:T(8,128)(2,1)S(1)}, bf16[32,3,32]{2,0,1:T(8,128)(2,1)}, u32[]{:S(2)}) copy-start(bf16[32,3,32]{2,0,1:T(8,128)(2,1)} %get-tuple-element.264) | copy-start | bytes 18436
  159.4 10.3 %copy-start.121 = (bf16[32,3,32]{2,0,1:T(8,128)(2,1)S(1)}, bf16[32,3,32]{2,0,1:T(8,128)(2,1)}, u32[]{:S(2)}) copy-start(bf16[32,3,32]{2,0,1:T(8,128)(2,1)} %get-tuple-element.265) | copy-start | bytes 18436
  161.5 8.3 %collective-permute-start.8 = (bf16[2,32,4,1,128]{1,2,4,3,0:T(4,128)(2,1)}, bf16[2,32,4,1,128]{1,2,4,3,0:T(4,128)(2,1)S(1)}, u32[]{:S(2)}, u32[]{:S(2)}) collective-permute-start(bf16[2,32,4,1,128]{1,2,4,3,0:T(4,128)(2,1)} %get-tuple-element.45), channel_id=1, source_target_pairs={{0,2},{2,4},{4,6},{1,3},{3,5},{5,7},{8,10},{10,12},{12,14},{9,11},... | collective-permute-start | bytes 196616 | tf_op jit(solution)/shard_map/ppermute | solution.py:16
  162.8 7.0 %collective-permute-start.9 = (bf16[2,32,4,1,128]{1,2,4,3,0:T(4,128)(2,1)}, bf16[2,32,4,1,128]{1,2,4,3,0:T(4,128)(2,1)}, u32[]{:S(2)}, u32[]{:S(2)}) collective-permute-start(bf16[2,32,4,1,128]{1,2,4,3,0:T(4,128)(2,1)} %get-tuple-element.46), channel_id=1, source_target_pairs={{2,0},{4,2},{6,4},{3,1},{5,3},{7,5},{10,8},{12,10},{14,12},{11,9},... | collective-permute-start | bytes 196616 | tf_op jit(solution)/shard_map/ppermute | solution.py:19
  169.8 13.4 %copy-start.146 = (f32[2,32]{1,0:T(2,128)S(1)}, f32[2,32]{1,0:T(2,128)}, u32[]{:S(2)}) copy-start(f32[2,32]{1,0:T(2,128)} %copy-done.145) | copy-start | bytes 772
  169.8 13.4 %copy-start.150 = (f32[32]{0:T(128)S(1)}, f32[32]{0:T(128)}, u32[]{:S(2)}) copy-start(f32[32]{0:T(128)} %param.13) | copy-start | bytes 388
  178.3 25.1 %collective-permute-start.10 = (bf16[2,32,4,18,1]{1,2,4,3,0:T(4,128)(2,1)S(1)}, bf16[2,32,4,18,1]{1,2,4,3,0:T(4,128)(2,1)S(1)}, u32[]{:S(2)}, u32[]{:S(2)}) collective-permute-start(bf16[2,32,4,18,1]{1,2,4,3,0:T(4,128)(2,1)S(1)} %get-tuple-element.41), channel_id=1, source_target_pairs={{0,1},{2,3},{4,5},{6,7},{8,9},{10,11},{12,13},{14,15},{16,17},{18,... | collective-permute-start | bytes 27656 | tf_op jit(solution)/shard_map/ppermute | solution.py:16
  181.9 20.5 %collective-permute-start.11 = (bf16[2,32,4,18,1]{1,2,4,3,0:T(4,128)(2,1)S(1)}, bf16[2,32,4,18,1]{1,2,4,3,0:T(4,128)(2,1)S(1)}, u32[]{:S(2)}, u32[]{:S(2)}) collective-permute-start(bf16[2,32,4,18,1]{1,2,4,3,0:T(4,128)(2,1)S(1)} %get-tuple-element.42), channel_id=1, source_target_pairs={{1,0},{3,2},{5,4},{7,6},{9,8},{11,10},{13,12},{15,14},{17,16},{19,... | collective-permute-start | bytes 27656 | tf_op jit(solution)/shard_map/ppermute | solution.py:19
  256.6 44.9 %copy-start.152 = (f32[32]{0:T(128)S(1)}, f32[32]{0:T(128)}, u32[]{:S(2)}) copy-start(f32[32]{0:T(128)} %param.15) | copy-start | bytes 388
  256.6 45.1 %copy-start.106 = (bf16[32,2,16,128]{3,2,1,0:T(8,128)(2,1)S(1)}, bf16[32,2,16,128]{3,2,1,0:T(8,128)(2,1)}, u32[]{:S(2)}) copy-start(bf16[32,2,16,128]{3,2,1,0:T(8,128)(2,1)} %param.17) | copy-start | bytes 786436
  256.6 45.1 %copy-start.151 = (f32[32]{0:T(128)S(1)}, f32[32]{0:T(128)}, u32[]{:S(2)}) copy-start(f32[32]{0:T(128)} %param.16) | copy-start | bytes 388
  257.2 44.5 %copy-start.43 = (f32[4,8,32,128]{3,2,1,0:T(8,128)S(1)}, f32[4,8,32,128]{3,2,1,0:T(8,128)}, u32[]{:S(2)}) copy-start(f32[4,8,32,128]{3,2,1,0:T(8,128)} %copy.606) | copy-start | bytes 1572868
  344.3 8.3 %copy-start.33 = (bf16[3,32,4096]{2,1,0:T(8,128)(2,1)S(1)}, bf16[3,32,4096]{2,1,0:T(8,128)(2,1)}, u32[]{:S(2)}) copy-start(bf16[3,32,4096]{2,1,0:T(8,128)(2,1)} %dot_general.398) | copy-start | bytes 2359300
  345.5 7.7 %copy-start.36 = (bf16[3,32,4096]{2,1,0:T(8,128)(2,1)S(1)}, bf16[3,32,4096]{2,1,0:T(8,128)(2,1)}, u32[]{:S(2)}) copy-start(bf16[3,32,4096]{2,1,0:T(8,128)(2,1)} %dot_general.400) | copy-start | bytes 2359300
  345.7 11.9 %collective-permute-start.12 = (bf16[32,1,16,128]{3,0,2,1:T(8,128)(2,1)}, bf16[32,1,16,128]{3,0,2,1:T(8,128)(2,1)S(1)}, u32[]{:S(2)}, u32[]{:S(2)}) collective-permute-start(bf16[32,1,16,128]{3,0,2,1:T(8,128)(2,1)} %get-tuple-element.237), channel_id=1, source_target_pairs={{0,8},{8,16},{16,24},{1,9},{9,17},{17,25},{2,10},{10,18},{18,26},{... | collective-permute-start | bytes 393224 | tf_op jit(solution)/shard_map/ppermute | solution.py:16
  349.4 8.2 %collective-permute-start.13 = (bf16[32,1,16,128]{3,0,2,1:T(8,128)(2,1)S(1)}, bf16[32,1,16,128]{3,0,2,1:T(8,128)(2,1)S(1)}, u32[]{:S(2)}, u32[]{:S(2)}) collective-permute-start(bf16[32,1,16,128]{3,0,2,1:T(8,128)(2,1)S(1)} %get-tuple-element.238), channel_id=1, source_target_pairs={{8,0},{16,8},{24,16},{9,1},{17,9},{25,17},{10,2},{18,10},{26,18},{... | collective-permute-start | bytes 393224 | tf_op jit(solution)/shard_map/ppermute | solution.py:19
  357.6 4.2 collective-permute-start.14
  358.9 5.6 collective-permute-start.15
  361.8 11.4 %copy-start.104 = (bf16[32,4,1,128]{3,0,2,1:T(8,128)(2,1)}, bf16[32,4,1,128]{3,0,2,1:T(8,128)(2,1)S(1)}, u32[]{:S(2)}) copy-start(bf16[32,4,1,128]{3,0,2,1:T(8,128)(2,1)S(1)} %collective-permute-done.14) | copy-start | bytes 98308
  364.5 8.7 %copy-start.105 = (bf16[32,4,1,128]{3,0,2,1:T(8,128)(2,1)}, bf16[32,4,1,128]{3,0,2,1:T(8,128)(2,1)S(1)}, u32[]{:S(2)}) copy-start(bf16[32,4,1,128]{3,0,2,1:T(8,128)(2,1)S(1)} %collective-permute-done.15) | copy-start | bytes 98308
  366.8 8.7 %collective-permute-start.17 = (bf16[32,4,18,1]{0,2,3,1:T(8,128)(2,1)S(1)}, bf16[32,4,18,1]{0,2,3,1:T(8,128)(2,1)}, u32[]{:S(2)}, u32[]{:S(2)}) collective-permute-start(bf16[32,4,18,1]{0,2,3,1:T(8,128)(2,1)S(1)} %copy.531), channel_id=1, source_target_pairs={{1,0},{3,2},{5,4},{7,6},{9,8},{11,10},{13,12},{15,14},{17,16},{19,... | collective-permute-start | bytes 13832 | tf_op jit(solution)/shard_map/ppermute | solution.py:19
  368.1 6.8 %collective-permute-start.16 = (bf16[32,4,18,1]{0,2,3,1:T(8,128)(2,1)}, bf16[32,4,18,1]{0,2,3,1:T(8,128)(2,1)S(1)}, u32[]{:S(2)}, u32[]{:S(2)}) collective-permute-start(bf16[32,4,18,1]{0,2,3,1:T(8,128)(2,1)} %copy.529), channel_id=1, source_target_pairs={{0,1},{2,3},{4,5},{6,7},{8,9},{10,11},{12,13},{14,15},{16,17},{18,... | collective-permute-start | bytes 13832 | tf_op jit(solution)/shard_map/ppermute | solution.py:16
  387.8 43.5 %copy-start.22 = (f32[4,8,32,128]{3,2,1,0:T(8,128)S(1)}, f32[4,8,32,128]{3,2,1,0:T(8,128)}, u32[]{:S(2)}) copy-start(f32[4,8,32,128]{3,2,1,0:T(8,128)} %copy-done.21) | copy-start | bytes 1572868
  432.1 10.2 %collective-permute-start.18 = (bf16[32,1,16,128]{3,0,2,1:T(8,128)(2,1)S(1)}, bf16[32,1,16,128]{3,0,2,1:T(8,128)(2,1)S(1)}, u32[]{:S(2)}, u32[]{:S(2)}) collective-permute-start(bf16[32,1,16,128]{3,0,2,1:T(8,128)(2,1)S(1)} %get-tuple-element.232), channel_id=1, source_target_pairs={{0,8},{8,16},{16,24},{1,9},{9,17},{17,25},{2,10},{10,18},{18,26},{... | collective-permute-start | bytes 393224 | tf_op jit(solution)/shard_map/ppermute | solution.py:16
  434.2 8.1 %collective-permute-start.19 = (bf16[32,1,16,128]{3,0,2,1:T(8,128)(2,1)S(1)}, bf16[32,1,16,128]{3,0,2,1:T(8,128)(2,1)S(1)}, u32[]{:S(2)}, u32[]{:S(2)}) collective-permute-start(bf16[32,1,16,128]{3,0,2,1:T(8,128)(2,1)S(1)} %get-tuple-element.233), channel_id=1, source_target_pairs={{8,0},{16,8},{24,16},{9,1},{17,9},{25,17},{10,2},{18,10},{26,18},{... | collective-permute-start | bytes 393224 | tf_op jit(solution)/shard_map/ppermute | solution.py:19
  442.3 3.2 collective-permute-start.20
  443.6 5.6 collective-permute-start.21
  450.9 7.9 %collective-permute-start.23 = (bf16[32,4,18,1]{0,2,3,1:T(8,128)(2,1)S(1)}, bf16[32,4,18,1]{0,2,3,1:T(8,128)(2,1)S(1)}, u32[]{:S(2)}, u32[]{:S(2)}) collective-permute-start(bf16[32,4,18,1]{0,2,3,1:T(8,128)(2,1)S(1)} %copy.546), channel_id=1, source_target_pairs={{1,0},{3,2},{5,4},{7,6},{9,8},{11,10},{13,12},{15,14},{17,16},{19,... | collective-permute-start | bytes 13832 | tf_op jit(solution)/shard_map/ppermute | solution.py:19
  452.2 6.1 %collective-permute-start.22 = (bf16[32,4,18,1]{0,2,3,1:T(8,128)(2,1)S(1)}, bf16[32,4,18,1]{0,2,3,1:T(8,128)(2,1)S(1)}, u32[]{:S(2)}, u32[]{:S(2)}) collective-permute-start(bf16[32,4,18,1]{0,2,3,1:T(8,128)(2,1)S(1)} %copy.544), channel_id=1, source_target_pairs={{0,1},{2,3},{4,5},{6,7},{8,9},{10,11},{12,13},{14,15},{16,17},{18,... | collective-permute-start | bytes 13832 | tf_op jit(solution)/shard_map/ppermute | solution.py:16
  (130 other events, 218.3 us)
Sparse Core Ops, SparseCore 0:
  442.4 132.2 all-reduce.6
where the time goes:
time: 592 us; the launch traced here: 585 us
  blocking collectives  170 us (29%)
  local copies, waits for them, and re-layouts  139 us (23%)
  waiting for transfers between devices  131 us (22%)
  starting transfers between devices  51.5 us (9%)
  other arithmetic  40.1 us (7%)
  matrix products  36.3 us (6%)
  between operations  17.5 us (3%)
    psum x1, waiting for transfers between devices, body(): grad_w_first = lax.psum(local_first, ('gx', 'gy', 'gz'))  105 us
    psum x2, blocking collectives, statistics(): sums, squares = lax.psum((local_sums, local_squares), ('gx', 'gy', 'gz'))  88.7 us
    psum x2, blocking collectives, backward_layer(): lax.psum((jnp.sum(slope, axis=(1, 2, 3)), jnp.sum(slope * normed, axis=(1...  81.7 us
    ppermute x12, starting transfers between devices, extended(): lax.ppermute(lax.slice_in_dim(block, block.shape[dim] - width, None, axis...  35.5 us
    dot_general x18, local copies, waits for them, and re-layouts, kernel_grad(): lax.dot_general(flat, stacked, (((1,), (1,)), ((), ())), preferred_elemen...  25 us
    dot_general x54, matrix products, convolve(): total = total + jnp.dot(matrix, stacked, preferred_element_type=jnp.float32)  24.8 us
    unnamed x315, local copies, waits for them, and re-layouts  23.4 us
    concatenate x4, local copies, waits for them, and re-layouts, extended(): block = jnp.concatenate([low, block, high], axis=dim)  22.8 us
  transfers between devices with their start and end apart: 25, of which 10 were waited for; matrix products, arithmetic and copies ran while one was open for 12% of the time, Pallas kernels for 0%

commit v1 on v0

v1 whole, which is shorter than its diff:
```python
import math

import jax
import jax.numpy as jnp
from jax import lax
from jax.experimental import pallas as pl
from jax.experimental.pallas import tpu as pltpu
from jax.sharding import PartitionSpec as P

EPSILON = 1e-05
AXES = ("gx", "gy", "gz")
LANES = 128
BF = jnp.bfloat16
F32 = jnp.float32
VM = pl.BlockSpec(memory_space=pltpu.VMEM)
SM = pl.BlockSpec(memory_space=pltpu.SMEM)


def kernel_call(body, name, out_shape, args, scratch=(), smem=0):
    return pl.pallas_call(
        body,
        out_shape=out_shape,
        in_specs=[SM] * smem + [VM] * (len(args) - smem),
        out_specs=[VM] * len(out_shape),
        scratch_shapes=list(scratch),
        name=name,
    )(*args)


def shape(dims, kind):
    return jax.ShapeDtypeStruct(dims, kind)


def shift_pair(low_source, high_source, axis):
    count = lax.axis_size(axis)
    if count == 2:
        at = lax.axis_index(axis)
        got = lax.ppermute(jnp.where(at == 0, low_source, high_source), axis, [(0, 1), (1, 0)])
        zero = jnp.zeros_like(got)
        return jnp.where(at == 1, got, zero), jnp.where(at == 0, got, zero)
    forward = [(i, i + 1) for i in range(count - 1)]
    backward = [(t, s) for s, t in forward]
    return lax.ppermute(low_source, axis, forward), lax.ppermute(high_source, axis, backward)


def extended(block, sides):
    for axis, dim, width in sides:
        size = block.shape[dim]
        low, high = shift_pair(
            lax.slice_in_dim(block, size - width, size, axis=dim),
            lax.slice_in_dim(block, 0, width, axis=dim),
            axis,
        )
        block = jnp.concatenate([low, block, high], axis=dim)
    return block


def exchange(spread_rows):
    return lax.all_to_all(spread_rows, AXES, 0, 0)


def order_matrix(chan, rows):
    size = chan * rows
    k = lax.broadcasted_iota(jnp.int32, (size, size), 0)
    n = lax.broadcasted_iota(jnp.int32, (size, size), 1)
    return (n == (k % rows) * chan + k // rows).astype(BF)


def band_conv(src, weight, group, planes, pitch):
    size = planes * pitch
    at = pl.multiple_of(group * LANES, LANES)
    parts = [src[pl.ds(d * pitch, size), pl.ds(at, 2 * LANES)] for d in range(3)]
    out = jnp.dot(jnp.concatenate(parts, axis=1), weight[...], preferred_element_type=F32)
    return (
        out[:, :LANES]
        + pltpu.roll(out[:, LANES : 2 * LANES], size - 1, 0)
        + pltpu.roll(out[:, 2 * LANES :], size - 2, 0)
    )


def tap_products(d_rows, h_ref, start, group, pitch, acc):
    size = d_rows.shape[0]
    three = jnp.concatenate([d_rows, pltpu.roll(d_rows, 1, 0), pltpu.roll(d_rows, 2, 0)], axis=1)
    left = three.T.astype(BF)
    at = pl.multiple_of(group * LANES, LANES)
    for d in range(3):
        right = h_ref[pl.ds(start + d * pitch, size), pl.ds(at, 2 * LANES)]
        acc[d] = acc[d] + jnp.dot(left, right, preferred_element_type=F32)


def fold_taps(acc, chan):
    rows = []
    for d in range(3):
        for t in range(3):
            base = t * LANES
            rows.append(
                sum(
                    acc[d, base + j * chan : base + (j + 1) * chan, j * chan : (j + 3) * chan]
                    for j in range(LANES // chan)
                )
            )
    return jnp.concatenate(rows, axis=0)


def fold_lanes(value, chan):
    step = chan
    while step < LANES:
        value = value + pltpu.roll(value, step, 1)
        step *= 2
    return value


def gathered(ref, row, chan):
    return fold_lanes(jnp.sum(ref[:, row, :], axis=0, keepdims=True), chan)


def sigmoid(value):
    return 0.5 + 0.5 * jnp.tanh(0.5 * value)


def body_maker(mesh):
    def body(x_a, x_b, w_first, w_second, gain_first, bias_first, gain_second, bias_second, grad_out):
        chan, span_x, span_y, span_z = x_a.shape
        world = lax.axis_size("gx") * lax.axis_size("gy") * lax.axis_size("gz")
        voxels = float(span_x * span_y * span_z * world)
        factor = 1.0 / math.sqrt(voxels)
        per = LANES // chan
        line = span_y * chan
        pitch = -(-(span_z + 4) // 16) * 16
        inner_groups = span_y // per
        outer_groups = -(-(span_y + 2) // per)
        wide = (outer_groups + 1) * LANES
        mid = outer_groups * LANES
        po, pi = span_x + 2, span_x
        so, si = po * pitch, pi * pitch

        def band(weight):
            turned = weight.transpose(0, 1, 4, 2, 3)
            parts = [
                jnp.pad(turned, ((0, 0), (j, 2 * per - 3 - j), (0, 0), (0, 0), (0, 0)))
                for j in range(per)
            ]
            return jnp.stack(parts, axis=4).reshape(3 * 2 * LANES, 3 * LANES)

        def flipped(weight):
            return jnp.flip(weight, (0, 1, 2)).transpose(0, 1, 2, 4, 3)

        band_one, band_two = band(w_first), band(w_second)
        back_one, back_two = band(flipped(w_first)), band(flipped(w_second))
        params = jnp.stack(
            [jnp.tile(v, per) for v in (gain_first, bias_first, gain_second, bias_second)]
        )

        def limits(axis, size):
            at, count = lax.axis_index(axis), lax.axis_size(axis)
            return [jnp.where(at == 0, 1, 0), jnp.where(at == count - 1, size + 1, size + 2)]

        bounds = jnp.stack(
            limits("gx", span_x) + limits("gy", span_y) + limits("gz", span_z)
        ).astype(jnp.int32)

        def inside(bound, group):
            row = lax.broadcasted_iota(jnp.int32, (so, LANES), 0)
            lane = lax.broadcasted_iota(jnp.int32, (so, LANES), 1) + group * LANES
            plane = row // pitch
            z = row - plane * pitch
            y = lane // chan
            ok = (plane >= bound[0]) & (plane < bound[1]) & (y >= bound[2]) & (y < bound[3])
            return ok & (z >= bound[4]) & (z < bound[5])

        def own(group):
            row = lax.broadcasted_iota(jnp.int32, (si, LANES), 0)
            lane = lax.broadcasted_iota(jnp.int32, (si, LANES), 1) + group * LANES
            z = row % pitch
            return (z >= 1) & (z <= span_z) & (lane >= chan) & (lane < chan + line)

        def own_rows():
            row = lax.broadcasted_iota(jnp.int32, (si, LANES), 0)
            return row % pitch < span_z

        def turn_in(a_ref, b_ref, g_ref, v_ref, o_ref):
            order = order_matrix(chan, span_y)
            for at, ref in enumerate((a_ref, b_ref)):
                for x in range(span_x):
                    block = ref[:, x].reshape(chan * span_y, span_z)
                    v_ref[at, x] = lax.dot_general(
                        block, order, (((0,), (0,)), ((), ())), preferred_element_type=F32
                    ).astype(BF)
            for x in range(span_x):
                block = g_ref[:, x].reshape(chan * span_y, span_z)
                o_ref[x * pitch : x * pitch + span_z, :] = lax.dot_general(
                    block, order, (((0,), (0,)), ((), ())), preferred_element_type=F32
                ).astype(BF)
                o_ref[x * pitch + span_z : (x + 1) * pitch, :] = jnp.zeros(
                    (pitch - span_z, line), BF
                )

        vols, cot = kernel_call(
            turn_in,
            "turn_in",
            [shape((2, span_x, span_z, line), BF), shape((si, line), BF)],
            [x_a, x_b, grad_out],
        )

        def two_wide(block):
            block = extended(block, (("gz", 2, 2), ("gy", 3, 2 * chan), ("gx", 1, 2)))
            fill = (0, pitch - block.shape[2]), (0, wide - block.shape[3])
            block = jnp.pad(block, ((0, 0), (0, 0)) + fill)
            return block.reshape(block.shape[0], (span_x + 4) * pitch, wide)

        padded = two_wide(vols)

        def first_conv(x_ref, w_ref, c_ref, st_ref):
            rows = []
            for v in range(2):

                def step(g, sums):
                    out = band_conv(x_ref.at[v], w_ref, g, po, pitch)
                    c_ref[v, :, pl.ds(pl.multiple_of(g * LANES, LANES), LANES)] = out
                    mine = jnp.where(own(g), out[pitch : pitch + si], 0.0)
                    return (
                        sums[0] + jnp.sum(mine, axis=0, keepdims=True),
                        sums[1] + jnp.sum(mine * mine, axis=0, keepdims=True),
                    )

                zero = jnp.zeros((1, LANES), F32)
                rows += list(lax.fori_loop(0, outer_groups, step, (zero, zero)))
            rows.append(jnp.zeros((4, LANES), F32))
            st_ref[...] = jnp.broadcast_to(jnp.concatenate(rows, axis=0)[None], st_ref.shape)

        stat_shape = shape((world, 8, LANES), F32)
        conv_one, stats = kernel_call(
            first_conv, "first_conv", [shape((2, so, mid), F32), stat_shape], [padded, band_one]
        )
        stats_one = exchange(stats)

        def moments(st_ref, v):
            mean = gathered(st_ref, 2 * v, chan) / voxels
            var = gathered(st_ref, 2 * v + 1, chan) / voxels - mean * mean
            return mean, lax.rsqrt(var + EPSILON)

        def second_conv(bound, c_ref, w_ref, st_in, p_ref, h_ref, c2_ref, st_ref, a_ref):
            rows = []
            for v in range(2):
                mean, rstd = moments(st_in, v)
                gain, bias = p_ref[0:1, :], p_ref[1:2, :]
                dest = a_ref if v == 0 else h_ref

                def act(g, carry):
                    at = pl.ds(pl.multiple_of(g * LANES, LANES), LANES)
                    z = gain * ((c_ref[v, :, at] - mean) * rstd) + bias
                    dest[:, at] = jnp.where(inside(bound, g), z * sigmoid(z), 0.0).astype(BF)
                    return carry

                lax.fori_loop(0, outer_groups, act, 0)

                def step(g, sums):
                    out = band_conv(dest, w_ref, g, pi, pitch)
                    c2_ref[v, :, pl.ds(pl.multiple_of(g * LANES, LANES), LANES)] = out
                    mine = jnp.where(own_rows(), out, 0.0)
                    return (
                        sums[0] + jnp.sum(mine, axis=0, keepdims=True),
                        sums[1] + jnp.sum(mine * mine, axis=0, keepdims=True),
                    )

                zero = jnp.zeros((1, LANES), F32)
                rows += list(lax.fori_loop(0, inner_groups, step, (zero, zero)))
            rows.append(jnp.zeros((4, LANES), F32))
            st_ref[...] = jnp.broadcast_to(jnp.concatenate(rows, axis=0)[None], st_ref.shape)

        hidden_b, conv_two, stats = kernel_call(
            second_conv,
            "second_conv",
            [shape((so, mid), BF), shape((2, si, line), F32), stat_shape],
            [bounds, conv_one, band_two, stats_one, params],
            scratch=[pltpu.VMEM((so, mid), BF)],
            smem=1,
        )
        stats_two = exchange(stats)

        def slope_two(c_ref, st_in, p_ref, go_ref, g):
            at = pl.ds(pl.multiple_of(g * LANES, LANES), LANES)
            mean, rstd = moments(st_in, 1)
            xhat = (c_ref[1, :, at] - mean) * rstd
            z = p_ref[2:3, :] * xhat + p_ref[3:4, :]
            s = sigmoid(z)
            d = go_ref[:, at].astype(F32) * (s * (1.0 + z * (1.0 - s)))
            return jnp.where(own_rows(), d, 0.0), xhat, rstd, at

        def sum_rows(ref, sums):
            rows = list(sums) + [jnp.zeros((6, LANES), F32)]
            ref[...] = jnp.broadcast_to(jnp.concatenate(rows, axis=0)[None], ref.shape)

        def native(value, order):
            return lax.dot_general(
                order, value, (((1,), (1,)), ((), ())), preferred_element_type=F32
            ).astype(BF).reshape(chan, span_y, span_z)

        def second_slope(c_ref, st_in, p_ref, go_ref, y_ref, st_ref):
            order = order_matrix(chan, span_y)
            mean, rstd = moments(st_in, 0)
            reps = line // LANES
            wide_mean, wide_rstd = jnp.tile(mean, (1, reps)), jnp.tile(rstd, (1, reps))
            gain, bias = jnp.tile(p_ref[2:3, :], (1, reps)), jnp.tile(p_ref[3:4, :], (1, reps))
            for x in range(span_x):
                c = c_ref[0, x * pitch : x * pitch + span_z, :]
                z = gain * ((c - wide_mean) * wide_rstd) + bias
                y_ref[:, x] = native((z * sigmoid(z)).astype(BF), order)

            def step(g, sums):
                d, xhat, _, _ = slope_two(c_ref, st_in, p_ref, go_ref, g)
                return (
                    sums[0] + jnp.sum(d, axis=0, keepdims=True),
                    sums[1] + jnp.sum(d * xhat, axis=0, keepdims=True),
                )

            zero = jnp.zeros((1, LANES), F32)
            sum_rows(st_ref, lax.fori_loop(0, inner_groups, step, (zero, zero)))

        y_a, stats = kernel_call(
            second_slope,
            "second_slope",
            [shape(x_a.shape, BF), stat_shape],
            [conv_two, stats_two, params, cot],
        )
        sums_two = exchange(stats)

        def second_delta(c_ref, st_in, p_ref, go_ref, sums_in, d_ref):
            sum_d, sum_x = gathered(sums_in, 0, chan) / voxels, gathered(sums_in, 1, chan) / voxels

            def step(g, carry):
                d, xhat, rstd, at = slope_two(c_ref, st_in, p_ref, go_ref, g)
                out = (p_ref[2:3, :] * rstd) * (d - sum_d - xhat * sum_x)
                d_ref[:, at] = jnp.where(own_rows(), out, 0.0).astype(BF)
                return carry

            lax.fori_loop(0, inner_groups, step, 0)

        (delta_two,) = kernel_call(
            second_delta,
            "second_delta",
            [shape((si, line), BF)],
            [conv_two, stats_two, params, cot, sums_two],
        )
        delta_pad = two_wide(delta_two.reshape(1, span_x, pitch, line)[:, :, :span_z])[0]

        def slope_one(c_ref, st_in, p_ref, g):
            at = pl.ds(pl.multiple_of(g * LANES, LANES), LANES)
            mean, rstd = moments(st_in, 1)
            xhat = (c_ref[:, at] - mean) * rstd
            z = p_ref[0:1, :] * xhat + p_ref[1:2, :]
            s = sigmoid(z)
            return s * (1.0 + z * (1.0 - s)), xhat, rstd, at

        def first_slope(dp_ref, w_ref, c_ref, st_in, p_ref, d2_ref, h_ref, d1_ref, st_ref, gw_ref, acc):
            acc[...] = jnp.zeros(acc.shape, F32)

            def step(g, sums):
                slope, xhat, _, at = slope_one(c_ref, st_in, p_ref, g)
                d = band_conv(dp_ref, w_ref, g, po, pitch) * slope
                d1_ref[:, at] = d
                mine = jnp.where(own(g), d[pitch : pitch + si], 0.0)
                return (
                    sums[0] + jnp.sum(mine, axis=0, keepdims=True),
                    sums[1] + jnp.sum(mine * xhat[pitch : pitch + si], axis=0, keepdims=True),
                )

            zero = jnp.zeros((1, LANES), F32)
            sum_rows(st_ref, lax.fori_loop(0, outer_groups, step, (zero, zero)))

            def taps(g, carry):
                at = pl.ds(pl.multiple_of(g * LANES, LANES), LANES)
                tap_products(d2_ref[:, at].astype(F32), h_ref, 0, g, pitch, acc)
                return carry

            lax.fori_loop(0, inner_groups, taps, 0)
            gw_ref[...] = fold_taps(acc, chan)

        taps_shape = shape((9 * chan, 3 * chan), F32)
        taps_scratch = [pltpu.VMEM((3, 3 * LANES, 2 * LANES), F32)]
        conv_one_b = conv_one[1]
        slope, stats, taps_two = kernel_call(
            first_slope,
            "first_slope",
            [shape((so, mid), F32), stat_shape, taps_shape],
            [delta_pad, back_two, conv_one_b, stats_one, params, delta_two, hidden_b],
            scratch=taps_scratch,
        )
        sums_one = exchange(stats)

        def first_delta(bound, s_ref, c_ref, st_in, p_ref, sums_in, w_ref, x_ref, dx_ref, gw_ref, d_ref, o_ref, acc):
            acc[...] = jnp.zeros(acc.shape, F32)
            sum_d, sum_x = gathered(sums_in, 0, chan) / voxels, gathered(sums_in, 1, chan) / voxels
            mean, rstd = moments(st_in, 1)

            def step(g, carry):
                at = pl.ds(pl.multiple_of(g * LANES, LANES), LANES)
                xhat = (c_ref[:, at] - mean) * rstd
                out = (p_ref[0:1, :] * rstd) * (s_ref[:, at] - sum_d - xhat * sum_x)
                out = jnp.where(inside(bound, g), out, 0.0).astype(BF)
                d_ref[:, at] = out
                mine = jnp.where(own(g), out[pitch : pitch + si].astype(F32), 0.0)
                tap_products(mine, x_ref, pitch, g, pitch, acc)
                return carry

            lax.fori_loop(0, outer_groups, step, 0)
            gw_ref[...] = fold_taps(acc, chan)

            def conv(g, carry):
                out = band_conv(d_ref, w_ref, g, pi, pitch)
                o_ref[:, pl.ds(pl.multiple_of(g * LANES, LANES), LANES)] = out.astype(BF)
                return carry

            lax.fori_loop(0, inner_groups, conv, 0)
            order = order_matrix(chan, span_y)
            for x in range(span_x):
                dx_ref[:, x] = native(o_ref[x * pitch : x * pitch + span_z, :], order)

        dx_b, taps_one = kernel_call(
            first_delta,
            "first_delta",
            [shape(x_a.shape, BF), taps_shape],
            [bounds, slope, conv_one_b, stats_one, params, sums_one, back_one, padded[1]],
            scratch=[pltpu.VMEM((so, mid), BF), pltpu.VMEM((si, line), BF)] + taps_scratch,
            smem=1,
        )

        both = jnp.stack([taps_one, taps_two]) * factor
        size = both.size
        share = -(-size // (world * 8 * LANES)) * 8
        flat = jnp.pad(both.reshape(-1), (0, share * world * LANES - size))
        part = jnp.sum(exchange(flat.reshape(world, share, LANES)), axis=0)
        whole = exchange(jnp.broadcast_to(part[None], (world, share, LANES)))
        whole = whole.reshape(-1)[:size].reshape(2, 3, 3, chan, 3, chan).transpose(0, 1, 4, 2, 3, 5)

        def channel_sums(got, row):
            return jnp.sum(jnp.sum(got[:, row], axis=0).reshape(per, chan), axis=0)

        grad_norm = factor * jnp.stack(
            [
                channel_sums(sums_one, 1),
                channel_sums(sums_one, 0),
                channel_sums(sums_two, 1),
                channel_sums(sums_two, 0),
            ]
        )
        return (y_a, dx_b, whole[0], whole[1], grad_norm)

    return body


def solution(mesh):
    block = P(None, "gx", "gy", "gz")
    placed = (block, block, P(), P(), P(), P(), P(), P(), block)
    return jax.shard_map(
        body_maker(mesh),
        mesh=mesh,
        in_specs=placed,
        out_specs=(block, block, P(), P(), P()),
        check_vma=False,
    )
```

time: 592 us -> 213 us (0.36)
  blocking collectives: 170 us -> 30.6 us
  waiting for transfers between devices: 131 us -> 26.6 us
  local copies, waits for them, and re-layouts: 139 us -> 45.8 us
  Pallas kernels: 0 us -> 48.3 us
  matrix products: 36.3 us -> 0 us
  other arithmetic: 40.1 us -> 20.7 us
  between operations: 17.5 us -> 1.09 us
  starting transfers between devices: 51.5 us -> 38.6 us
    psum x4 -> x0, blocking collectives: 170 us -> none  [the longest x2 88.7 us: statistics(): sums, squares = lax.psum((local_sums, local_squares), ('gx', 'gy', 'gz'))]
    psum x1 -> x0, waiting for transfers between devices: 105 us -> none  [body(): grad_w_first = lax.psum(local_first, ('gx', 'gy', 'gz'))]
    pallas_call x0 -> x7, Pallas kernels: none -> 48.3 us  [kernel_call(): pl.pallas_call(body, out_shape=out_shape, in_specs=[SM] * smem + [VM] * (...]
    dot_general x72 -> x0, matrix products: 36.3 us -> none  [the longest x54 24.8 us: convolve(): total = total + jnp.dot(matrix, stacked, preferred_element_type=jnp.float32)]
    all_to_all x0 -> x2, blocking collectives: none -> 30.6 us  [exchange(): return lax.all_to_all(spread_rows, AXES, 0, 0)]
    ppermute x24 -> x10, starting transfers between devices: 51.5 us -> 21.2 us  [the longest x4 12.6 us: shift_pair(): lax.ppermute(low_source, axis, forward)]
    slice x29 -> x3, local copies, waits for them, and re-layouts: 27.6 us -> 1.2 us  [the longest x1 1.16 us: body(): padded[1]]
    dot_general x18 -> x0, local copies, waits for them, and re-layouts: 25 us -> none  [kernel_grad(): lax.dot_general(flat, stacked, (((1,), (1,)), ((), ())), preferred_elemen...]
  transfers between devices with their start and end apart: 25 -> 14, of which waited for: 10 -> 7; matrix products, arithmetic and copies ran while one was open for 12% -> 21% of each run, Pallas kernels for 0% -> 0%
where the time goes in v1:
time: 213 us; the launch traced here: 212 us
  Pallas kernels  48.3 us (23%)
  local copies, waits for them, and re-layouts  45.8 us (22%)
  starting transfers between devices  38.6 us (18%)
  blocking collectives  30.6 us (14%)
  waiting for transfers between devices  26.6 us (12%)
  other arithmetic  20.7 us (10%)
    pallas_call x7, Pallas kernels, kernel_call(): pl.pallas_call(body, out_shape=out_shape, in_specs=[SM] * smem + [VM] * (...  48.3 us
    all_to_all x2, blocking collectives, exchange(): return lax.all_to_all(spread_rows, AXES, 0, 0)  30.6 us
    all_to_all x4, starting transfers between devices, exchange(): return lax.all_to_all(spread_rows, AXES, 0, 0)  17.5 us
    all_to_all x4, waiting for transfers between devices, exchange(): return lax.all_to_all(spread_rows, AXES, 0, 0)  16 us
    reshape x4, local copies, waits for them, and re-layouts, band(): return jnp.stack(parts, axis=4).reshape(3 * 2 * LANES, 3 * LANES)  14.8 us
    another operation x8, local copies, waits for them, and re-layouts, band(): return jnp.stack(parts, axis=4).reshape(3 * 2 * LANES, 3 * LANES)  14.3 us
    ppermute x4, starting transfers between devices, shift_pair(): lax.ppermute(low_source, axis, forward)  12.6 us
    concatenate x4, other arithmetic, extended(): block = jnp.concatenate([low, block, high], axis=dim)  9.8 us
  transfers between devices with their start and end apart: 14, of which 7 were waited for; matrix products, arithmetic and copies ran while one was open for 21% of the time, Pallas kernels for 0%

profile of v1, /device:TPU:0, one launch (start us, length us, event | category | flops | bytes accessed | tf_op | source)
XLA Modules:
  0.0 211.7 jit_solution(14290177208432013746)
XLA Ops:
  0.7 2.6 %turn_in.1 = (bf16[2,2,128,512]{3,2,1,0:T(8,128)(2,1)}, bf16[288,512]{1,0:T(8,128)(2,1)}) custom-call(bf16[32,2,16,128]{3,2,1,0:T(8,128)(2,1)} %a_ref.1, bf16[32,2,16,128]{3,2,1,0:T(8,128)(2,1)} %b_ref.1, bf16[32,2,16,128]{3,2,1,0:T(8,128)(2,1)} %g_ref.1), custom_call_target="tpu_custom_call" | custom-call | tf_op jit(solution)/shard_map/turn_in/pallas_call | solution.py:20
  4.0 3.1 %collective-permute-start = (bf16[2,2,2,512]{3,2,1,0:T(2,128)(2,1)S(1)}, bf16[2,2,2,512]{3,2,1,0:T(2,128)(2,1)S(1)}, u32[]{:S(2)}, u32[]{:S(2)}) collective-permute-start(bf16[2,2,2,512]{3,2,1,0:T(2,128)(2,1)S(1)} %broadcast_select_fusion.1), channel_id=1, source_target_pairs={{0,1},{1,0},{2,3},{3,2},{4,5},{5,4},{6,7},{7,6},{8,9},{9,8},{10,11... | collective-permute-start | bytes 24584 | tf_op jit(solution)/shard_map/ppermute | solution.py:38
  7.1 1.6 collective-permute-done
  8.8 1.1 pad_maximum_fusion.8
  9.9 1.3 collective-permute-start.1
  11.2 1.3 collective-permute-start.2
  12.5 4.2 %collective-permute-done.2 = bf16[2,2,132,64]{3,2,1,0:T(8,128)(2,1)S(1)} collective-permute-done((bf16[2,2,132,64]{3,2,1,0:T(8,128)(2,1)S(1)}, bf16[2,2,132,64]{3,2,1,0:T(8,128)(2,1)S(1)}, u32[]{:S(2)}, u32[]{:S(2)}) %collective-permute-start.2) | collective-permute-done | bytes 67616 | tf_op jit(solution)/shard_map/ppermute | solution.py:43
  17.3 1.6 pad_maximum_fusion.4
  18.9 1.4 copy.34
  20.3 1.3 collective-permute-start.4
  21.6 5.4 %collective-permute-start.3 = (bf16[2,2,132,640]{3,1,2,0:T(2,128)(2,1)}, bf16[2,2,132,640]{3,1,2,0:T(2,128)(2,1)}, u32[]{:S(2)}, u32[]{:S(2)}) collective-permute-start(bf16[2,2,132,640]{3,1,2,0:T(2,128)(2,1)} %copy.34), channel_id=1, source_target_pairs={{0,8},{8,16},{16,24},{1,9},{9,17},{17,25},{2,10},{10,18},{18,26},{... | collective-permute-start | bytes 2027528 | tf_op jit(solution)/shard_map/ppermute | solution.py:43
  30.6 3.2 %copy.38 = bf16[3,8,32,3,4,32]{5,4,3,2,1,0:T(4,128)(2,1)} copy(bf16[3,8,32,3,4,32]{2,5,3,1,0,4:T(8,128)(2,1)S(1)} %pad_maximum_fusion) | data formatting | bytes 1179648 | tf_op jit(solution)/shard_map/stack | solution.py:143
  33.9 4.2 %reshape.61.w_ref = bf16[768,384]{1,0:T(8,128)(2,1)} reshape(bf16[3,8,32,3,4,32]{5,4,3,2,1,0:T(4,128)(2,1)} %copy.38) | data formatting | bytes 1179648 | tf_op jit(solution)/shard_map/reshape | solution.py:143
  38.1 1.5 pad_bitcast_fusion.11
  39.6 1.2 copy.37
  40.7 1.2 copy.36
  42.0 4.5 %fusion.10 = bf16[2,6,144,768]{3,2,1,0:T(8,128)(2,1)} fusion(bf16[2,2,132,640]{3,2,1,0:T(8,128)(2,1)S(1)} %copy.37, bf16[2,2,132,640]{3,2,1,0:T(8,128)(2,1)S(1)} %copy.36, bf16[2,2,132,64]{3,2,1,0:T(8,128)(2,1)S(1)} %copy-done.12, bf16[2,2,132,64]{3,2,1,0:T(8,128)(2,1)S(1)} %copy-done.10, bf16[2,2,2,512]{3,2,1,0:T(2,128)(2,1)S(1)} %get-tuple-element.75, ...), kind=kLoop, calls=%fused_computation.12 | loop fusion | flops 41140224 | bytes 4681728 | tf_op jit(solution)/shard_map/concatenate | solution.py:54
  46.5 9.8 %first_conv.1 = (f32[2,576,640]{2,1,0:T(8,128)}, f32[32,8,128]{2,1,0:T(8,128)}) custom-call(bf16[2,864,768]{2,1,0:T(8,128)(2,1)} %bitcast.62, bf16[768,384]{1,0:T(8,128)(2,1)} %reshape.61.w_ref), custom_call_target="tpu_custom_call" | custom-call | tf_op jit(solution)/shard_map/first_conv/pallas_call | solution.py:20
  56.3 7.5 %all-to-all-start = ((f32[32,8,128]{2,1,0:T(8,128)}), f32[32,8,128]{2,1,0:T(8,128)}, u32[]{:S(2)}, u32[]{:S(2)}) async-start(f32[32,8,128]{2,1,0:T(8,128)} %get-tuple-element.21), calls=%async_computation | async-start | bytes 262144 | tf_op jit(solution)/shard_map/all_to_all | solution.py:59
  63.8 1.9 pad_maximum_fusion.1
  65.7 3.3 %copy.39 = bf16[3,8,32,3,4,32]{5,4,3,2,1,0:T(4,128)(2,1)} copy(bf16[3,8,32,3,4,32]{2,5,3,1,0,4:T(8,128)(2,1)S(1)} %pad_maximum_fusion.1) | data formatting | bytes 1179648 | tf_op jit(solution)/shard_map/stack | solution.py:143
  69.0 4.2 %reshape.62.w_ref = bf16[768,384]{1,0:T(8,128)(2,1)} reshape(bf16[3,8,32,3,4,32]{5,4,3,2,1,0:T(4,128)(2,1)} %copy.39) | data formatting | bytes 1179648 | tf_op jit(solution)/shard_map/reshape | solution.py:143
  74.4 9.4 %second_conv.1 = (bf16[576,640]{1,0:T(8,128)(2,1)}, f32[2,288,512]{2,1,0:T(8,128)}, f32[32,8,128]{2,1,0:T(8,128)}) custom-call(s32[6]{0:T(128)} %stack.114.bound, f32[2,576,640]{2,1,0:T(8,128)} %get-tuple-element.20.c_ref, bf16[768,384]{1,0:T(8,128)(2,1)} %reshape.62.w_ref, f32[32,8,128]{2,1,0:T(8,128)} %all-to-all-done.st_in, f32[4,128]{1,0:T(4,128)} %pad_maximum_fusion.12.p_ref), custom_call_target="tpu_custom_call" | custom-call | tf_op jit(solution)/shard_map/second_conv/pallas_call | solution.py:20
  83.8 14.5 %all_to_all.30.st_in = f32[32,8,128]{2,1,0:T(8,128)} all-to-all(f32[32,8,128]{2,1,0:T(8,128)} %get-tuple-element.23), channel_id=1, replica_groups=mesh['gx'=4,'gy'=4,'gz'=2] {'gx','gy','gz'}, dimensions={0} | all-to-all | bytes 262144 | tf_op jit(solution)/shard_map/all_to_all | solution.py:59
  98.3 4.2 %second_slope.1 = (bf16[32,2,16,128]{3,2,1,0:T(8,128)(2,1)}, f32[32,8,128]{2,1,0:T(8,128)}) custom-call(f32[2,288,512]{2,1,0:T(8,128)} %get-tuple-element.22.c_ref, f32[32,8,128]{2,1,0:T(8,128)} %all_to_all.30.st_in, f32[4,128]{1,0:T(4,128)} %pad_maximum_fusion.12.p_ref, bf16[288,512]{1,0:T(8,128)(2,1)} %get-tuple-element.24.go_ref), custom_call_target="tpu_custom_call" | custom-call | tf_op jit(solution)/shard_map/second_slope/pallas_call | solution.py:20
  102.5 2.8 %all-to-all-start.2 = ((f32[32,8,128]{2,1,0:T(8,128)}), f32[32,8,128]{2,1,0:T(8,128)S(1)}, u32[]{:S(2)}, u32[]{:S(2)}) async-start(f32[32,8,128]{2,1,0:T(8,128)} %get-tuple-element.26), calls=%async_computation.2 | async-start | bytes 262144 | tf_op jit(solution)/shard_map/all_to_all | solution.py:59
  105.3 8.4 %all-to-all-done.2.sums_in = f32[32,8,128]{2,1,0:T(8,128)S(1)} async-done(((f32[32,8,128]{2,1,0:T(8,128)}), f32[32,8,128]{2,1,0:T(8,128)S(1)}, u32[]{:S(2)}, u32[]{:S(2)}) %all-to-all-start.2) | async-done | bytes 131104 | tf_op jit(solution)/shard_map/all_to_all | solution.py:59
  114.3 3.7 %second_delta.1.d2_ref = bf16[288,512]{1,0:T(8,128)(2,1)} custom-call(f32[2,288,512]{2,1,0:T(8,128)} %get-tuple-element.22.c_ref, f32[32,8,128]{2,1,0:T(8,128)} %all_to_all.30.st_in, f32[4,128]{1,0:T(4,128)} %pad_maximum_fusion.12.p_ref, bf16[288,512]{1,0:T(8,128)(2,1)} %get-tuple-element.24.go_ref, f32[32,8,128]{2,1,0:T(8,128)} %copy-done.7), custom_call_target="tpu_custom_call" | custom-call | tf_op jit(solution)/shard_map/second_delta/pallas_call | solution.py:20
  119.6 2.9 %collective-permute-done.5 = bf16[1,2,2,512]{3,2,1,0:T(2,128)(2,1)S(1)} collective-permute-done((bf16[1,2,2,512]{3,2,1,0:T(2,128)(2,1)S(1)}, bf16[1,2,2,512]{3,2,1,0:T(2,128)(2,1)S(1)}, u32[]{:S(2)}, u32[]{:S(2)}) %collective-permute-start.5) | collective-permute-done | bytes 4128 | tf_op jit(solution)/shard_map/ppermute | solution.py:38
  122.6 1.3 collective-permute-start.6
  123.9 1.3 collective-permute-start.7
  125.9 1.5 collective-permute-done.7
  128.4 1.3 collective-permute-start.9
  129.7 4.6 %collective-permute-start.8 = (bf16[1,2,132,640]{3,2,1,0:T(8,128)(2,1)}, bf16[1,2,132,640]{3,2,1,0:T(8,128)(2,1)S(1)}, u32[]{:S(2)}, u32[]{:S(2)}) collective-permute-start(bf16[1,2,132,640]{3,2,1,0:T(8,128)(2,1)} %pad_maximum_fusion.5), channel_id=1, source_target_pairs={{0,8},{8,16},{16,24},{1,9},{9,17},{17,25},{2,10},{10,18},{18,26},{... | collective-permute-start | bytes 1013768 | tf_op jit(solution)/shard_map/ppermute | solution.py:43
  134.3 1.8 copy.40
  136.1 2.1 reshape.64.w_ref
  138.2 2.6 %slice_bitcast_fusion.c_ref = f32[576,640]{1,0:T(8,128)} fusion(f32[2,576,640]{2,1,0:T(8,128)} %get-tuple-element.20.c_ref), kind=kLoop, calls=%fused_computation.37 | loop fusion | bytes 2949120 | tf_op jit(solution)/shard_map/squeeze | solution.py:381
  141.3 2.7 %fusion.31 = bf16[1,6,144,768]{3,2,1,0:T(8,128)(2,1)} fusion(bf16[1,2,132,640]{3,2,1,0:T(8,128)(2,1)S(1)} %collective-permute-done.9, bf16[1,2,132,640]{3,2,1,0:T(8,128)(2,1)S(1)} %collective-permute-done.8, bf16[1,2,132,64]{3,2,1,0:T(8,128)(2,1)S(1)} %copy-done.16, bf16[1,2,132,64]{3,2,1,0:T(8,128)(2,1)S(1)} %copy-done.14, ...), kind=kLoop, calls=%fused_computation.40 | loop fusion | flops 20570112 | bytes 2340864 | tf_op jit(solution)/shard_map/concatenate | solution.py:54
  144.0 8.9 %first_slope.1 = (f32[576,640]{1,0:T(8,128)}, f32[32,8,128]{2,1,0:T(8,128)}, f32[288,96]{1,0:T(8,128)}) custom-call(bf16[864,768]{1,0:T(8,128)(2,1)} %bitcast.63, bf16[768,384]{1,0:T(8,128)(2,1)} %reshape.64.w_ref, f32[576,640]{1,0:T(8,128)} %slice_bitcast_fusion.c_ref, f32[32,8,128]{2,1,0:T(8,128)} %all-to-all-done.st_in, ...), custom_call_target="tpu_custom_call" | custom-call | tf_op jit(solution)/shard_map/first_slope/pallas_call | solution.py:20
  153.0 4.6 %all-to-all-start.3 = ((f32[32,8,128]{2,1,0:T(8,128)}), f32[32,8,128]{2,1,0:T(8,128)S(1)}, u32[]{:S(2)}, u32[]{:S(2)}) async-start(f32[32,8,128]{2,1,0:T(8,128)} %get-tuple-element.29), calls=%async_computation.3 | async-start | bytes 262144 | tf_op jit(solution)/shard_map/all_to_all | solution.py:59
  158.6 3.3 %copy.41 = bf16[3,8,32,3,4,32]{5,4,3,2,1,0:T(4,128)(2,1)} copy(bf16[3,8,32,3,4,32]{5,2,3,1,0,4:T(8,128)(2,1)S(1)} %pad_maximum_fusion.3) | data formatting | bytes 1179648 | tf_op jit(solution)/shard_map/stack | solution.py:143
  161.9 4.3 %reshape.65.w_ref = bf16[768,384]{1,0:T(8,128)(2,1)} reshape(bf16[3,8,32,3,4,32]{5,4,3,2,1,0:T(4,128)(2,1)} %copy.41) | data formatting | bytes 1179648 | tf_op jit(solution)/shard_map/reshape | solution.py:143
  166.3 1.2 slice.79
  168.1 9.7 %first_delta.1 = (bf16[32,2,16,128]{3,2,1,0:T(8,128)(2,1)}, f32[288,96]{1,0:T(8,128)}) custom-call(s32[6]{0:T(128)} %stack.114.bound, f32[576,640]{1,0:T(8,128)} %get-tuple-element.28.s_ref, f32[576,640]{1,0:T(8,128)} %slice_bitcast_fusion.c_ref, f32[32,8,128]{2,1,0:T(8,128)} %all-to-all-done.st_in, f32[4,128]{1,0:T(4,128)} %pad_maximum_fusion.12.p_ref, ...), custom_call_target="tpu_custom_call" | custom-call | tf_op jit(solution)/shard_map/first_delta/pallas_call | solution.py:20
  179.0 16.1 %all_to_all.31 = f32[32,16,128]{2,1,0:T(8,128)S(1)} all-to-all(f32[32,16,128]{2,1,0:T(8,128)S(1)} %bitcast.68), channel_id=1, replica_groups=mesh['gx'=4,'gy'=4,'gz'=2] {'gx','gy','gz'}, dimensions={0} | all-to-all | bytes 524288 | tf_op jit(solution)/shard_map/all_to_all | solution.py:59
  195.8 2.6 %all-to-all-start.5 = ((f32[32,16,128]{2,1,0:T(8,128)}), f32[32,16,128]{2,1,0:T(8,128)S(1)}, u32[]{:S(2)}, u32[]{:S(2)}) async-start(f32[32,16,128]{2,1,0:T(8,128)} %broadcast_in_dim.14), calls=%async_computation.5 | async-start | bytes 524288 | tf_op jit(solution)/shard_map/all_to_all | solution.py:59
  199.7 1.0 slice_reduce_fusion.3
  201.5 7.6 %all-to-all-done.5 = f32[32,16,128]{2,1,0:T(8,128)S(1)} async-done(((f32[32,16,128]{2,1,0:T(8,128)}), f32[32,16,128]{2,1,0:T(8,128)S(1)}, u32[]{:S(2)}, u32[]{:S(2)}) %all-to-all-start.5) | async-done | bytes 262176 | tf_op jit(solution)/shard_map/all_to_all | solution.py:59
  (106 shorter events, 19.1 us)
Async XLA Ops:
  0.6 26.4 %copy-start.22 = (f32[32]{0:T(128)S(1)}, f32[32]{0:T(128)}, u32[]{:S(2)}) copy-start(f32[32]{0:T(128)} %param.13) | copy-start | bytes 388
  0.6 27.1 %copy-start.23 = (f32[32]{0:T(128)S(1)}, f32[32]{0:T(128)}, u32[]{:S(2)}) copy-start(f32[32]{0:T(128)} %param.14) | copy-start | bytes 388
  0.7 27.7 %copy-start.24 = (f32[32]{0:T(128)S(1)}, f32[32]{0:T(128)}, u32[]{:S(2)}) copy-start(f32[32]{0:T(128)} %param.15) | copy-start | bytes 388
  0.7 28.3 %copy-start.25 = (f32[32]{0:T(128)S(1)}, f32[32]{0:T(128)}, u32[]{:S(2)}) copy-start(f32[32]{0:T(128)} %param.16) | copy-start | bytes 388
  0.7 28.9 %copy-start.5 = (bf16[3,3,3,32,32]{4,3,2,1,0:T(8,128)(2,1)S(1)}, bf16[3,3,3,32,32]{4,3,2,1,0:T(8,128)(2,1)}, u32[]{:S(2)}) copy-start(bf16[3,3,3,32,32]{4,3,2,1,0:T(8,128)(2,1)} %param.11) | copy-start | bytes 165892
  4.0 4.7 %collective-permute-start = (bf16[2,2,2,512]{3,2,1,0:T(2,128)(2,1)S(1)}, bf16[2,2,2,512]{3,2,1,0:T(2,128)(2,1)S(1)}, u32[]{:S(2)}, u32[]{:S(2)}) collective-permute-start(bf16[2,2,2,512]{3,2,1,0:T(2,128)(2,1)S(1)} %broadcast_select_fusion.1), channel_id=1, source_target_pairs={{0,1},{1,0},{2,3},{3,2},{4,5},{5,4},{6,7},{7,6},{8,9},{9,8},{10,11... | collective-permute-start | bytes 24584 | tf_op jit(solution)/shard_map/ppermute | solution.py:38
  9.9 2.6 %collective-permute-start.1 = (bf16[2,2,132,64]{3,2,1,0:T(8,128)(2,1)S(1)}, bf16[2,2,132,64]{3,2,1,0:T(8,128)(2,1)S(1)}, u32[]{:S(2)}, u32[]{:S(2)}) collective-permute-start(bf16[2,2,132,64]{3,2,1,0:T(8,128)(2,1)S(1)} %get-tuple-element.54), channel_id=1, source_target_pairs={{0,2},{2,4},{4,6},{1,3},{3,5},{5,7},{8,10},{10,12},{12,14},{9,11},... | collective-permute-start | bytes 202760 | tf_op jit(solution)/shard_map/ppermute | solution.py:43
  11.2 5.5 %collective-permute-start.2 = (bf16[2,2,132,64]{3,2,1,0:T(8,128)(2,1)S(1)}, bf16[2,2,132,64]{3,2,1,0:T(8,128)(2,1)S(1)}, u32[]{:S(2)}, u32[]{:S(2)}) collective-permute-start(bf16[2,2,132,64]{3,2,1,0:T(8,128)(2,1)S(1)} %get-tuple-element.55), channel_id=1, source_target_pairs={{2,0},{4,2},{6,4},{3,1},{5,3},{7,5},{10,8},{12,10},{14,12},{11,9},... | collective-permute-start | bytes 202760 | tf_op jit(solution)/shard_map/ppermute | solution.py:43
  12.5 4.2 %copy-start.9 = (bf16[2,2,132,64]{3,2,1,0:T(8,128)(2,1)}, bf16[2,2,132,64]{3,2,1,0:T(8,128)(2,1)S(1)}, u32[]{:S(2)}) copy-start(bf16[2,2,132,64]{3,2,1,0:T(8,128)(2,1)S(1)} %collective-permute-done.1) | copy-start | bytes 202756
  16.7 0.7 copy-start.11
  20.3 19.2 %collective-permute-start.4 = (bf16[2,2,132,640]{3,1,2,0:T(2,128)(2,1)}, bf16[2,2,132,640]{3,1,2,0:T(2,128)(2,1)}, u32[]{:S(2)}, u32[]{:S(2)}) collective-permute-start(bf16[2,2,132,640]{3,1,2,0:T(2,128)(2,1)} %copy.34), channel_id=1, source_target_pairs={{8,0},{16,8},{24,16},{9,1},{17,9},{25,17},{10,2},{18,10},{26,18},{... | collective-permute-start | bytes 2027528 | tf_op jit(solution)/shard_map/ppermute | solution.py:43
  21.6 19.1 %collective-permute-start.3 = (bf16[2,2,132,640]{3,1,2,0:T(2,128)(2,1)}, bf16[2,2,132,640]{3,1,2,0:T(2,128)(2,1)}, u32[]{:S(2)}, u32[]{:S(2)}) collective-permute-start(bf16[2,2,132,640]{3,1,2,0:T(2,128)(2,1)} %copy.34), channel_id=1, source_target_pairs={{0,8},{8,16},{16,24},{1,9},{9,17},{17,25},{2,10},{10,18},{18,26},{... | collective-permute-start | bytes 2027528 | tf_op jit(solution)/shard_map/ppermute | solution.py:43
  33.9 4.2 %copy-start.3 = (bf16[3,3,3,32,32]{4,3,2,1,0:T(8,128)(2,1)S(1)}, bf16[3,3,3,32,32]{4,3,2,1,0:T(8,128)(2,1)}, u32[]{:S(2)}) copy-start(bf16[3,3,3,32,32]{4,3,2,1,0:T(8,128)(2,1)} %param.12) | copy-start | bytes 165892
  38.1 3.8 %copy-start.1 = (bf16[2,2,128,512]{3,2,1,0:T(8,128)(2,1)S(1)}, bf16[2,2,128,512]{3,2,1,0:T(8,128)(2,1)}, u32[]{:S(2)}) copy-start(bf16[2,2,128,512]{3,2,1,0:T(8,128)(2,1)} %get-tuple-element.19) | copy-start | bytes 1572868
  38.1 3.9 %copy-start.10 = (bf16[2,2,132,64]{3,2,1,0:T(8,128)(2,1)S(1)}, bf16[2,2,132,64]{3,2,1,0:T(8,128)(2,1)}, u32[]{:S(2)}) copy-start(bf16[2,2,132,64]{3,2,1,0:T(8,128)(2,1)} %copy-done.9) | copy-start | bytes 202756
  38.1 3.9 %copy-start.12 = (bf16[2,2,132,64]{3,2,1,0:T(8,128)(2,1)S(1)}, bf16[2,2,132,64]{3,2,1,0:T(8,128)(2,1)}, u32[]{:S(2)}) copy-start(bf16[2,2,132,64]{3,2,1,0:T(8,128)(2,1)} %copy-done.11) | copy-start | bytes 202756
  56.3 18.1 %all-to-all-start = ((f32[32,8,128]{2,1,0:T(8,128)}), f32[32,8,128]{2,1,0:T(8,128)}, u32[]{:S(2)}, u32[]{:S(2)}) async-start(f32[32,8,128]{2,1,0:T(8,128)} %get-tuple-element.21), calls=%async_computation | async-start | bytes 262144 | tf_op jit(solution)/shard_map/all_to_all | solution.py:59
  69.0 4.8 %copy-start.18 = (f32[1,128]{1,0:T(1,128)S(1)}, f32[1,128]{1,0:T(1,128)}, u32[]{:S(2)}) copy-start(f32[1,128]{1,0:T(1,128)} %stack_tile.12) | copy-start | bytes 1540
  69.0 4.8 %copy-start.19 = (f32[1,128]{1,0:T(1,128)S(1)}, f32[1,128]{1,0:T(1,128)}, u32[]{:S(2)}) copy-start(f32[1,128]{1,0:T(1,128)} %stack_tile.13) | copy-start | bytes 1540
  69.0 4.8 %copy-start.20 = (f32[1,128]{1,0:T(1,128)S(1)}, f32[1,128]{1,0:T(1,128)}, u32[]{:S(2)}) copy-start(f32[1,128]{1,0:T(1,128)} %stack_tile.14) | copy-start | bytes 1540
  69.0 4.8 %copy-start.21 = (f32[1,128]{1,0:T(1,128)S(1)}, f32[1,128]{1,0:T(1,128)}, u32[]{:S(2)}) copy-start(f32[1,128]{1,0:T(1,128)} %stack_tile.15) | copy-start | bytes 1540
  74.4 30.8 %copy-start.4 = (bf16[3,3,3,32,32]{4,3,2,1,0:T(8,128)(2,1)S(1)}, bf16[3,3,3,32,32]{4,3,2,1,0:T(8,128)(2,1)}, u32[]{:S(2)}) copy-start(bf16[3,3,3,32,32]{4,3,2,1,0:T(8,128)(2,1)} %param.12) | copy-start | bytes 165892
  102.5 11.2 %all-to-all-start.2 = ((f32[32,8,128]{2,1,0:T(8,128)}), f32[32,8,128]{2,1,0:T(8,128)S(1)}, u32[]{:S(2)}, u32[]{:S(2)}) async-start(f32[32,8,128]{2,1,0:T(8,128)} %get-tuple-element.26), calls=%async_computation.2 | async-start | bytes 262144 | tf_op jit(solution)/shard_map/all_to_all | solution.py:59
  113.6 0.7 copy-start.7
  118.0 1.6 copy-start.2
  118.8 3.7 %collective-permute-start.5 = (bf16[1,2,2,512]{3,2,1,0:T(2,128)(2,1)S(1)}, bf16[1,2,2,512]{3,2,1,0:T(2,128)(2,1)S(1)}, u32[]{:S(2)}, u32[]{:S(2)}) collective-permute-start(bf16[1,2,2,512]{3,2,1,0:T(2,128)(2,1)S(1)} %broadcast_select_fusion.4), channel_id=1, source_target_pairs={{0,1},{1,0},{2,3},{3,2},{4,5},{5,4},{6,7},{7,6},{8,9},{9,8},{10,11... | collective-permute-start | bytes 12296 | tf_op jit(solution)/shard_map/ppermute | solution.py:38
  122.6 3.2 %collective-permute-start.6 = (bf16[1,2,132,64]{3,2,1,0:T(8,128)(2,1)S(1)}, bf16[1,2,132,64]{3,2,1,0:T(8,128)(2,1)S(1)}, u32[]{:S(2)}, u32[]{:S(2)}) collective-permute-start(bf16[1,2,132,64]{3,2,1,0:T(8,128)(2,1)S(1)} %get-tuple-element.56), channel_id=1, source_target_pairs={{0,2},{2,4},{4,6},{1,3},{3,5},{5,7},{8,10},{10,12},{12,14},{9,11},... | collective-permute-start | bytes 101384 | tf_op jit(solution)/shard_map/ppermute | solution.py:43
  123.9 3.5 %collective-permute-start.7 = (bf16[1,2,132,64]{3,2,1,0:T(8,128)(2,1)S(1)}, bf16[1,2,132,64]{3,2,1,0:T(8,128)(2,1)S(1)}, u32[]{:S(2)}, u32[]{:S(2)}) collective-permute-start(bf16[1,2,132,64]{3,2,1,0:T(8,128)(2,1)S(1)} %get-tuple-element.57), channel_id=1, source_target_pairs={{2,0},{4,2},{6,4},{3,1},{5,3},{7,5},{10,8},{12,10},{14,12},{11,9},... | collective-permute-start | bytes 101384 | tf_op jit(solution)/shard_map/ppermute | solution.py:43
  125.2 9.0 %copy-start.6 = (bf16[3,3,3,32,32]{4,3,2,1,0:T(8,128)(2,1)S(1)}, bf16[3,3,3,32,32]{4,3,2,1,0:T(8,128)(2,1)}, u32[]{:S(2)}) copy-start(bf16[3,3,3,32,32]{4,3,2,1,0:T(8,128)(2,1)} %param.11) | copy-start | bytes 165892
  125.9 8.4 %copy-start.13 = (bf16[1,2,132,64]{3,2,1,0:T(8,128)(2,1)}, bf16[1,2,132,64]{3,2,1,0:T(8,128)(2,1)S(1)}, u32[]{:S(2)}) copy-start(bf16[1,2,132,64]{3,2,1,0:T(8,128)(2,1)S(1)} %collective-permute-done.6) | copy-start | bytes 101380
  127.4 6.9 %copy-start.15 = (bf16[1,2,132,64]{3,2,1,0:T(8,128)(2,1)}, bf16[1,2,132,64]{3,2,1,0:T(8,128)(2,1)S(1)}, u32[]{:S(2)}) copy-start(bf16[1,2,132,64]{3,2,1,0:T(8,128)(2,1)S(1)} %collective-permute-done.7) | copy-start | bytes 101380
  128.4 12.5 %collective-permute-start.9 = (bf16[1,2,132,640]{3,2,1,0:T(8,128)(2,1)}, bf16[1,2,132,640]{3,2,1,0:T(8,128)(2,1)S(1)}, u32[]{:S(2)}, u32[]{:S(2)}) collective-permute-start(bf16[1,2,132,640]{3,2,1,0:T(8,128)(2,1)} %pad_maximum_fusion.5), channel_id=1, source_target_pairs={{8,0},{16,8},{24,16},{9,1},{17,9},{25,17},{10,2},{18,10},{26,18},{... | collective-permute-start | bytes 1013768 | tf_op jit(solution)/shard_map/ppermute | solution.py:43
  129.7 11.7 %collective-permute-start.8 = (bf16[1,2,132,640]{3,2,1,0:T(8,128)(2,1)}, bf16[1,2,132,640]{3,2,1,0:T(8,128)(2,1)S(1)}, u32[]{:S(2)}, u32[]{:S(2)}) collective-permute-start(bf16[1,2,132,640]{3,2,1,0:T(8,128)(2,1)} %pad_maximum_fusion.5), channel_id=1, source_target_pairs={{0,8},{8,16},{16,24},{1,9},{9,17},{17,25},{2,10},{10,18},{18,26},{... | collective-permute-start | bytes 1013768 | tf_op jit(solution)/shard_map/ppermute | solution.py:43
  138.2 3.1 %copy-start.14 = (bf16[1,2,132,64]{3,2,1,0:T(8,128)(2,1)S(1)}, bf16[1,2,132,64]{3,2,1,0:T(8,128)(2,1)}, u32[]{:S(2)}) copy-start(bf16[1,2,132,64]{3,2,1,0:T(8,128)(2,1)} %copy-done.13) | copy-start | bytes 101380
  138.2 3.1 %copy-start.16 = (bf16[1,2,132,64]{3,2,1,0:T(8,128)(2,1)S(1)}, bf16[1,2,132,64]{3,2,1,0:T(8,128)(2,1)}, u32[]{:S(2)}) copy-start(bf16[1,2,132,64]{3,2,1,0:T(8,128)(2,1)} %copy-done.15) | copy-start | bytes 101380
  153.0 14.5 %all-to-all-start.3 = ((f32[32,8,128]{2,1,0:T(8,128)}), f32[32,8,128]{2,1,0:T(8,128)S(1)}, u32[]{:S(2)}, u32[]{:S(2)}) async-start(f32[32,8,128]{2,1,0:T(8,128)} %get-tuple-element.29), calls=%async_computation.3 | async-start | bytes 262144 | tf_op jit(solution)/shard_map/all_to_all | solution.py:59
  161.9 4.3 %copy-start = (bf16[2,6,144,768]{3,2,1,0:T(8,128)(2,1)S(1)}, bf16[2,6,144,768]{3,2,1,0:T(8,128)(2,1)}, u32[]{:S(2)}) copy-start(bf16[2,6,144,768]{3,2,1,0:T(8,128)(2,1)} %fusion.10) | copy-start | bytes 7962628
  167.4 0.6 copy-start.8
  168.1 9.7 %copy-start.17 = (f32[288,96]{1,0:T(8,128)S(1)}, f32[288,96]{1,0:T(8,128)}, u32[]{:S(2)}) copy-start(f32[288,96]{1,0:T(8,128)} %get-tuple-element.32) | copy-start | bytes 331780
  195.8 13.3 %all-to-all-start.5 = ((f32[32,16,128]{2,1,0:T(8,128)}), f32[32,16,128]{2,1,0:T(8,128)S(1)}, u32[]{:S(2)}, u32[]{:S(2)}) async-start(f32[32,16,128]{2,1,0:T(8,128)} %broadcast_in_dim.14), calls=%async_computation.5 | async-start | bytes 524288 | tf_op jit(solution)/shard_map/all_to_all | solution.py:59

commit v2 on v0

v2 whole, which is shorter than its diff:
```python
import math

import jax
import jax.numpy as jnp
from jax import lax
from jax.experimental import pallas as pl
from jax.experimental.pallas import tpu as pltpu
from jax.sharding import PartitionSpec as P

EPSILON = 1e-05
AXES = ("gx", "gy", "gz")
LANES = 128
SEAM = 16
BF = jnp.bfloat16
F32 = jnp.float32
VM = pl.BlockSpec(memory_space=pltpu.VMEM)
SM = pl.BlockSpec(memory_space=pltpu.SMEM)


def kernel_call(body, name, out_shape, args, scratch=(), smem=0, work=0):
    return pl.pallas_call(
        body,
        out_shape=out_shape,
        in_specs=[SM] * smem + [VM] * (len(args) - smem),
        out_specs=[VM] * len(out_shape),
        scratch_shapes=list(scratch),
        cost_estimate=pl.CostEstimate(flops=work, bytes_accessed=1 << 20, transcendentals=0),
        compiler_params=pltpu.CompilerParams(vmem_limit_bytes=8 << 20),
        name=name,
    )(*args)


def shape(dims, kind):
    return jax.ShapeDtypeStruct(dims, kind)


def exchange(spread_rows):
    return lax.all_to_all(spread_rows, AXES, 0, 0)


def neighbours(axis):
    count = lax.axis_size(axis)
    forward = [(i, i + 1) for i in range(count - 1)]
    return forward, [(t, s) for s, t in forward]


def order_matrix(chan, rows):
    size = chan * rows
    k = lax.broadcasted_iota(jnp.int32, (size, size), 0)
    n = lax.broadcasted_iota(jnp.int32, (size, size), 1)
    return (n == (k % rows) * chan + k // rows).astype(BF)


def lane_at(group):
    return pl.ds(pl.multiple_of(group * LANES, LANES), LANES)


def band_conv(src, weight, group, planes, pitch):
    size = planes * pitch + SEAM
    at = pl.multiple_of(group * LANES, LANES)
    parts = [src[pl.ds(d * pitch, size), pl.ds(at, 2 * LANES)] for d in range(3)]
    out = jnp.dot(jnp.concatenate(parts, axis=1), weight[...], preferred_element_type=F32)
    return (
        pltpu.roll(out[:, :LANES], 1, 0)
        + out[:, LANES : 2 * LANES]
        + pltpu.roll(out[:, 2 * LANES :], size - 1, 0)
    )


def tap_products(d_rows, h_ref, start, group, pitch, acc):
    size = d_rows.shape[0]
    three = jnp.concatenate(
        [pltpu.roll(d_rows, size - 1, 0), d_rows, pltpu.roll(d_rows, 1, 0)], axis=1
    )
    left = three.T.astype(BF)
    at = pl.multiple_of(group * LANES, LANES)
    for d in range(3):
        right = h_ref[pl.ds(start + d * pitch, size), pl.ds(at, 2 * LANES)]
        acc[d] = acc[d] + jnp.dot(left, right, preferred_element_type=F32)


def fold_taps(acc, out, first, chan, offset):
    per = LANES // chan
    for d in range(3):
        for t in range(3):
            rows = sum(
                acc[
                    d,
                    t * LANES + j * chan : t * LANES + (j + 1) * chan,
                    (j + offset) * chan : (j + offset + 3) * chan,
                ]
                for j in range(per)
            )
            for y in range(3):
                row, lane = divmod((d * 3 + y) * 3 + t, per)
                out[
                    first + row * chan : first + (row + 1) * chan, lane * chan : (lane + 1) * chan
                ] = rows[:, y * chan : (y + 1) * chan].astype(out.dtype)


def fold_lanes(value, chan):
    step = chan
    while step < LANES:
        value = value + pltpu.roll(value, step, 1)
        step *= 2
    return value


def gathered(ref, row, chan):
    return fold_lanes(jnp.sum(ref[:, row, :], axis=0, keepdims=True), chan)


def sigmoid(value):
    return 0.5 + 0.5 * jnp.tanh(0.5 * value)


def body(x_a, x_b, w_first, w_second, gain_first, bias_first, gain_second, bias_second, grad_out):
    chan, span_x, span_y, span_z = x_a.shape
    world = lax.axis_size("gx") * lax.axis_size("gy") * lax.axis_size("gz")
    voxels = float(span_x * span_y * span_z * world)
    factor = 1.0 / math.sqrt(voxels)
    per = LANES // chan
    line = span_y * chan
    tiles = line // LANES
    pitch = span_z + SEAM
    inner_groups = span_y // per
    outer_groups = inner_groups + 1
    wide = line + 2 * LANES
    mid = outer_groups * LANES
    po, pi = span_x + 2, span_x
    so, si, sw = po * pitch + SEAM, pi * pitch + SEAM, (span_x + 4) * pitch + SEAM
    flat_rows = span_x * span_z
    seams = (span_x + 1) * SEAM
    strip = si + tiles * seams
    swap = lax.axis_size("gz") == 2
    edges = 1 if swap else 2

    def limits(axis, low, high):
        at, count = lax.axis_index(axis), lax.axis_size(axis)
        return [jnp.where(at == 0, low + 1, low), jnp.where(at == count - 1, high - 1, high)]

    bounds = jnp.stack(
        limits("gx", 0, span_x + 2)
        + limits("gy", 0, span_y + 2)
        + limits("gz", -1, span_z + 1)
        + [lax.axis_index("gz"), lax.axis_index("gy") % 2]
    ).astype(jnp.int32)

    def fill_inside(bound, ref):
        row = lax.broadcasted_iota(jnp.int32, (so, LANES), 0) + (pitch - SEAM + 2)
        plane = row // pitch - 1
        z = row % pitch - 2
        ok = (plane >= bound[0]) & (plane < bound[1]) & (z >= bound[4]) & (z < bound[5])
        ref[...] = ok.astype(F32)

    def inside(bound, ref, group):
        lane = lax.broadcasted_iota(jnp.int32, (so, LANES), 1) + group * LANES
        y = lane // chan
        return (ref[...] > 0.5) & (y >= bound[2]) & (y < bound[3])

    def fill_own(ref):
        row = lax.broadcasted_iota(jnp.int32, (si, LANES), 0)
        ref[...] = ((row >= SEAM) & ((row - SEAM + pitch) % pitch < span_z)).astype(F32)

    def own(ref, group):
        lane = lax.broadcasted_iota(jnp.int32, (si, LANES), 1) + group * LANES
        return (ref[...] > 0.5) & (lane >= chan) & (lane < chan + line)

    own_scratch = pltpu.VMEM((si, LANES), F32)
    in_scratch = pltpu.VMEM((so, LANES), F32)


    def fill_bands(work):
        for out, w_ref, back, offset in work:
            out[...] = jnp.zeros(out.shape, BF)
            for dx in range(3):
                for dy in range(3):
                    for dz in range(3):
                        if back:
                            block = w_ref[2 - dx, 2 - dy, 2 - dz]
                        else:
                            block = w_ref[dx, dy, dz].astype(F32).T.astype(BF)
                        for j in range(per):
                            row = (dx * 2 * per + dy + j + offset) * chan
                            lane = dz * LANES + j * chan
                            out[row : row + chan, lane : lane + chan] = block

    def bands(w1_ref, w2_ref, g1_ref, b1_ref, g2_ref, b2_ref, one_ref, two_ref, p_ref):
        fill_bands(((one_ref, w1_ref, False, 2), (two_ref, w2_ref, False, 0)))
        p_ref[...] = jnp.zeros(p_ref.shape, F32)
        for row, ref in enumerate((g1_ref, b1_ref, g2_ref, b2_ref)):
            for j in range(per):
                p_ref[row : row + 1, j * chan : (j + 1) * chan] = ref[...]

    def back_bands(w1_ref, w2_ref, token, two_ref, one_ref):
        del token
        fill_bands(((two_ref, w2_ref, True, 2), (one_ref, w1_ref, True, 0)))

    band_shape = shape((6 * LANES, 3 * LANES), BF)
    token_shape = shape((8, LANES), F32)
    vectors = (gain_first, bias_first, gain_second, bias_second)
    band_one, band_two, params = kernel_call(
        bands,
        "bands",
        [band_shape, band_shape, token_shape],
        [w_first, w_second] + [v.reshape(1, chan) for v in vectors],
        work=1 << 31,
    )


    def turned(block, order):
        return lax.dot_general(
            block.reshape(chan * span_y, span_z),
            order,
            (((0,), (0,)), ((), ())),
            preferred_element_type=F32,
        ).astype(BF)

    def native(value, order):
        return lax.dot_general(
            order, value, (((1,), (1,)), ((), ())), preferred_element_type=F32
        ).astype(BF).reshape(chan, span_y, span_z)

    def z_tiles(bound, ref, at, v, z_ref):
        first = ref[at * span_z : at * span_z + SEAM, :]
        last = ref[(at + 1) * span_z - SEAM : (at + 1) * span_z, :]
        rows = slice(at * SEAM, (at + 1) * SEAM)
        if swap:
            pick = jnp.full(first.shape, bound[6], jnp.int32) == 0
            z_ref[0, rows] = jnp.where(pick, last.astype(F32), first.astype(F32)).astype(BF)
        else:
            z_ref[0, rows] = last
            z_ref[1, rows] = first

    def turn_in(bound, a_ref, b_ref, t_ref, z_ref):
        order = order_matrix(chan, span_y)
        for v, ref in enumerate((a_ref, b_ref)):
            for x in range(span_x):
                at = v * span_x + x
                t_ref[at * span_z : (at + 1) * span_z, :] = turned(ref[:, x], order)
                z_tiles(bound, t_ref, at, v, z_ref)

    def turn_cot(g_ref, o_ref):
        order = order_matrix(chan, span_y)
        o_ref[...] = jnp.zeros(o_ref.shape, BF)
        for x in range(span_x):
            at = SEAM + x * pitch
            o_ref[at : at + span_z, :] = turned(g_ref[:, x], order)


    def halo(block, tiles_z, count, token):
        forward_x, backward_x = neighbours("gx")
        rows_y = lax.axis_size("gy")
        pairs_y = [
            [p for i in range(first, rows_y - 1, 2) for p in ((i, i + 1), (i + 1, i))]
            for first in range(2)
        ]
        forward_z, backward_z = neighbours("gz")
        if swap:
            got_z = [lax.ppermute(tiles_z[0], "gz", [(0, 1), (1, 0)])]
        else:
            got_z = [
                lax.ppermute(tiles_z[0], "gz", forward_z),
                lax.ppermute(tiles_z[1], "gz", backward_z),
            ]

        def edge(bound, t_ref, *refs):
            got, (a_ref, b_ref, s_ref) = refs[:edges], refs[edges:]
            even = jnp.full((SEAM, LANES), bound[7], jnp.int32) == 0
            even_block = jnp.full((span_z, LANES), bound[7], jnp.int32) == 0

            def send(rows, low, high, ok):
                low, high = low.astype(F32), high.astype(F32)
                a_ref[rows, :] = jnp.where(ok, high, low).astype(BF)
                b_ref[rows, :] = jnp.where(ok, low, high).astype(BF)

            row = lax.broadcasted_iota(jnp.int32, (SEAM, line), 0)
            for v in range(count):
                parts = []
                for x in range(span_x + 1):
                    tile = jnp.zeros((SEAM, line), F32)
                    if x < span_x:
                        at = (v * span_x + x) * SEAM
                        value = got[0][at : at + SEAM, :].astype(F32)
                        ok = row >= SEAM - 2
                        if swap:
                            ok = ok & (jnp.full(row.shape, bound[6], jnp.int32) == 1)
                        tile = jnp.where(ok, value, tile)
                    if x > 0:
                        at = (v * span_x + x - 1) * SEAM
                        value = got[-1][at : at + SEAM, :].astype(F32)
                        ok = row < 2
                        if swap:
                            ok = ok & (jnp.full(row.shape, bound[6], jnp.int32) == 0)
                        tile = jnp.where(ok, value, tile)
                    parts.append(tile.astype(BF))
                for x in range(span_x + 1):
                    s_ref[v * seams + x * SEAM : v * seams + (x + 1) * SEAM, :] = parts[x]
                    base = v * si + x * pitch
                    send(
                        slice(base, base + SEAM),
                        parts[x][:, :LANES],
                        parts[x][:, line - LANES :],
                        even,
                    )
                    if x < span_x:
                        own_rows = slice((v * span_x + x) * span_z, (v * span_x + x + 1) * span_z)
                        rows = slice(base + SEAM, base + pitch)
                        send(
                            rows,
                            t_ref[own_rows, :LANES],
                            t_ref[own_rows, line - LANES :],
                            even_block,
                        )

        send_a, send_b, seam_rows = kernel_call(
            edge,
            "edge",
            [shape((count * si, LANES), BF)] * 2 + [shape((count * seams, line), BF)],
            [bounds, block] + got_z,
            smem=1,
        )
        got_a = lax.ppermute(send_a, "gy", pairs_y[0])
        got_b = lax.ppermute(send_b, "gy", pairs_y[1])

        def strips(bound, a_ref, b_ref, s_ref, token_ref, o_ref):
            del token_ref
            lane = lax.broadcasted_iota(jnp.int32, (si, LANES), 1)
            from_a = (lane < 2 * chan) == (jnp.full(lane.shape, bound[7], jnp.int32) == 0)
            for v in range(count):
                rows = slice(v * si, (v + 1) * si)
                o_ref[v * strip : v * strip + si, :] = jnp.where(
                    from_a, a_ref[rows, :].astype(F32), b_ref[rows, :].astype(F32)
                ).astype(BF)
                for t in range(tiles):
                    at = v * strip + si + t * seams
                    o_ref[at : at + seams, :] = s_ref[
                        v * seams : (v + 1) * seams, t * LANES : (t + 1) * LANES
                    ]

        (mine,) = kernel_call(
            strips,
            "strips",
            [shape((count * strip, LANES), BF)],
            [bounds, got_a, got_b, seam_rows, token],
            smem=1,
        )
        return [
            lax.ppermute(block, "gx", forward_x),
            block,
            lax.ppermute(block, "gx", backward_x),
            lax.ppermute(mine, "gx", forward_x),
            mine,
            lax.ppermute(mine, "gx", backward_x),
        ]

    def assemble(dest, v, pieces):
        blocks, strip_refs = pieces[:3], pieces[3:]
        lane = lax.broadcasted_iota(jnp.int32, (si, LANES), 1)
        edge_tiles = {}

        def put(seam, columns, value):
            if seam in edge_tiles and columns in edge_tiles[seam]:
                value = edge_tiles[seam].pop(columns) + value
                dest[seam : seam + SEAM, columns[0] : columns[1]] = value
            else:
                edge_tiles.setdefault(seam, {})[columns] = value

        for b in range(3):
            base = b * span_x * pitch
            for x in range(span_x):
                at = base + SEAM + x * pitch
                rows = slice((v * span_x + x) * span_z, (v * span_x + x + 1) * span_z)
                dest[at : at + span_z, LANES : LANES + line] = blocks[b][rows, :]
            ys = strip_refs[b][v * strip : v * strip + si, :].astype(F32)
            low = jnp.where(lane >= 2 * chan, ys, 0.0).astype(BF)
            high = jnp.where(lane < 2 * chan, ys, 0.0).astype(BF)
            last = si - SEAM
            for columns, value in (((0, LANES), low), ((LANES + line, wide), high)):
                dest[base + SEAM : base + last, columns[0] : columns[1]] = value[SEAM:last]
                put(base, columns, value[:SEAM])
                put(base + last, columns, value[last:])
            for t in range(tiles):
                at = v * strip + si + t * seams
                columns = (LANES * (t + 1), LANES * (t + 2))
                for x in range(span_x + 1):
                    value = strip_refs[b][at + x * SEAM : at + (x + 1) * SEAM, :]
                    seam = base + x * pitch
                    if 0 < x < span_x:
                        dest[seam : seam + SEAM, columns[0] : columns[1]] = value
                    else:
                        put(seam, columns, value)
        for seam, left in edge_tiles.items():
            for columns, value in left.items():
                dest[seam : seam + SEAM, columns[0] : columns[1]] = value


    stat_shape = shape((world, 4, LANES), F32)

    def send_rows(ref, rows):
        rows = list(rows)
        spare = ref.shape[1] - sum(r.shape[0] for r in rows)
        if spare:
            rows.append(jnp.zeros((spare, LANES), F32))
        ref[...] = jnp.broadcast_to(jnp.concatenate(rows, axis=0)[None], ref.shape)

    def moments(st_ref, row):
        mean = gathered(st_ref, row, chan) / voxels
        var = gathered(st_ref, row + 1, chan) / voxels - mean * mean
        return mean, lax.rsqrt(var + EPSILON)

    def add_up(sums, value, other):
        return (
            sums[0] + jnp.sum(value, axis=0, keepdims=True),
            sums[1] + jnp.sum(value * other, axis=0, keepdims=True),
        )

    def conv_one_of(v, w_ref, pieces, dest, c_ref, own_ref):
        fill_own(own_ref)
        assemble(dest, v, pieces)

        def step(g, sums):
            out = band_conv(dest, w_ref, g, po, pitch)
            c_ref[:, lane_at(g)] = out
            mine = jnp.where(own(own_ref, g), out[pitch : pitch + si], 0.0)
            return add_up(sums, mine, mine)

        return lax.fori_loop(0, outer_groups, step, (zero(), zero()))

    def zero():
        return jnp.zeros((1, LANES), F32)

    def first_conv_b(w_ref, *refs):
        pieces, (c_ref, x_ref, st_ref, own_ref) = refs[:6], refs[6:]
        send_rows(st_ref, conv_one_of(1, w_ref, pieces, x_ref, c_ref, own_ref))

    def first_conv_a(w_ref, *refs):
        pieces, (c_ref, st_ref, x_ref, own_ref) = refs[:6], refs[6:]
        rows = list(conv_one_of(0, w_ref, pieces, x_ref, c_ref, own_ref))
        st_ref[...] = jnp.concatenate(rows + [jnp.zeros((6, LANES), F32)], axis=0)

    def conv_two_of(bound, c_ref, w_ref, st_in, row, p_ref, h_ref, c2_ref, own_ref, in_ref):
        fill_own(own_ref)
        fill_inside(bound, in_ref)
        mean, rstd = moments(st_in, row)
        gain, bias = p_ref[0:1, :], p_ref[1:2, :]

        def act(g, carry):
            at = lane_at(g)
            z = gain * ((c_ref[:, at] - mean) * rstd) + bias
            h_ref[:, at] = jnp.where(inside(bound, in_ref, g), z * sigmoid(z), 0.0).astype(BF)
            return carry

        lax.fori_loop(0, outer_groups, act, 0)

        def step(g, sums):
            out = band_conv(h_ref, w_ref, g, pi, pitch)
            c2_ref[:, lane_at(g)] = out
            mine = jnp.where(own_ref[...] > 0.5, out, 0.0)
            return add_up(sums, mine, mine)

        return lax.fori_loop(0, inner_groups, step, (zero(), zero()))

    def second_conv_b(bound, c_ref, w_ref, st_in, p_ref, more, h_ref, c2_ref, st_ref, token_ref, own_ref, in_ref):
        token_ref[...] = jnp.zeros(token_ref.shape, F32)
        rows = conv_two_of(bound, c_ref, w_ref, st_in, 0, p_ref, h_ref, c2_ref, own_ref, in_ref)
        send_rows(st_ref, list(rows) + [more[0:2, :]])

    def second_conv_a(bound, c_ref, w_ref, st_in, p_ref, after, c2_ref, st_ref, h_ref, own_ref, in_ref):
        del after
        rows = conv_two_of(bound, c_ref, w_ref, st_in, 2, p_ref, h_ref, c2_ref, own_ref, in_ref)
        st_ref[...] = jnp.concatenate(list(rows) + [jnp.zeros((6, LANES), F32)], axis=0)

    def slope_two(c_ref, moment, p_ref, go_ref, own_ref, at):
        mean, rstd = moment
        xhat = (c_ref[:, at] - mean) * rstd
        z = p_ref[2:3, :] * xhat + p_ref[3:4, :]
        s = sigmoid(z)
        d = go_ref[:, at].astype(F32) * (s * (1.0 + z * (1.0 - s)))
        return jnp.where(own_ref[...] > 0.5, d, 0.0), xhat

    def second_slope(c_ref, st_in, p_ref, go_ref, st_ref, token_ref, own_ref):
        token_ref[...] = jnp.zeros(token_ref.shape, F32)
        fill_own(own_ref)
        moment = moments(st_in, 0)

        def step(g, sums):
            d, xhat = slope_two(c_ref, moment, p_ref, go_ref, own_ref, lane_at(g))
            return add_up(sums, d, xhat)

        send_rows(st_ref, lax.fori_loop(0, inner_groups, step, (zero(), zero())))

    def second_delta(bound, c_ref, st_in, p_ref, go_ref, sums_in, after, d_ref, t_ref, z_ref, own_ref):
        del after
        fill_own(own_ref)
        moment = moments(st_in, 0)
        scale = p_ref[2:3, :] * moment[1]
        sum_d, sum_x = gathered(sums_in, 0, chan) / voxels, gathered(sums_in, 1, chan) / voxels

        def step(g, carry):
            at = lane_at(g)
            d, xhat = slope_two(c_ref, moment, p_ref, go_ref, own_ref, at)
            out = scale * (d - sum_d - xhat * sum_x)
            d_ref[:, at] = jnp.where(own_ref[...] > 0.5, out, 0.0).astype(BF)
            return carry

        lax.fori_loop(0, inner_groups, step, 0)
        for x in range(span_x):
            base = SEAM + x * pitch
            t_ref[x * span_z : (x + 1) * span_z, :] = d_ref[base : base + span_z, :]
            z_tiles(bound, t_ref, x, 0, z_ref)

    def second_taps(d_ref, h_ref, after, gw_ref, acc):
        del after
        acc[...] = jnp.zeros(acc.shape, F32)

        def taps(g, carry):
            tap_products(d_ref[:, lane_at(g)].astype(F32), h_ref, 0, g, pitch, acc)
            return carry

        lax.fori_loop(0, inner_groups, taps, 0)
        gw_ref[...] = jnp.zeros(gw_ref.shape, F32)
        fold_taps(acc, gw_ref, 0, chan, 0)

    def first_slope(w_ref, c_ref, st_in, p_ref, more, *refs):
        pieces, (d1_ref, st_ref, token_ref, pad_ref, own_ref) = refs[:6], refs[6:]
        token_ref[...] = jnp.zeros(token_ref.shape, F32)
        fill_own(own_ref)
        assemble(pad_ref, 0, pieces)
        mean, rstd = moments(st_in, 0)

        def step(g, sums):
            at = lane_at(g)
            xhat = (c_ref[:, at] - mean) * rstd
            z = p_ref[0:1, :] * xhat + p_ref[1:2, :]
            s = sigmoid(z)
            d = band_conv(pad_ref, w_ref, g, po, pitch) * (s * (1.0 + z * (1.0 - s)))
            d1_ref[:, at] = d
            mine = jnp.where(own(own_ref, g), d[pitch : pitch + si], 0.0)
            return add_up(sums, mine, xhat[pitch : pitch + si])

        rows = lax.fori_loop(0, outer_groups, step, (zero(), zero()))
        send_rows(st_ref, list(rows) + [more[0:2, :]])

    def first_delta(bound, s_ref, c_ref, st_in, p_ref, sums_in, x_ref, more, d_ref, gw_ref, acc, own_ref, in_ref):
        fill_own(own_ref)
        fill_inside(bound, in_ref)
        acc[...] = jnp.zeros(acc.shape, F32)
        sum_d, sum_x = gathered(sums_in, 0, chan) / voxels, gathered(sums_in, 1, chan) / voxels
        mean, rstd = moments(st_in, 0)
        scale = p_ref[0:1, :] * rstd

        def step(g, carry):
            at = lane_at(g)
            xhat = (c_ref[:, at] - mean) * rstd
            out = scale * (s_ref[:, at] - sum_d - xhat * sum_x)
            out = jnp.where(inside(bound, in_ref, g), out, 0.0).astype(BF)
            d_ref[:, at] = out
            mine = jnp.where(own(own_ref, g), out[pitch : pitch + si].astype(F32), 0.0)
            tap_products(mine, x_ref, pitch, g, pitch, acc)
            return carry

        lax.fori_loop(0, outer_groups, step, 0)
        gw_ref[...] = jnp.zeros(gw_ref.shape, F32)
        fold_taps(acc, gw_ref, 0, chan, 2)
        gw_ref[tap_rows : 2 * tap_rows, :] = more[...]

    def mix(got_ref, after, out_ref):
        del after
        whole = jnp.sum(got_ref[...], axis=0, keepdims=True) * factor
        out_ref[...] = jnp.broadcast_to(whole.astype(BF), out_ref.shape)

    def last(got_ref, one_ref, two_ref):
        for out, first in ((one_ref, 0), (two_ref, tap_rows)):
            for at in range(27):
                row, lane = divmod(at, per)
                begin = first + row * chan
                block = got_ref[begin : begin + chan, lane * chan : (lane + 1) * chan]
                out[at // 9, at // 3 % 3, at % 3] = block.astype(F32)

    def last_conv(d_ref, w_ref, dx_ref, o_ref):
        def conv(g, carry):
            o_ref[:, lane_at(g)] = band_conv(d_ref, w_ref, g, pi, pitch).astype(BF)
            return carry

        lax.fori_loop(0, inner_groups, conv, 0)
        order = order_matrix(chan, span_y)
        for x in range(span_x):
            at = SEAM + x * pitch
            dx_ref[:, x] = native(o_ref[at : at + span_z, :], order)

    def out_a(c_ref, st_in, st_two, p_ref, y_ref, n_ref, h_ref):
        for row, (ref, at) in enumerate(((st_in, 1), (st_in, 0), (st_two, 1), (st_two, 0))):
            n_ref[row : row + 1, :] = factor * gathered(ref, at, chan)[:, :chan]
        order = order_matrix(chan, span_y)
        mean, rstd = moments(st_in, 2)

        def act(g, carry):
            at = lane_at(g)
            z = p_ref[2:3, :] * ((c_ref[:, at] - mean) * rstd) + p_ref[3:4, :]
            h_ref[:, at] = (z * sigmoid(z)).astype(BF)
            return carry

        lax.fori_loop(0, inner_groups, act, 0)
        for x in range(span_x):
            at = SEAM + x * pitch
            y_ref[:, x] = native(h_ref[at : at + span_z, :], order)


    vols, tiles_z = kernel_call(
        turn_in,
        "turn_in",
        [shape((2 * flat_rows, line), BF), shape((edges, 2 * span_x * SEAM, line), BF)],
        [bounds, x_a, x_b],
        smem=1,
    )
    pieces = halo(vols, tiles_z, 2, params)
    (cot,) = kernel_call(
        turn_cot, "turn_cot", [shape((si, line), BF)], [grad_out], work=1 << 27
    )
    c1_b, pad_b, stats = kernel_call(
        first_conv_b,
        "first_conv_b",
        [shape((so, mid), F32), shape((sw, wide), BF), stat_shape],
        [band_one] + pieces,
        scratch=[own_scratch],
        work=1 << 30,
    )
    stats_one = exchange(stats)
    c1_a, local_a = kernel_call(
        first_conv_a,
        "first_conv_a",
        [shape((so, mid), F32), shape((8, LANES), F32)],
        [band_one] + pieces,
        scratch=[pltpu.VMEM((sw, wide), BF), own_scratch],
        work=1 << 32,
    )
    hidden_b, c2_b, stats, token = kernel_call(
        second_conv_b,
        "second_conv_b",
        [shape((so, mid), BF), shape((si, line), F32), stat_shape, token_shape],
        [bounds, c1_b, band_two, stats_one, params, local_a],
        scratch=[own_scratch, in_scratch],
        smem=1,
        work=1 << 30,
    )
    stats_two = exchange(stats)
    back_two, back_one = kernel_call(
        back_bands,
        "back_bands",
        [band_shape, band_shape],
        [w_first, w_second, token],
        work=1 << 31,
    )
    stats, token = kernel_call(
        second_slope,
        "second_slope",
        [stat_shape, token_shape],
        [c2_b, stats_two, params, cot],
        scratch=[own_scratch],
        work=1 << 27,
    )
    sums_two = exchange(stats)
    c2_a, local_a = kernel_call(
        second_conv_a,
        "second_conv_a",
        [shape((si, line), F32), shape((8, LANES), F32)],
        [bounds, c1_a, band_two, stats_two, params, token],
        scratch=[pltpu.VMEM((so, mid), BF), own_scratch, in_scratch],
        smem=1,
        work=1 << 32,
    )
    delta_two, block, tiles_z = kernel_call(
        second_delta,
        "second_delta",
        [
            shape((si, line), BF),
            shape((flat_rows, line), BF),
            shape((edges, span_x * SEAM, line), BF),
        ],
        [bounds, c2_b, stats_two, params, cot, sums_two, local_a],
        scratch=[own_scratch],
        smem=1,
        work=1 << 27,
    )
    pieces = halo(block, tiles_z, 1, local_a)
    tap_rows = -(-27 // per) * chan
    taps_shape = shape((tap_rows, LANES), F32)
    acc_scratch = pltpu.VMEM((3, 3 * LANES, 2 * LANES), F32)
    slope, stats, token = kernel_call(
        first_slope,
        "first_slope",
        [shape((so, mid), F32), stat_shape, token_shape],
        [back_two, c1_b, stats_one, params, local_a] + pieces,
        scratch=[pltpu.VMEM((sw, wide), BF), own_scratch],
        work=1 << 30,
    )
    sums_one = exchange(stats)
    (taps_two,) = kernel_call(
        second_taps,
        "second_taps",
        [taps_shape],
        [delta_two, hidden_b, token],
        scratch=[acc_scratch],
        work=1 << 32,
    )
    share = -(-2 * tap_rows // (world * 8)) * 8
    delta_one, taps = kernel_call(
        first_delta,
        "first_delta",
        [shape((so, mid), BF), shape((share * world, LANES), F32)],
        [bounds, slope, c1_b, stats_one, params, sums_one, pad_b, taps_two],
        scratch=[acc_scratch, own_scratch, in_scratch],
        smem=1,
        work=1 << 30,
    )
    (dx_b,) = kernel_call(
        last_conv,
        "last_conv",
        [shape(x_a.shape, BF)],
        [delta_one, back_one],
        scratch=[pltpu.VMEM((si, line), BF)],
        work=1 << 32,
    )
    y_a, grad_norm = kernel_call(
        out_a,
        "out_a",
        [shape(x_a.shape, BF), shape((4, chan), F32)],
        [c2_a, sums_one, sums_two, params],
        scratch=[pltpu.VMEM((si, line), BF)],
        work=1 << 32,
    )

    part = exchange(taps.reshape(world, share, LANES))
    (whole,) = kernel_call(mix, "mix", [shape(part.shape, BF)], [part, grad_norm])
    whole = exchange(whole).reshape(world * share, LANES)
    weight_shape = shape((3, 3, 3, chan, chan), F32)
    grad_one, grad_two = kernel_call(last, "last", [weight_shape, weight_shape], [whole])
    return (y_a, dx_b, grad_one, grad_two, grad_norm)


def solution(mesh):
    block = P(None, "gx", "gy", "gz")
    placed = (block, block, P(), P(), P(), P(), P(), P(), block)
    return jax.shard_map(
        body,
        mesh=mesh,
        in_specs=placed,
        out_specs=(block, block, P(), P(), P()),
        check_vma=False,
    )
```

time: 592 us -> 164 us (0.28)
  blocking collectives: 170 us -> 0 us
  local copies, waits for them, and re-layouts: 139 us -> 22.3 us
  waiting for transfers between devices: 131 us -> 40.9 us
  Pallas kernels: 0 us -> 42.2 us
  other arithmetic: 40.1 us -> 0 us
  matrix products: 36.3 us -> 0 us
  between operations: 17.5 us -> 1.09 us
    psum x4 -> x0, blocking collectives: 170 us -> none  [the longest x2 88.7 us: statistics(): sums, squares = lax.psum((local_sums, local_squares), ('gx', 'gy', 'gz'))]
    psum x1 -> x0, waiting for transfers between devices: 105 us -> none  [body(): grad_w_first = lax.psum(local_first, ('gx', 'gy', 'gz'))]
    pallas_call x0 -> x21, Pallas kernels: none -> 42.2 us  [kernel_call(): pl.pallas_call(body, out_shape=out_shape, in_specs=[SM] * smem + [VM] * (...]
    concatenate x58 -> x0, local copies, waits for them, and re-layouts: 42 us -> none  [the longest x4 22.8 us: extended(): block = jnp.concatenate([low, block, high], axis=dim)]
    dot_general x72 -> x0, matrix products: 36.3 us -> none  [the longest x54 24.8 us: convolve(): total = total + jnp.dot(matrix, stacked, preferred_element_type=jnp.float32)]
    concatenate x56 -> x0, other arithmetic: 30.3 us -> none  [the longest x12 21.6 us: extended(): block = jnp.concatenate([low, block, high], axis=dim)]
    all_to_all x0 -> x6, waiting for transfers between devices: none -> 28.5 us  [exchange(): return lax.all_to_all(spread_rows, AXES, 0, 0)]
    all_to_all x0 -> x6, starting transfers between devices: none -> 27.7 us  [exchange(): return lax.all_to_all(spread_rows, AXES, 0, 0)]
  transfers between devices with their start and end apart: 25 -> 20, of which waited for: 10 -> 11; matrix products, arithmetic and copies ran while one was open for 12% -> 0% of each run, Pallas kernels for 0% -> 11%
where the time goes in v2:
time: 164 us; the launch traced here: 163 us
  starting transfers between devices  56.1 us (34%)
  Pallas kernels  42.2 us (26%)
  waiting for transfers between devices  40.9 us (25%)
  local copies, waits for them, and re-layouts  22.3 us (14%)
    pallas_call x21, Pallas kernels, kernel_call(): pl.pallas_call(body, out_shape=out_shape, in_specs=[SM] * smem + [VM] * (...  42.2 us
    all_to_all x6, waiting for transfers between devices, exchange(): return lax.all_to_all(spread_rows, AXES, 0, 0)  28.5 us
    all_to_all x6, starting transfers between devices, exchange(): return lax.all_to_all(spread_rows, AXES, 0, 0)  27.7 us
    unnamed x70, local copies, waits for them, and re-layouts  22.2 us
    ppermute x2, starting transfers between devices, halo(): lax.ppermute(block, 'gx', forward_x)  10.2 us
    ppermute x2, starting transfers between devices, halo(): lax.ppermute(mine, 'gx', forward_x)  9.12 us
    ppermute x2, waiting for transfers between devices, halo(): got_z = [lax.ppermute(tiles_z[0], 'gz', [(0, 1), (1, 0)])]  5.8 us
    ppermute x2, waiting for transfers between devices, halo(): lax.ppermute(mine, 'gx', forward_x)  3.34 us
  transfers between devices with their start and end apart: 20, of which 11 were waited for; matrix products, arithmetic and copies ran while one was open for 0% of the time, Pallas kernels for 11%

profile of v2, /device:TPU:0, one launch (start us, length us, event | category | flops | bytes accessed | tf_op | source)
XLA Modules:
  0.0 162.5 jit_solution(11838523597896049522)
XLA Ops:
  0.8 1.0 copy-done.4
  2.7 1.0 turn_in.1
  3.7 1.3 collective-permute-start.1
  5.0 5.6 %collective-permute-start = (bf16[512,512]{1,0:T(8,128)(2,1)S(1)}, bf16[512,512]{1,0:T(8,128)(2,1)S(1)}, u32[]{:S(2)}, u32[]{:S(2)}) collective-permute-start(bf16[512,512]{1,0:T(8,128)(2,1)S(1)} %get-tuple-element.44.t_ref.refs_1_), channel_id=1, source_target_pairs={{0,8},{8,16},{16,24},{1,9},{9,17},{17,25},{2,10},{10,18},{18,26},{... | collective-permute-start | bytes 1572872 | tf_op jit(solution)/shard_map/ppermute | solution.py:349
  10.6 2.0 %collective-permute-start.2 = (bf16[64,512]{1,0:T(8,128)(2,1)S(1)}, bf16[64,512]{1,0:T(8,128)(2,1)S(1)}, u32[]{:S(2)}, u32[]{:S(2)}) collective-permute-start(bf16[64,512]{1,0:T(8,128)(2,1)S(1)} %bitcast.17), channel_id=1, source_target_pairs={{0,1},{1,0},{2,3},{3,2},{4,5},{5,4},{6,7},{7,6},{8,9},{9,8},{10,11... | collective-permute-start | bytes 196616 | tf_op jit(solution)/shard_map/ppermute | solution.py:260
  12.7 2.3 %collective-permute-done.2.refs_0_ = bf16[64,512]{1,0:T(8,128)(2,1)S(1)} collective-permute-done((bf16[64,512]{1,0:T(8,128)(2,1)S(1)}, bf16[64,512]{1,0:T(8,128)(2,1)S(1)}, u32[]{:S(2)}, u32[]{:S(2)}) %collective-permute-start.2) | collective-permute-done | bytes 65568 | tf_op jit(solution)/shard_map/ppermute | solution.py:260
  22.4 1.3 collective-permute-start.6
  23.7 4.6 %collective-permute-start.5 = (bf16[992,128]{1,0:T(8,128)(2,1)S(1)}, bf16[992,128]{1,0:T(8,128)(2,1)S(1)}, u32[]{:S(2)}, u32[]{:S(2)}) collective-permute-start(bf16[992,128]{1,0:T(8,128)(2,1)S(1)} %strips.2.refs_4_), channel_id=1, source_target_pairs={{0,8},{8,16},{16,24},{1,9},{9,17},{17,25},{2,10},{10,18},{18,26},{... | collective-permute-start | bytes 761864 | tf_op jit(solution)/shard_map/ppermute | solution.py:352
  28.2 2.7 %collective-permute-done.6.refs_5_ = bf16[992,128]{1,0:T(8,128)(2,1)S(1)} collective-permute-done((bf16[992,128]{1,0:T(8,128)(2,1)S(1)}, bf16[992,128]{1,0:T(8,128)(2,1)S(1)}, u32[]{:S(2)}, u32[]{:S(2)}) %collective-permute-start.6) | collective-permute-done | bytes 253984 | tf_op jit(solution)/shard_map/ppermute | solution.py:354
  31.0 1.7 %collective-permute-done.5.refs_3_ = bf16[992,128]{1,0:T(8,128)(2,1)S(1)} collective-permute-done((bf16[992,128]{1,0:T(8,128)(2,1)S(1)}, bf16[992,128]{1,0:T(8,128)(2,1)S(1)}, u32[]{:S(2)}, u32[]{:S(2)}) %collective-permute-start.5) | collective-permute-done | bytes 253984 | tf_op jit(solution)/shard_map/ppermute | solution.py:352
  32.7 4.0 %first_conv_b.1 = (f32[592,640]{1,0:T(8,128)S(1)}, bf16[880,768]{1,0:T(8,128)(2,1)S(1)}, f32[32,4,128]{2,1,0:T(4,128)}) custom-call(bf16[768,384]{1,0:T(8,128)(2,1)S(1)} %get-tuple-element.43.w_ref, bf16[512,512]{1,0:T(8,128)(2,1)S(1)} %collective-permute-done.refs_0_, bf16[512,512]{1,0:T(8,128)(2,1)S(1)} %get-tuple-element.44.t_ref.refs_1_, ...), custom_call_target="tpu_custom_call" | custom-call | flops 1073741824 | bytes 1048576 | tf_op jit(solution)/shard_map/first_conv_b/pallas_call | solution.py:21
  36.8 1.1 copy-done.2
  37.9 8.5 %all-to-all-start = ((f32[32,4,128]{2,1,0:T(4,128)}), f32[32,4,128]{2,1,0:T(4,128)S(1)}, u32[]{:S(2)}, u32[]{:S(2)}) async-start(f32[32,4,128]{2,1,0:T(4,128)} %get-tuple-element.53), calls=%async_computation | async-start | bytes 131072 | tf_op jit(solution)/shard_map/all_to_all | solution.py:38
  46.4 1.0 copy-done.11
  48.3 1.1 copy-done.23
  49.4 3.4 %first_conv_a.1 = (f32[592,640]{1,0:T(8,128)S(1)}, f32[8,128]{1,0:T(8,128)S(1)}) custom-call(bf16[768,384]{1,0:T(8,128)(2,1)S(1)} %copy-done.23, bf16[512,512]{1,0:T(8,128)(2,1)S(1)} %copy-done.11, bf16[512,512]{1,0:T(8,128)(2,1)S(1)} %get-tuple-element.44.t_ref.refs_1_, bf16[512,512]{1,0:T(8,128)(2,1)S(1)} %collective-permute-done.1.refs_2_, ...), custom_call_target="tpu_custom_call" | custom-call | flops 4294967296 | bytes 1048576 | tf_op jit(solution)/shard_map/first_conv_a/pallas_call | solution.py:21
  52.8 1.2 copy-done.31
  54.0 1.1 copy-done.27
  55.0 4.2 %second_conv_b.1 = (bf16[592,640]{1,0:T(8,128)(2,1)S(1)}, f32[304,512]{1,0:T(8,128)S(1)}, f32[32,4,128]{2,1,0:T(4,128)}, f32[8,128]{1,0:T(8,128)S(1)}) custom-call(s32[8]{0:T(128)S(1)} %stack.35.bound, f32[592,640]{1,0:T(8,128)S(1)} %get-tuple-element.52.c_ref, bf16[768,384]{1,0:T(8,128)(2,1)S(1)} %copy-done.27, f32[32,4,128]{2,1,0:T(4,128)S(1)} %all-to-all-done.st_in, ...), custom_call_target="tpu_custom_call" | custom-call | flops 1073741824 | bytes 1048576 | tf_op jit(solution)/shard_map/second_conv_b/pallas_call | solution.py:21
  60.2 5.8 %all-to-all-start.1 = ((f32[32,4,128]{2,1,0:T(4,128)}), f32[32,4,128]{2,1,0:T(4,128)S(1)}, u32[]{:S(2)}, u32[]{:S(2)}) async-start(f32[32,4,128]{2,1,0:T(4,128)} %get-tuple-element.55), calls=%async_computation.1 | async-start | bytes 131072 | tf_op jit(solution)/shard_map/all_to_all | solution.py:38
  66.4 7.2 %all-to-all-done.1.st_in = f32[32,4,128]{2,1,0:T(4,128)S(1)} async-done(((f32[32,4,128]{2,1,0:T(4,128)}), f32[32,4,128]{2,1,0:T(4,128)S(1)}, u32[]{:S(2)}, u32[]{:S(2)}) %all-to-all-start.1) | async-done | bytes 65568 | tf_op jit(solution)/shard_map/all_to_all | solution.py:38
  73.6 1.3 second_slope.1
  74.9 2.6 %all-to-all-start.2 = ((f32[32,4,128]{2,1,0:T(4,128)}), f32[32,4,128]{2,1,0:T(4,128)S(1)}, u32[]{:S(2)}, u32[]{:S(2)}) async-start(f32[32,4,128]{2,1,0:T(4,128)} %get-tuple-element.62), calls=%async_computation.2 | async-start | bytes 131072 | tf_op jit(solution)/shard_map/all_to_all | solution.py:38
  77.5 1.4 copy-done.32
  78.9 3.6 %second_conv_a.1 = (f32[304,512]{1,0:T(8,128)S(1)}, f32[8,128]{1,0:T(8,128)S(1)}) custom-call(s32[8]{0:T(128)S(1)} %stack.35.bound, f32[592,640]{1,0:T(8,128)S(1)} %copy-done.32, bf16[768,384]{1,0:T(8,128)(2,1)S(1)} %copy-done.28, f32[32,4,128]{2,1,0:T(4,128)S(1)} %all-to-all-done.1.st_in, f32[8,128]{1,0:T(8,128)S(1)} %get-tuple-element.49.token_ref.p_ref, ...), custom_call_target="tpu_custom_call" | custom-call | flops 4294967296 | bytes 1048576 | tf_op jit(solution)/shard_map/second_conv_a/pallas_call | solution.py:21
  83.4 1.8 %all-to-all-done.2.sums_in.st_two = f32[32,4,128]{2,1,0:T(4,128)S(1)} async-done(((f32[32,4,128]{2,1,0:T(4,128)}), f32[32,4,128]{2,1,0:T(4,128)S(1)}, u32[]{:S(2)}, u32[]{:S(2)}) %all-to-all-start.2) | async-done | bytes 65568 | tf_op jit(solution)/shard_map/all_to_all | solution.py:38
  85.1 1.3 second_delta.1
  86.9 3.5 %collective-permute-done.9.refs_0_ = bf16[32,512]{1,0:T(8,128)(2,1)S(1)} collective-permute-done((bf16[32,512]{1,0:T(8,128)(2,1)S(1)}, bf16[32,512]{1,0:T(8,128)(2,1)S(1)}, u32[]{:S(2)}, u32[]{:S(2)}) %collective-permute-start.9) | collective-permute-done | bytes 32800 | tf_op jit(solution)/shard_map/ppermute | solution.py:260
  91.7 1.3 collective-permute-start.8
  93.0 4.6 %collective-permute-start.7 = (bf16[256,512]{1,0:T(8,128)(2,1)S(1)}, bf16[256,512]{1,0:T(8,128)(2,1)S(1)}, u32[]{:S(2)}, u32[]{:S(2)}) collective-permute-start(bf16[256,512]{1,0:T(8,128)(2,1)S(1)} %get-tuple-element.63.t_ref.refs_1_), channel_id=1, source_target_pairs={{0,8},{8,16},{16,24},{1,9},{9,17},{17,25},{2,10},{10,18},{18,26},{... | collective-permute-start | bytes 786440 | tf_op jit(solution)/shard_map/ppermute | solution.py:349
  98.2 1.3 collective-permute-start.13
  99.5 4.6 %collective-permute-start.12 = (bf16[496,128]{1,0:T(8,128)(2,1)S(1)}, bf16[496,128]{1,0:T(8,128)(2,1)S(1)}, u32[]{:S(2)}, u32[]{:S(2)}) collective-permute-start(bf16[496,128]{1,0:T(8,128)(2,1)S(1)} %strips.3.refs_4_), channel_id=1, source_target_pairs={{0,8},{8,16},{16,24},{1,9},{9,17},{17,25},{2,10},{10,18},{18,26},{... | collective-permute-start | bytes 380936 | tf_op jit(solution)/shard_map/ppermute | solution.py:352
  106.1 1.6 collective-permute-done.12.refs_3_
  107.7 4.3 %first_slope.1 = (f32[592,640]{1,0:T(8,128)S(1)}, f32[32,4,128]{2,1,0:T(4,128)}, f32[8,128]{1,0:T(8,128)S(1)}) custom-call(bf16[768,384]{1,0:T(8,128)(2,1)S(1)} %get-tuple-element.60.w_ref, f32[592,640]{1,0:T(8,128)S(1)} %get-tuple-element.52.c_ref, f32[32,4,128]{2,1,0:T(4,128)S(1)} %all-to-all-done.st_in, f32[8,128]{1,0:T(8,128)S(1)} %get-tuple-element.49.token_ref.p_ref, ...), custom_call_target="tpu_custom_call" | custom-call | flops 1073741824 | bytes 1048576 | tf_op jit(solution)/shard_map/first_slope/pallas_call | solution.py:21
  112.0 1.2 copy-done
  113.2 5.6 %all-to-all-start.3 = ((f32[32,4,128]{2,1,0:T(4,128)}), f32[32,4,128]{2,1,0:T(4,128)S(1)}, u32[]{:S(2)}, u32[]{:S(2)}) async-start(f32[32,4,128]{2,1,0:T(4,128)} %get-tuple-element.68), calls=%async_computation.3 | async-start | bytes 131072 | tf_op jit(solution)/shard_map/all_to_all | solution.py:38
  118.8 2.8 %second_taps.1.more = f32[224,128]{1,0:T(8,128)S(1)} custom-call(bf16[304,512]{1,0:T(8,128)(2,1)S(1)} %get-tuple-element.72.d_ref, bf16[592,640]{1,0:T(8,128)(2,1)S(1)} %copy-done.25, f32[8,128]{1,0:T(8,128)S(1)} %get-tuple-element.74.after), custom_call_target="tpu_custom_call" | custom-call | flops 4294967296 | bytes 1048576 | tf_op jit(solution)/shard_map/second_taps/pallas_call | solution.py:21
  121.7 4.7 %all-to-all-done.3.st_in.sums_in = f32[32,4,128]{2,1,0:T(4,128)S(1)} async-done(((f32[32,4,128]{2,1,0:T(4,128)}), f32[32,4,128]{2,1,0:T(4,128)S(1)}, u32[]{:S(2)}, u32[]{:S(2)}) %all-to-all-start.3) | async-done | bytes 65568 | tf_op jit(solution)/shard_map/all_to_all | solution.py:38
  126.4 1.4 copy-done.1
  127.8 1.3 copy-done.3
  129.2 5.6 %first_delta.1 = (bf16[592,640]{1,0:T(8,128)(2,1)S(1)}, f32[512,128]{1,0:T(8,128)}) custom-call(s32[8]{0:T(128)S(1)} %stack.35.bound, f32[592,640]{1,0:T(8,128)S(1)} %copy-done.1, f32[592,640]{1,0:T(8,128)S(1)} %get-tuple-element.52.c_ref, f32[32,4,128]{2,1,0:T(4,128)S(1)} %all-to-all-done.st_in, f32[8,128]{1,0:T(8,128)S(1)} %get-tuple-element.49.token_ref.p_ref, ...), custom_call_target="tpu_custom_call" | custom-call | flops 1073741824 | bytes 1048576 | tf_op jit(solution)/shard_map/first_delta/pallas_call | solution.py:21
  135.7 2.6 %all-to-all-start.4 = ((f32[32,16,128]{2,1,0:T(8,128)}), f32[32,16,128]{2,1,0:T(8,128)S(1)}, u32[]{:S(2)}, u32[]{:S(2)}) async-start(f32[32,16,128]{2,1,0:T(8,128)} %bitcast.14), calls=%async_computation.4 | async-start | bytes 524288 | tf_op jit(solution)/shard_map/all_to_all | solution.py:38
  138.3 1.7 %out_a.1 = (bf16[32,2,16,128]{3,2,1,0:T(8,128)(2,1)}, f32[4,32]{1,0:T(4,128)}) custom-call(f32[304,512]{1,0:T(8,128)S(1)} %copy-done.34, f32[32,4,128]{2,1,0:T(4,128)S(1)} %all-to-all-done.3.st_in.sums_in, f32[32,4,128]{2,1,0:T(4,128)S(1)} %all-to-all-done.2.sums_in.st_two, f32[8,128]{1,0:T(8,128)S(1)} %get-tuple-element.49.token_ref.p_ref), custom_call_target="tpu_custom_call" | custom-call | flops 4294967296 | bytes 1048576 | tf_op jit(solution)/shard_map/out_a/pallas_call | solution.py:21
  140.0 9.0 %all-to-all-done.4.got_ref = f32[32,16,128]{2,1,0:T(8,128)S(1)} async-done(((f32[32,16,128]{2,1,0:T(8,128)}), f32[32,16,128]{2,1,0:T(8,128)S(1)}, u32[]{:S(2)}, u32[]{:S(2)}) %all-to-all-start.4) | async-done | bytes 262176 | tf_op jit(solution)/shard_map/all_to_all | solution.py:38
  150.3 2.6 %all-to-all-start.5 = ((bf16[32,16,128]{2,1,0:T(8,128)(2,1)}), bf16[32,16,128]{2,1,0:T(8,128)(2,1)S(1)}, u32[]{:S(2)}, u32[]{:S(2)}) async-start(bf16[32,16,128]{2,1,0:T(8,128)(2,1)} %mix.1), calls=%async_computation.5 | async-start | bytes 262144 | tf_op jit(solution)/shard_map/all_to_all | solution.py:38
  152.9 2.8 %last_conv.1 = bf16[32,2,16,128]{3,2,1,0:T(8,128)(2,1)} custom-call(bf16[592,640]{1,0:T(8,128)(2,1)S(1)} %copy-done.9, bf16[768,384]{1,0:T(8,128)(2,1)S(1)} %copy-done.30), custom_call_target="tpu_custom_call" | custom-call | flops 4294967296 | bytes 1048576 | tf_op jit(solution)/shard_map/last_conv/pallas_call | solution.py:21
  155.7 5.8 %all-to-all-done.5 = bf16[32,16,128]{2,1,0:T(8,128)(2,1)S(1)} async-done(((bf16[32,16,128]{2,1,0:T(8,128)(2,1)}), bf16[32,16,128]{2,1,0:T(8,128)(2,1)S(1)}, u32[]{:S(2)}, u32[]{:S(2)}) %all-to-all-start.5) | async-done | bytes 131104 | tf_op jit(solution)/shard_map/all_to_all | solution.py:38
  161.5 1.0 last.1
  (84 shorter events, 18.2 us)
Async XLA Ops:
  0.7 1.0 copy-start.4
  1.7 0.9 copy-start.5
  3.7 29.0 %collective-permute-start.1 = (bf16[512,512]{1,0:T(8,128)(2,1)S(1)}, bf16[512,512]{1,0:T(8,128)(2,1)S(1)}, u32[]{:S(2)}, u32[]{:S(2)}) collective-permute-start(bf16[512,512]{1,0:T(8,128)(2,1)S(1)} %get-tuple-element.44.t_ref.refs_1_), channel_id=1, source_target_pairs={{8,0},{16,8},{24,16},{9,1},{17,9},{25,17},{10,2},{18,10},{26,18},{... | collective-permute-start | bytes 1572872 | tf_op jit(solution)/shard_map/ppermute | solution.py:351
  5.0 27.7 %collective-permute-start = (bf16[512,512]{1,0:T(8,128)(2,1)S(1)}, bf16[512,512]{1,0:T(8,128)(2,1)S(1)}, u32[]{:S(2)}, u32[]{:S(2)}) collective-permute-start(bf16[512,512]{1,0:T(8,128)(2,1)S(1)} %get-tuple-element.44.t_ref.refs_1_), channel_id=1, source_target_pairs={{0,8},{8,16},{16,24},{1,9},{9,17},{17,25},{2,10},{10,18},{18,26},{... | collective-permute-start | bytes 1572872 | tf_op jit(solution)/shard_map/ppermute | solution.py:349
  10.6 4.3 %collective-permute-start.2 = (bf16[64,512]{1,0:T(8,128)(2,1)S(1)}, bf16[64,512]{1,0:T(8,128)(2,1)S(1)}, u32[]{:S(2)}, u32[]{:S(2)}) collective-permute-start(bf16[64,512]{1,0:T(8,128)(2,1)S(1)} %bitcast.17), channel_id=1, source_target_pairs={{0,1},{1,0},{2,3},{3,2},{4,5},{5,4},{6,7},{7,6},{8,9},{9,8},{10,11... | collective-permute-start | bytes 196616 | tf_op jit(solution)/shard_map/ppermute | solution.py:260
  15.6 6.2 %collective-permute-start.3 = (bf16[608,128]{1,0:T(8,128)(2,1)S(1)}, bf16[608,128]{1,0:T(8,128)(2,1)S(1)}, u32[]{:S(2)}, u32[]{:S(2)}) collective-permute-start(bf16[608,128]{1,0:T(8,128)(2,1)S(1)} %get-tuple-element.46), channel_id=1, source_target_pairs={{0,2},{2,0},{4,6},{6,4},{1,3},{3,1},{5,7},{7,5},{8,10},{10,8},{12,... | collective-permute-start | bytes 466952 | tf_op jit(solution)/shard_map/ppermute | solution.py:323
  15.6 6.1 %collective-permute-start.4 = (bf16[608,128]{1,0:T(8,128)(2,1)S(1)}, bf16[608,128]{1,0:T(8,128)(2,1)S(1)}, u32[]{:S(2)}, u32[]{:S(2)}) collective-permute-start(bf16[608,128]{1,0:T(8,128)(2,1)S(1)} %get-tuple-element.47), channel_id=1, source_target_pairs={{2,4},{4,2},{3,5},{5,3},{10,12},{12,10},{11,13},{13,11},{18,20},{2... | collective-permute-start | bytes 466952 | tf_op jit(solution)/shard_map/ppermute | solution.py:324
  16.3 0.9 copy-start.14
  17.3 0.9 copy-start.16
  21.8 15.0 %copy-start.22 = (bf16[768,384]{1,0:T(8,128)(2,1)}, bf16[768,384]{1,0:T(8,128)(2,1)S(1)}, u32[]{:S(2)}) copy-start(bf16[768,384]{1,0:T(8,128)(2,1)S(1)} %get-tuple-element.43.w_ref) | copy-start | bytes 1769476
  21.8 15.0 %copy-start.26 = (bf16[768,384]{1,0:T(8,128)(2,1)}, bf16[768,384]{1,0:T(8,128)(2,1)S(1)}, u32[]{:S(2)}) copy-start(bf16[768,384]{1,0:T(8,128)(2,1)S(1)} %get-tuple-element.51.w_ref) | copy-start | bytes 1769476
  22.4 8.6 %collective-permute-start.6 = (bf16[992,128]{1,0:T(8,128)(2,1)S(1)}, bf16[992,128]{1,0:T(8,128)(2,1)S(1)}, u32[]{:S(2)}, u32[]{:S(2)}) collective-permute-start(bf16[992,128]{1,0:T(8,128)(2,1)S(1)} %strips.2.refs_4_), channel_id=1, source_target_pairs={{8,0},{16,8},{24,16},{9,1},{17,9},{25,17},{10,2},{18,10},{26,18},{... | collective-permute-start | bytes 761864 | tf_op jit(solution)/shard_map/ppermute | solution.py:354
  23.7 9.0 %collective-permute-start.5 = (bf16[992,128]{1,0:T(8,128)(2,1)S(1)}, bf16[992,128]{1,0:T(8,128)(2,1)S(1)}, u32[]{:S(2)}, u32[]{:S(2)}) collective-permute-start(bf16[992,128]{1,0:T(8,128)(2,1)S(1)} %strips.2.refs_4_), channel_id=1, source_target_pairs={{0,8},{8,16},{16,24},{1,9},{9,17},{17,25},{2,10},{10,18},{18,26},{... | collective-permute-start | bytes 761864 | tf_op jit(solution)/shard_map/ppermute | solution.py:352
  32.7 4.0 %copy-start.12 = (bf16[992,128]{1,0:T(8,128)(2,1)}, bf16[992,128]{1,0:T(8,128)(2,1)S(1)}, u32[]{:S(2)}) copy-start(bf16[992,128]{1,0:T(8,128)(2,1)S(1)} %collective-permute-done.5.refs_3_) | copy-start | bytes 761860
  32.7 4.0 %copy-start.10 = (bf16[512,512]{1,0:T(8,128)(2,1)}, bf16[512,512]{1,0:T(8,128)(2,1)S(1)}, u32[]{:S(2)}) copy-start(bf16[512,512]{1,0:T(8,128)(2,1)S(1)} %collective-permute-done.refs_0_) | copy-start | bytes 1572868
  36.8 1.1 copy-start.2
  37.9 16.1 %all-to-all-start = ((f32[32,4,128]{2,1,0:T(4,128)}), f32[32,4,128]{2,1,0:T(4,128)S(1)}, u32[]{:S(2)}, u32[]{:S(2)}) async-start(f32[32,4,128]{2,1,0:T(4,128)} %get-tuple-element.53), calls=%async_computation | async-start | bytes 131072 | tf_op jit(solution)/shard_map/all_to_all | solution.py:38
  46.4 1.0 copy-start.11
  47.4 0.9 copy-start.13
  48.3 1.1 copy-start.23
  52.8 1.2 copy-start.31
  54.0 1.1 copy-start.27
  55.0 11.0 %copy-start.6 = (bf16[32,2,16,128]{3,2,1,0:T(8,128)(2,1)S(1)}, bf16[32,2,16,128]{3,2,1,0:T(8,128)(2,1)}, u32[]{:S(2)}) copy-start(bf16[32,2,16,128]{3,2,1,0:T(8,128)(2,1)} %g_ref.1) | copy-start | bytes 786436
  59.3 0.9 copy-start.24
  60.2 17.4 %copy-start.28 = (bf16[768,384]{1,0:T(8,128)(2,1)S(1)}, bf16[768,384]{1,0:T(8,128)(2,1)}, u32[]{:S(2)}) copy-start(bf16[768,384]{1,0:T(8,128)(2,1)} %copy-done.26) | copy-start | bytes 1769476
  60.2 13.4 %all-to-all-start.1 = ((f32[32,4,128]{2,1,0:T(4,128)}), f32[32,4,128]{2,1,0:T(4,128)S(1)}, u32[]{:S(2)}, u32[]{:S(2)}) async-start(f32[32,4,128]{2,1,0:T(4,128)} %get-tuple-element.55), calls=%async_computation.1 | async-start | bytes 131072 | tf_op jit(solution)/shard_map/all_to_all | solution.py:38
  74.9 10.2 %all-to-all-start.2 = ((f32[32,4,128]{2,1,0:T(4,128)}), f32[32,4,128]{2,1,0:T(4,128)S(1)}, u32[]{:S(2)}, u32[]{:S(2)}) async-start(f32[32,4,128]{2,1,0:T(4,128)} %get-tuple-element.62), calls=%async_computation.2 | async-start | bytes 131072 | tf_op jit(solution)/shard_map/all_to_all | solution.py:38
  77.5 1.4 copy-start.32
  83.4 20.7 %copy-start.15 = (bf16[3,3,3,32,32]{4,3,2,1,0:T(8,128)(2,1)S(1)}, bf16[3,3,3,32,32]{4,3,2,1,0:T(8,128)(2,1)}, u32[]{:S(2)}) copy-start(bf16[3,3,3,32,32]{4,3,2,1,0:T(8,128)(2,1)} %w1_ref.3) | copy-start | bytes 165892
  85.1 18.9 %copy-start.17 = (bf16[3,3,3,32,32]{4,3,2,1,0:T(8,128)(2,1)S(1)}, bf16[3,3,3,32,32]{4,3,2,1,0:T(8,128)(2,1)}, u32[]{:S(2)}) copy-start(bf16[3,3,3,32,32]{4,3,2,1,0:T(8,128)(2,1)} %w2_ref.3) | copy-start | bytes 165892
  86.4 4.0 %collective-permute-start.9 = (bf16[32,512]{1,0:T(8,128)(2,1)S(1)}, bf16[32,512]{1,0:T(8,128)(2,1)S(1)}, u32[]{:S(2)}, u32[]{:S(2)}) collective-permute-start(bf16[32,512]{1,0:T(8,128)(2,1)S(1)} %bitcast.18), channel_id=1, source_target_pairs={{0,1},{1,0},{2,3},{3,2},{4,5},{5,4},{6,7},{7,6},{8,9},{9,8},{10,11... | collective-permute-start | bytes 98312 | tf_op jit(solution)/shard_map/ppermute | solution.py:260
  90.9 6.6 %collective-permute-start.10 = (bf16[304,128]{1,0:T(8,128)(2,1)S(1)}, bf16[304,128]{1,0:T(8,128)(2,1)S(1)}, u32[]{:S(2)}, u32[]{:S(2)}) collective-permute-start(bf16[304,128]{1,0:T(8,128)(2,1)S(1)} %get-tuple-element.65), channel_id=1, source_target_pairs={{0,2},{2,0},{4,6},{6,4},{1,3},{3,1},{5,7},{7,5},{8,10},{10,8},{12,... | collective-permute-start | bytes 233480 | tf_op jit(solution)/shard_map/ppermute | solution.py:323
  91.0 6.6 %collective-permute-start.11 = (bf16[304,128]{1,0:T(8,128)(2,1)S(1)}, bf16[304,128]{1,0:T(8,128)(2,1)S(1)}, u32[]{:S(2)}, u32[]{:S(2)}) collective-permute-start(bf16[304,128]{1,0:T(8,128)(2,1)S(1)} %get-tuple-element.66), channel_id=1, source_target_pairs={{2,4},{4,2},{3,5},{5,3},{10,12},{12,10},{11,13},{13,11},{18,20},{2... | collective-permute-start | bytes 233480 | tf_op jit(solution)/shard_map/ppermute | solution.py:324
  91.7 16.0 %collective-permute-start.8 = (bf16[256,512]{1,0:T(8,128)(2,1)S(1)}, bf16[256,512]{1,0:T(8,128)(2,1)S(1)}, u32[]{:S(2)}, u32[]{:S(2)}) collective-permute-start(bf16[256,512]{1,0:T(8,128)(2,1)S(1)} %get-tuple-element.63.t_ref.refs_1_), channel_id=1, source_target_pairs={{8,0},{16,8},{24,16},{9,1},{17,9},{25,17},{10,2},{18,10},{26,18},{... | collective-permute-start | bytes 786440 | tf_op jit(solution)/shard_map/ppermute | solution.py:351
  93.0 14.7 %collective-permute-start.7 = (bf16[256,512]{1,0:T(8,128)(2,1)S(1)}, bf16[256,512]{1,0:T(8,128)(2,1)S(1)}, u32[]{:S(2)}, u32[]{:S(2)}) collective-permute-start(bf16[256,512]{1,0:T(8,128)(2,1)S(1)} %get-tuple-element.63.t_ref.refs_1_), channel_id=1, source_target_pairs={{0,8},{8,16},{16,24},{1,9},{9,17},{17,25},{2,10},{10,18},{18,26},{... | collective-permute-start | bytes 786440 | tf_op jit(solution)/shard_map/ppermute | solution.py:349
  98.2 8.0 %collective-permute-start.13 = (bf16[496,128]{1,0:T(8,128)(2,1)S(1)}, bf16[496,128]{1,0:T(8,128)(2,1)S(1)}, u32[]{:S(2)}, u32[]{:S(2)}) collective-permute-start(bf16[496,128]{1,0:T(8,128)(2,1)S(1)} %strips.3.refs_4_), channel_id=1, source_target_pairs={{8,0},{16,8},{24,16},{9,1},{17,9},{25,17},{10,2},{18,10},{26,18},{... | collective-permute-start | bytes 380936 | tf_op jit(solution)/shard_map/ppermute | solution.py:354
  99.5 8.3 %collective-permute-start.12 = (bf16[496,128]{1,0:T(8,128)(2,1)S(1)}, bf16[496,128]{1,0:T(8,128)(2,1)S(1)}, u32[]{:S(2)}, u32[]{:S(2)}) collective-permute-start(bf16[496,128]{1,0:T(8,128)(2,1)S(1)} %strips.3.refs_4_), channel_id=1, source_target_pairs={{0,8},{8,16},{16,24},{1,9},{9,17},{17,25},{2,10},{10,18},{18,26},{... | collective-permute-start | bytes 380936 | tf_op jit(solution)/shard_map/ppermute | solution.py:352
  107.7 11.1 %copy-start.25 = (bf16[592,640]{1,0:T(8,128)(2,1)S(1)}, bf16[592,640]{1,0:T(8,128)(2,1)}, u32[]{:S(2)}) copy-start(bf16[592,640]{1,0:T(8,128)(2,1)} %copy-done.24) | copy-start | bytes 2273284
  112.0 1.2 copy-start
  113.2 13.2 %all-to-all-start.3 = ((f32[32,4,128]{2,1,0:T(4,128)}), f32[32,4,128]{2,1,0:T(4,128)S(1)}, u32[]{:S(2)}, u32[]{:S(2)}) async-start(f32[32,4,128]{2,1,0:T(4,128)} %get-tuple-element.68), calls=%async_computation.3 | async-start | bytes 131072 | tf_op jit(solution)/shard_map/all_to_all | solution.py:38
  126.4 1.4 copy-start.1
  127.8 1.3 copy-start.3
  129.2 9.1 %copy-start.34 = (f32[304,512]{1,0:T(8,128)S(1)}, f32[304,512]{1,0:T(8,128)}, u32[]{:S(2)}) copy-start(f32[304,512]{1,0:T(8,128)} %copy-done.33) | copy-start | bytes 1867780
  134.8 0.9 copy-start.8
  135.7 13.3 %all-to-all-start.4 = ((f32[32,16,128]{2,1,0:T(8,128)}), f32[32,16,128]{2,1,0:T(8,128)S(1)}, u32[]{:S(2)}, u32[]{:S(2)}) async-start(f32[32,16,128]{2,1,0:T(8,128)} %bitcast.14), calls=%async_computation.4 | async-start | bytes 524288 | tf_op jit(solution)/shard_map/all_to_all | solution.py:38
  138.3 14.6 %copy-start.9 = (bf16[592,640]{1,0:T(8,128)(2,1)S(1)}, bf16[592,640]{1,0:T(8,128)(2,1)}, u32[]{:S(2)}) copy-start(bf16[592,640]{1,0:T(8,128)(2,1)} %copy-done.8) | copy-start | bytes 2273284
  138.3 14.6 %copy-start.30 = (bf16[768,384]{1,0:T(8,128)(2,1)S(1)}, bf16[768,384]{1,0:T(8,128)(2,1)}, u32[]{:S(2)}) copy-start(bf16[768,384]{1,0:T(8,128)(2,1)} %copy-done.29) | copy-start | bytes 1769476
  150.3 11.2 %all-to-all-start.5 = ((bf16[32,16,128]{2,1,0:T(8,128)(2,1)}), bf16[32,16,128]{2,1,0:T(8,128)(2,1)S(1)}, u32[]{:S(2)}, u32[]{:S(2)}) async-start(bf16[32,16,128]{2,1,0:T(8,128)(2,1)} %mix.1), calls=%async_computation.5 | async-start | bytes 262144 | tf_op jit(solution)/shard_map/all_to_all | solution.py:38
  (7 other events, 5.0 us)

commit v3 on v2

--- a/solution.py
+++ b/solution.py
@@ -15,17 +15,25 @@
 F32 = jnp.float32
 VM = pl.BlockSpec(memory_space=pltpu.VMEM)
 SM = pl.BlockSpec(memory_space=pltpu.SMEM)
-
-
-def kernel_call(body, name, out_shape, args, scratch=(), smem=0, work=0):
+HB = pl.BlockSpec(memory_space=pltpu.HBM)
+
+
+def kernel_call(body, name, out_shape, args, scratch=(), smem=0, work=0, far=(), far_out=()):
+    args = [
+        pltpu.with_memory_space_constraint(a, pltpu.HBM) if i in far else a
+        for i, a in enumerate(args)
+    ]
+    out_shape = [
+        pltpu.HBM(o.shape, o.dtype) if i in far_out else o for i, o in enumerate(out_shape)
+    ]
     return pl.pallas_call(
         body,
         out_shape=out_shape,
-        in_specs=[SM] * smem + [VM] * (len(args) - smem),
-        out_specs=[VM] * len(out_shape),
+        in_specs=[SM if i < smem else HB if i in far else VM for i in range(len(args))],
+        out_specs=[HB if i in far_out else VM for i in range(len(out_shape))],
         scratch_shapes=list(scratch),
         cost_estimate=pl.CostEstimate(flops=work, bytes_accessed=1 << 20, transcendentals=0),
-        compiler_params=pltpu.CompilerParams(vmem_limit_bytes=8 << 20),
+        compiler_params=pltpu.CompilerParams(vmem_limit_bytes=12 << 20),
         name=name,
     )(*args)
 
@@ -106,8 +114,18 @@
     return value
 
 
-def gathered(ref, row, chan):
-    return fold_lanes(jnp.sum(ref[:, row, :], axis=0, keepdims=True), chan)
+def packed(sums, chan):
+    lane = lax.broadcasted_iota(jnp.int32, (1, LANES), 1)
+    out = jnp.zeros((1, LANES), F32)
+    for k, value in enumerate(sums):
+        out = jnp.where(lane // chan == k, fold_lanes(value, chan), out)
+    return out
+
+
+def gathered(ref, k, chan):
+    total = jnp.sum(ref[:, 0, :], axis=0, keepdims=True)
+    lane = lax.broadcasted_iota(jnp.int32, (1, LANES), 1)
+    return fold_lanes(jnp.where(lane // chan == k, total, 0.0), chan)
 
 
 def sigmoid(value):
@@ -133,6 +151,8 @@
     seams = (span_x + 1) * SEAM
     strip = si + tiles * seams
     swap = lax.axis_size("gz") == 2
+    tap_rows = -(-27 // per) * chan
+    hold = -(-tap_rows // world)
     edges = 1 if swap else 2
 
     def limits(axis, low, high):
@@ -143,7 +163,7 @@
         limits("gx", 0, span_x + 2)
         + limits("gy", 0, span_y + 2)
         + limits("gz", -1, span_z + 1)
-        + [lax.axis_index("gz"), lax.axis_index("gy") % 2]
+        + [lax.axis_index("gz"), lax.axis_index("gy") % 2, lax.axis_index(AXES)]
     ).astype(jnp.int32)
 
     def fill_inside(bound, ref):
@@ -170,40 +190,59 @@
     in_scratch = pltpu.VMEM((so, LANES), F32)
 
 
-    def fill_bands(work):
-        for out, w_ref, back, offset in work:
-            out[...] = jnp.zeros(out.shape, BF)
+    def prepare(w1_ref, w2_ref, g1_ref, b1_ref, g2_ref, b2_ref, c_ref, p_ref, w1, w2, v, sems):
+        copies = [
+            pltpu.make_async_copy(source, dest, sems.at[i])
+            for i, (source, dest) in enumerate(
+                ((w1_ref, w1), (w2_ref, w2))
+                + tuple((r, v.at[i : i + 1]) for i, r in enumerate((g1_ref, b1_ref, g2_ref, b2_ref)))
+            )
+        ]
+        for copy in copies:
+            copy.start()
+        c_ref[...] = jnp.zeros(c_ref.shape, BF)
+        p_ref[...] = jnp.zeros(p_ref.shape, F32)
+        for copy in copies:
+            copy.wait()
+        for j in range(per):
+            p_ref[0:4, j * chan : (j + 1) * chan] = v[0:4, 0:chan]
+        for kind, (w, back) in enumerate(((w1, False), (w2, False), (w2, True), (w1, True))):
             for dx in range(3):
                 for dy in range(3):
                     for dz in range(3):
                         if back:
-                            block = w_ref[2 - dx, 2 - dy, 2 - dz]
+                            block = w[2 - dx, 2 - dy, 2 - dz]
                         else:
-                            block = w_ref[dx, dy, dz].astype(F32).T.astype(BF)
-                        for j in range(per):
-                            row = (dx * 2 * per + dy + j + offset) * chan
-                            lane = dz * LANES + j * chan
-                            out[row : row + chan, lane : lane + chan] = block
-
-    def bands(w1_ref, w2_ref, g1_ref, b1_ref, g2_ref, b2_ref, one_ref, two_ref, p_ref):
-        fill_bands(((one_ref, w1_ref, False, 2), (two_ref, w2_ref, False, 0)))
-        p_ref[...] = jnp.zeros(p_ref.shape, F32)
-        for row, ref in enumerate((g1_ref, b1_ref, g2_ref, b2_ref)):
-            for j in range(per):
-                p_ref[row : row + 1, j * chan : (j + 1) * chan] = ref[...]
-
-    def back_bands(w1_ref, w2_ref, token, two_ref, one_ref):
-        del token
-        fill_bands(((two_ref, w2_ref, True, 2), (one_ref, w1_ref, True, 0)))
-
-    band_shape = shape((6 * LANES, 3 * LANES), BF)
+                            block = w[dx, dy, dz].astype(F32).T.astype(BF)
+                        row = ((kind * 3 + dx) * 3 + dy) * chan
+                        c_ref[row : row + chan, dz * chan : (dz + 1) * chan] = block
+
+    def fill_band(band, c_ref, kind, offset):
+        band[...] = jnp.zeros(band.shape, BF)
+        for dx in range(3):
+            at = (kind * 3 + dx) * 3 * chan
+            for dz in range(3):
+                block = c_ref[at : at + 3 * chan, dz * chan : (dz + 1) * chan]
+                for j in range(per):
+                    row = (dx * 2 * per + j + offset) * chan
+                    lane = dz * LANES + j * chan
+                    band[row : row + 3 * chan, lane : lane + chan] = block
+
+    band_scratch = pltpu.VMEM((6 * LANES, 3 * LANES), BF)
     token_shape = shape((8, LANES), F32)
     vectors = (gain_first, bias_first, gain_second, bias_second)
-    band_one, band_two, params = kernel_call(
-        bands,
-        "bands",
-        [band_shape, band_shape, token_shape],
+    weights, params = kernel_call(
+        prepare,
+        "prepare",
+        [shape((4 * 9 * chan, LANES), BF), token_shape],
         [w_first, w_second] + [v.reshape(1, chan) for v in vectors],
+        scratch=[
+            pltpu.VMEM(w_first.shape, BF),
+            pltpu.VMEM(w_second.shape, BF),
+            pltpu.VMEM((8, chan), F32),
+            pltpu.SemaphoreType.DMA((6,)),
+        ],
+        far=range(6),
         work=1 << 31,
     )
 
@@ -232,12 +271,20 @@
             z_ref[0, rows] = last
             z_ref[1, rows] = first
 
-    def turn_in(bound, a_ref, b_ref, t_ref, z_ref):
+    def turn_in(bound, a_ref, b_ref, t_ref, z_ref, buf, sems):
+        copies = [
+            pltpu.make_async_copy(ref.at[:, x], buf.at[v * span_x + x], sems.at[v * span_x + x])
+            for v, ref in enumerate((a_ref, b_ref))
+            for x in range(span_x)
+        ]
+        for copy in copies:
+            copy.start()
         order = order_matrix(chan, span_y)
-        for v, ref in enumerate((a_ref, b_ref)):
+        for v in range(2):
             for x in range(span_x):
                 at = v * span_x + x
-                t_ref[at * span_z : (at + 1) * span_z, :] = turned(ref[:, x], order)
+                copies[at].wait()
+                t_ref[at * span_z : (at + 1) * span_z, :] = turned(buf[at], order)
                 z_tiles(bound, t_ref, at, v, z_ref)
 
     def turn_cot(g_ref, o_ref):
@@ -269,7 +316,7 @@
             even = jnp.full((SEAM, LANES), bound[7], jnp.int32) == 0
             even_block = jnp.full((span_z, LANES), bound[7], jnp.int32) == 0
 
-            def send(rows, low, high, ok):
+            def choose(rows, low, high, ok):
                 low, high = low.astype(F32), high.astype(F32)
                 a_ref[rows, :] = jnp.where(ok, high, low).astype(BF)
                 b_ref[rows, :] = jnp.where(ok, low, high).astype(BF)
@@ -297,7 +344,7 @@
                 for x in range(span_x + 1):
                     s_ref[v * seams + x * SEAM : v * seams + (x + 1) * SEAM, :] = parts[x]
                     base = v * si + x * pitch
-                    send(
+                    choose(
                         slice(base, base + SEAM),
                         parts[x][:, :LANES],
                         parts[x][:, line - LANES :],
@@ -306,7 +353,7 @@
                     if x < span_x:
                         own_rows = slice((v * span_x + x) * span_z, (v * span_x + x + 1) * span_z)
                         rows = slice(base + SEAM, base + pitch)
-                        send(
+                        choose(
                             rows,
                             t_ref[own_rows, :LANES],
                             t_ref[own_rows, line - LANES :],
@@ -395,14 +442,14 @@
                 dest[seam : seam + SEAM, columns[0] : columns[1]] = value
 
 
-    stat_shape = shape((world, 4, LANES), F32)
-
-    def send_rows(ref, rows):
-        rows = list(rows)
-        spare = ref.shape[1] - sum(r.shape[0] for r in rows)
-        if spare:
-            rows.append(jnp.zeros((spare, LANES), F32))
-        ref[...] = jnp.broadcast_to(jnp.concatenate(rows, axis=0)[None], ref.shape)
+    def stat_shape(rows):
+        return shape((world, rows, LANES), F32)
+
+    def send(ref, sums, *parts):
+        ref[:, 0:1, :] = jnp.broadcast_to(packed(sums, chan)[None], (world, 1, LANES))
+        for i, part in enumerate(parts):
+            for d in range(world):
+                ref[d, 1 + i * hold : 1 + (i + 1) * hold, :] = part[d * hold : (d + 1) * hold, :]
 
     def moments(st_ref, row):
         mean = gathered(st_ref, row, chan) / voxels
@@ -415,13 +462,18 @@
             sums[1] + jnp.sum(value * other, axis=0, keepdims=True),
         )
 
-    def conv_one_of(v, w_ref, pieces, dest, c_ref, own_ref):
+    def conv_one_of(v, w_ref, pieces, dest, c_ref, own_ref, band, after=None, to=None):
         fill_own(own_ref)
         assemble(dest, v, pieces)
+        if after is not None:
+            after.start()
+        fill_band(band, w_ref, 0, 2)
 
         def step(g, sums):
-            out = band_conv(dest, w_ref, g, po, pitch)
+            out = band_conv(dest, band, g, po, pitch)
             c_ref[:, lane_at(g)] = out
+            if to is not None:
+                column(c_ref, to[0], to[1], g).start()
             mine = jnp.where(own(own_ref, g), out[pitch : pitch + si], 0.0)
             return add_up(sums, mine, mine)
 
@@ -431,15 +483,33 @@
         return jnp.zeros((1, LANES), F32)
 
     def first_conv_b(w_ref, *refs):
-        pieces, (c_ref, x_ref, st_ref, own_ref) = refs[:6], refs[6:]
-        send_rows(st_ref, conv_one_of(1, w_ref, pieces, x_ref, c_ref, own_ref))
-
-    def first_conv_a(w_ref, *refs):
-        pieces, (c_ref, st_ref, x_ref, own_ref) = refs[:6], refs[6:]
-        rows = list(conv_one_of(0, w_ref, pieces, x_ref, c_ref, own_ref))
-        st_ref[...] = jnp.concatenate(rows + [jnp.zeros((6, LANES), F32)], axis=0)
-
-    def conv_two_of(bound, c_ref, w_ref, st_in, row, p_ref, h_ref, c2_ref, own_ref, in_ref):
+        pieces, rest = refs[:6], refs[6:]
+        c_ref, x_out, st_ref, m_ref, x_ref, own_ref, band, sem = rest
+        copy = pltpu.make_async_copy(x_ref, x_out, sem)
+        send(st_ref, conv_one_of(1, w_ref, pieces, x_ref, c_ref, own_ref, band, copy))
+        plain_taps(x_ref, m_ref)
+        copy.wait()
+
+    def first_conv_a(w_ref, after, *refs):
+        del after
+        pieces, (c_out, st_ref, x_ref, c_ref, own_ref, band, sems) = refs[:6], refs[6:]
+        st_ref[...] = jnp.zeros(st_ref.shape, F32)
+        rows = conv_one_of(0, w_ref, pieces, x_ref, c_ref, own_ref, band, None, (c_out, sems))
+        for k in range(2):
+            st_ref[k : k + 1, :] = rows[k]
+        columns(c_ref, c_out, sems)
+
+    def column(source, dest, sems, g):
+        return pltpu.make_async_copy(source.at[:, lane_at(g)], dest.at[:, lane_at(g)], sems.at[g])
+
+    def columns(source, dest, sems):
+        def wait(g, carry):
+            column(source, dest, sems, g).wait()
+            return carry
+
+        lax.fori_loop(0, outer_groups, wait, 0)
+
+    def conv_two_of(bound, c_ref, w_ref, st_in, row, p_ref, h_ref, c2_ref, own_ref, in_ref, band, after=None):
         fill_own(own_ref)
         fill_inside(bound, in_ref)
         mean, rstd = moments(st_in, row)
@@ -452,24 +522,79 @@
             return carry
 
         lax.fori_loop(0, outer_groups, act, 0)
+        if after is not None:
+            after.start()
+        fill_band(band, w_ref, 1, 0)
 
         def step(g, sums):
-            out = band_conv(h_ref, w_ref, g, pi, pitch)
+            out = band_conv(h_ref, band, g, pi, pitch)
             c2_ref[:, lane_at(g)] = out
             mine = jnp.where(own_ref[...] > 0.5, out, 0.0)
             return add_up(sums, mine, mine)
 
         return lax.fori_loop(0, inner_groups, step, (zero(), zero()))
 
-    def second_conv_b(bound, c_ref, w_ref, st_in, p_ref, more, h_ref, c2_ref, st_ref, token_ref, own_ref, in_ref):
+    def second_conv_b(bound, c_ref, w_ref, st_in, p_ref, more, m_ref, h_out, c2_ref, st_ref, token_ref, h_ref, own_ref, in_ref, band, sem):
         token_ref[...] = jnp.zeros(token_ref.shape, F32)
-        rows = conv_two_of(bound, c_ref, w_ref, st_in, 0, p_ref, h_ref, c2_ref, own_ref, in_ref)
-        send_rows(st_ref, list(rows) + [more[0:2, :]])
-
-    def second_conv_a(bound, c_ref, w_ref, st_in, p_ref, after, c2_ref, st_ref, h_ref, own_ref, in_ref):
+        copy = pltpu.make_async_copy(h_ref, h_out, sem)
+        rows = conv_two_of(bound, c_ref, w_ref, st_in, 0, p_ref, h_ref, c2_ref, own_ref, in_ref, band, copy)
+        send(st_ref, list(rows) + [more[0:1, :], more[1:2, :]])
+        for d in range(world):
+            for k in range(2):
+                row = min(d * hold // chan + k, m_ref.shape[0] - 1)
+                st_ref[d, 1 + k : 2 + k, :] = m_ref[row : row + 1, :]
+        copy.wait()
+
+    def second_conv_a(bound, c_far, w_ref, st_in, p_ref, after, c2_ref, st_ref, c_ref, h_ref, own_ref, in_ref, band, sem):
         del after
-        rows = conv_two_of(bound, c_ref, w_ref, st_in, 2, p_ref, h_ref, c2_ref, own_ref, in_ref)
+        copy = pltpu.make_async_copy(c_far, c_ref, sem)
+        copy.start()
+        copy.wait()
+        rows = conv_two_of(bound, c_ref, w_ref, st_in, 2, p_ref, h_ref, c2_ref, own_ref, in_ref, band)
         st_ref[...] = jnp.concatenate(list(rows) + [jnp.zeros((6, LANES), F32)], axis=0)
+
+    def early_taps(c_ref, st_in, x_far, after, t_ref, x_ref, acc, own_ref, sem):
+        del after
+        copy = pltpu.make_async_copy(x_far, x_ref, sem)
+        copy.start()
+        fill_own(own_ref)
+        mean, rstd = moments(st_in, 0)
+        acc[...] = jnp.zeros(acc.shape, F32)
+        copy.wait()
+
+        def step(g, carry):
+            xhat = (c_ref[pl.ds(pitch, si), lane_at(g)] - mean) * rstd
+            tap_products(jnp.where(own(own_ref, g), xhat, 0.0), x_ref, pitch, g, pitch, acc)
+            return carry
+
+        lax.fori_loop(0, outer_groups, step, 0)
+        t_ref[...] = jnp.zeros(t_ref.shape, F32)
+        fold_taps(acc, t_ref, 0, chan, 2)
+
+    def plain_taps(x_ref, m_ref):
+        m_ref[...] = jnp.zeros(m_ref.shape, F32)
+        row = lax.broadcasted_iota(jnp.int32, (8, si), 0)
+        at = lax.broadcasted_iota(jnp.int32, (8, si), 1)
+        pick = jnp.zeros((8, si), F32)
+        for x in range(span_x):
+            for t in range(3):
+                low = SEAM + x * pitch + t - 1
+                pick = jnp.where((row == t) & (at >= low) & (at < low + span_z), 1.0, pick)
+        pick = pick.astype(BF)
+        for d in range(3):
+            cols = jnp.dot(
+                pick, x_ref[pl.ds((1 + d) * pitch, si), :], preferred_element_type=F32
+            )
+            for y in range(3):
+                begin = LANES + (y - 1) * chan
+                own_cols = cols[:, begin : begin + line]
+                total = sum(own_cols[:, k * LANES : (k + 1) * LANES] for k in range(tiles))
+                total = fold_lanes(total, chan)
+                for t in range(3):
+                    group, place = divmod((d * 3 + y) * 3 + t, per)
+                    m_ref[group : group + 1, place * chan : (place + 1) * chan] = total[
+                        t : t + 1, place * chan : (place + 1) * chan
+                    ]
 
     def slope_two(c_ref, moment, p_ref, go_ref, own_ref, at):
         mean, rstd = moment
@@ -479,7 +604,7 @@
         d = go_ref[:, at].astype(F32) * (s * (1.0 + z * (1.0 - s)))
         return jnp.where(own_ref[...] > 0.5, d, 0.0), xhat
 
-    def second_slope(c_ref, st_in, p_ref, go_ref, st_ref, token_ref, own_ref):
+    def second_slope(c_ref, st_in, p_ref, go_ref, t_ref, st_ref, token_ref, own_ref):
         token_ref[...] = jnp.zeros(token_ref.shape, F32)
         fill_own(own_ref)
         moment = moments(st_in, 0)
@@ -488,7 +613,8 @@
             d, xhat = slope_two(c_ref, moment, p_ref, go_ref, own_ref, lane_at(g))
             return add_up(sums, d, xhat)
 
-        send_rows(st_ref, lax.fori_loop(0, inner_groups, step, (zero(), zero())))
+        rows = lax.fori_loop(0, inner_groups, step, (zero(), zero()))
+        send(st_ref, rows, t_ref)
 
     def second_delta(bound, c_ref, st_in, p_ref, go_ref, sums_in, after, d_ref, t_ref, z_ref, own_ref):
         del after
@@ -510,42 +636,57 @@
             t_ref[x * span_z : (x + 1) * span_z, :] = d_ref[base : base + span_z, :]
             z_tiles(bound, t_ref, x, 0, z_ref)
 
-    def second_taps(d_ref, h_ref, after, gw_ref, acc):
-        del after
+    def second_taps(d_ref, h_far, gw_ref, h_ref, acc, sem):
+        copy = pltpu.make_async_copy(h_far, h_ref, sem)
+        copy.start()
         acc[...] = jnp.zeros(acc.shape, F32)
+        gw_ref[...] = jnp.zeros(gw_ref.shape, F32)
+        copy.wait()
 
         def taps(g, carry):
             tap_products(d_ref[:, lane_at(g)].astype(F32), h_ref, 0, g, pitch, acc)
             return carry
 
         lax.fori_loop(0, inner_groups, taps, 0)
-        gw_ref[...] = jnp.zeros(gw_ref.shape, F32)
         fold_taps(acc, gw_ref, 0, chan, 0)
 
-    def first_slope(w_ref, c_ref, st_in, p_ref, more, *refs):
-        pieces, (d1_ref, st_ref, token_ref, pad_ref, own_ref) = refs[:6], refs[6:]
-        token_ref[...] = jnp.zeros(token_ref.shape, F32)
+    def first_slope(w_ref, c_ref, st_in, p_ref, more, gw_two, x_far, *refs):
+        pieces, rest = refs[:6], refs[6:]
+        d1_out, st_ref, pad_ref, own_ref, band, x_ref, acc, gw_ref, d1_ref, sem, sems = rest
+        copy = pltpu.make_async_copy(x_far, x_ref, sem)
+        copy.start()
         fill_own(own_ref)
         assemble(pad_ref, 0, pieces)
+        fill_band(band, w_ref, 2, 2)
         mean, rstd = moments(st_in, 0)
+        acc[...] = jnp.zeros(acc.shape, F32)
+        gw_ref[...] = jnp.zeros(gw_ref.shape, F32)
+        copy.wait()
 
         def step(g, sums):
             at = lane_at(g)
             xhat = (c_ref[:, at] - mean) * rstd
             z = p_ref[0:1, :] * xhat + p_ref[1:2, :]
             s = sigmoid(z)
-            d = band_conv(pad_ref, w_ref, g, po, pitch) * (s * (1.0 + z * (1.0 - s)))
+            d = band_conv(pad_ref, band, g, po, pitch) * (s * (1.0 + z * (1.0 - s)))
             d1_ref[:, at] = d
+            column(d1_ref, d1_out, sems, g).start()
             mine = jnp.where(own(own_ref, g), d[pitch : pitch + si], 0.0)
+            tap_products(mine, x_ref, pitch, g, pitch, acc)
             return add_up(sums, mine, xhat[pitch : pitch + si])
 
         rows = lax.fori_loop(0, outer_groups, step, (zero(), zero()))
-        send_rows(st_ref, list(rows) + [more[0:2, :]])
-
-    def first_delta(bound, s_ref, c_ref, st_in, p_ref, sums_in, x_ref, more, d_ref, gw_ref, acc, own_ref, in_ref):
-        fill_own(own_ref)
+        fold_taps(acc, gw_ref, 0, chan, 2)
+        send(st_ref, list(rows) + [more[0:1, :], more[1:2, :]], gw_ref, gw_two)
+        columns(d1_ref, d1_out, sems)
+
+    def first_delta(bound, s_far, c_ref, st_in, p_ref, sums_in, w_ref, after, dx_ref, s_ref, d_ref, o_ref, in_ref, band, sem):
+        del after
+        copy = pltpu.make_async_copy(s_far, s_ref, sem)
+        copy.start()
         fill_inside(bound, in_ref)
-        acc[...] = jnp.zeros(acc.shape, F32)
+        fill_band(band, w_ref, 3, 0)
+        copy.wait()
         sum_d, sum_x = gathered(sums_in, 0, chan) / voxels, gathered(sums_in, 1, chan) / voxels
         mean, rstd = moments(st_in, 0)
         scale = p_ref[0:1, :] * rstd
@@ -554,33 +695,13 @@
             at = lane_at(g)
             xhat = (c_ref[:, at] - mean) * rstd
             out = scale * (s_ref[:, at] - sum_d - xhat * sum_x)
-            out = jnp.where(inside(bound, in_ref, g), out, 0.0).astype(BF)
-            d_ref[:, at] = out
-            mine = jnp.where(own(own_ref, g), out[pitch : pitch + si].astype(F32), 0.0)
-            tap_products(mine, x_ref, pitch, g, pitch, acc)
+            d_ref[:, at] = jnp.where(inside(bound, in_ref, g), out, 0.0).astype(BF)
             return carry
 
         lax.fori_loop(0, outer_groups, step, 0)
-        gw_ref[...] = jnp.zeros(gw_ref.shape, F32)
-        fold_taps(acc, gw_ref, 0, chan, 2)
-        gw_ref[tap_rows : 2 * tap_rows, :] = more[...]
-
-    def mix(got_ref, after, out_ref):
-        del after
-        whole = jnp.sum(got_ref[...], axis=0, keepdims=True) * factor
-        out_ref[...] = jnp.broadcast_to(whole.astype(BF), out_ref.shape)
-
-    def last(got_ref, one_ref, two_ref):
-        for out, first in ((one_ref, 0), (two_ref, tap_rows)):
-            for at in range(27):
-                row, lane = divmod(at, per)
-                begin = first + row * chan
-                block = got_ref[begin : begin + chan, lane * chan : (lane + 1) * chan]
-                out[at // 9, at // 3 % 3, at % 3] = block.astype(F32)
-
-    def last_conv(d_ref, w_ref, dx_ref, o_ref):
+
         def conv(g, carry):
-            o_ref[:, lane_at(g)] = band_conv(d_ref, w_ref, g, pi, pitch).astype(BF)
+            o_ref[:, lane_at(g)] = band_conv(d_ref, band, g, pi, pitch).astype(BF)
             return carry
 
         lax.fori_loop(0, inner_groups, conv, 0)
@@ -589,7 +710,41 @@
             at = SEAM + x * pitch
             dx_ref[:, x] = native(o_ref[at : at + span_z, :], order)
 
-    def out_a(c_ref, st_in, st_two, p_ref, y_ref, n_ref, h_ref):
+    def mix(bound, st_in, p_ref, plain_ref, early_ref, late_ref, out_ref, token_ref):
+        token_ref[...] = jnp.zeros(token_ref.shape, F32)
+        sum_d, sum_x = gathered(late_ref, 0, chan) / voxels, gathered(late_ref, 1, chan) / voxels
+        scale = p_ref[0:1, :] * moments(st_in, 0)[1]
+        row = lax.broadcasted_iota(jnp.int32, (hold, LANES), 0) + bound[8] * hold
+        lane = lax.broadcasted_iota(jnp.int32, (hold, LANES), 1)
+
+        def of_row(value):
+            return jnp.sum(jnp.where(lane == row % chan, value, 0.0), axis=1, keepdims=True)
+
+        def part(ref, i):
+            return jnp.sum(ref[:, 1 + i * hold : 1 + (i + 1) * hold, :], axis=0)
+
+        plain = jnp.sum(plain_ref[:, 1:3, :], axis=0)
+        plain = jnp.where(row // chan == bound[8] * hold // chan, plain[0:1, :], plain[1:2, :])
+        one = of_row(scale) * (
+            part(late_ref, 0) - of_row(sum_d) * plain - of_row(sum_x) * part(early_ref, 0)
+        )
+        out = jnp.concatenate([one, part(late_ref, 1)], axis=0) * factor
+        spare = out_ref.shape[1] - out.shape[0]
+        if spare:
+            out = jnp.concatenate([out, jnp.zeros((spare, LANES), F32)], axis=0)
+        out_ref[...] = jnp.broadcast_to(out.astype(BF)[None], out_ref.shape)
+
+    def last(got_ref, one_ref, two_ref, flat):
+        for i, out in enumerate((one_ref, two_ref)):
+            for d in range(world):
+                flat[d * hold : (d + 1) * hold, :] = got_ref[d, i * hold : (i + 1) * hold, :].astype(F32)
+            for at in range(27):
+                row, lane = divmod(at, per)
+                block = flat[row * chan : (row + 1) * chan, lane * chan : (lane + 1) * chan]
+                out[at // 9, at // 3 % 3, at % 3] = block
+
+    def out_a(c_ref, st_in, st_two, p_ref, after, y_ref, n_ref, h_ref):
+        del after
         for row, (ref, at) in enumerate(((st_in, 1), (st_in, 0), (st_two, 1), (st_two, 0))):
             n_ref[row : row + 1, :] = factor * gathered(ref, at, chan)[:, :chan]
         order = order_matrix(chan, span_y)
@@ -612,18 +767,29 @@
         "turn_in",
         [shape((2 * flat_rows, line), BF), shape((edges, 2 * span_x * SEAM, line), BF)],
         [bounds, x_a, x_b],
+        scratch=[
+            pltpu.VMEM((2 * span_x, chan, span_y, span_z), BF),
+            pltpu.SemaphoreType.DMA((2 * span_x,)),
+        ],
         smem=1,
+        far=(1, 2),
     )
     pieces = halo(vols, tiles_z, 2, params)
     (cot,) = kernel_call(
         turn_cot, "turn_cot", [shape((si, line), BF)], [grad_out], work=1 << 27
     )
-    c1_b, pad_b, stats = kernel_call(
+    wide_scratch = pltpu.VMEM((sw, wide), BF)
+    one_copy = pltpu.SemaphoreType.DMA
+    mid_scratch = pltpu.VMEM((so, mid), F32)
+    group_copies = pltpu.SemaphoreType.DMA((outer_groups,))
+    acc_scratch = pltpu.VMEM((3, 3 * LANES, 2 * LANES), F32)
+    c1_b, pad_b, stats, plain = kernel_call(
         first_conv_b,
         "first_conv_b",
-        [shape((so, mid), F32), shape((sw, wide), BF), stat_shape],
-        [band_one] + pieces,
-        scratch=[own_scratch],
+        [shape((so, mid), F32), shape((sw, wide), BF), stat_shape(1), token_shape],
+        [weights] + pieces,
+        scratch=[wide_scratch, own_scratch, band_scratch, one_copy],
+        far_out=(1,),
         work=1 << 30,
     )
     stats_one = exchange(stats)
@@ -631,32 +797,36 @@
         first_conv_a,
         "first_conv_a",
         [shape((so, mid), F32), shape((8, LANES), F32)],
-        [band_one] + pieces,
-        scratch=[pltpu.VMEM((sw, wide), BF), own_scratch],
+        [weights, plain] + pieces,
+        scratch=[wide_scratch, mid_scratch, own_scratch, band_scratch, group_copies],
+        far_out=(0,),
         work=1 << 32,
     )
     hidden_b, c2_b, stats, token = kernel_call(
         second_conv_b,
         "second_conv_b",
-        [shape((so, mid), BF), shape((si, line), F32), stat_shape, token_shape],
-        [bounds, c1_b, band_two, stats_one, params, local_a],
-        scratch=[own_scratch, in_scratch],
+        [shape((so, mid), BF), shape((si, line), F32), stat_shape(3), token_shape],
+        [bounds, c1_b, weights, stats_one, params, local_a, plain],
+        scratch=[pltpu.VMEM((so, mid), BF), own_scratch, in_scratch, band_scratch, one_copy],
         smem=1,
+        far_out=(0,),
         work=1 << 30,
     )
     stats_two = exchange(stats)
-    back_two, back_one = kernel_call(
-        back_bands,
-        "back_bands",
-        [band_shape, band_shape],
-        [w_first, w_second, token],
-        work=1 << 31,
+    (taps_early,) = kernel_call(
+        early_taps,
+        "early_taps",
+        [shape((world * hold, LANES), F32)],
+        [c1_b, stats_one, pad_b, token],
+        scratch=[wide_scratch, acc_scratch, own_scratch, one_copy],
+        far=(2,),
+        work=1 << 32,
     )
     stats, token = kernel_call(
         second_slope,
         "second_slope",
-        [stat_shape, token_shape],
-        [c2_b, stats_two, params, cot],
+        [stat_shape(1 + hold), token_shape],
+        [c2_b, stats_two, params, cot, taps_early],
         scratch=[own_scratch],
         work=1 << 27,
     )
@@ -665,9 +835,10 @@
         second_conv_a,
         "second_conv_a",
         [shape((si, line), F32), shape((8, LANES), F32)],
-        [bounds, c1_a, band_two, stats_two, params, token],
-        scratch=[pltpu.VMEM((so, mid), BF), own_scratch, in_scratch],
+        [bounds, c1_a, weights, stats_two, params, token],
+        scratch=[mid_scratch, pltpu.VMEM((so, mid), BF), own_scratch, in_scratch, band_scratch, one_copy],
         smem=1,
+        far=(1,),
         work=1 << 32,
     )
     delta_two, block, tiles_z = kernel_call(
@@ -683,59 +854,78 @@
         smem=1,
         work=1 << 27,
     )
-    pieces = halo(block, tiles_z, 1, local_a)
-    tap_rows = -(-27 // per) * chan
-    taps_shape = shape((tap_rows, LANES), F32)
-    acc_scratch = pltpu.VMEM((3, 3 * LANES, 2 * LANES), F32)
-    slope, stats, token = kernel_call(
-        first_slope,
-        "first_slope",
-        [shape((so, mid), F32), stat_shape, token_shape],
-        [back_two, c1_b, stats_one, params, local_a] + pieces,
-        scratch=[pltpu.VMEM((sw, wide), BF), own_scratch],
-        work=1 << 30,
-    )
-    sums_one = exchange(stats)
     (taps_two,) = kernel_call(
         second_taps,
         "second_taps",
-        [taps_shape],
-        [delta_two, hidden_b, token],
-        scratch=[acc_scratch],
+        [shape((world * hold, LANES), F32)],
+        [delta_two, hidden_b],
+        scratch=[pltpu.VMEM((so, mid), BF), acc_scratch, one_copy],
+        far=(1,),
         work=1 << 32,
     )
-    share = -(-2 * tap_rows // (world * 8)) * 8
-    delta_one, taps = kernel_call(
+    pieces = halo(block, tiles_z, 1, local_a)
+    slope, stats = kernel_call(
+        first_slope,
+        "first_slope",
+        [shape((so, mid), F32), stat_shape(1 + 2 * hold)],
+        [weights, c1_b, stats_one, params, local_a, taps_two, pad_b] + pieces,
+        scratch=[
+            wide_scratch,
+            own_scratch,
+            band_scratch,
+            wide_scratch,
+            acc_scratch,
+            pltpu.VMEM((world * hold, LANES), F32),
+            mid_scratch,
+            one_copy,
+            group_copies,
+        ],
+        far=(6,),
+        far_out=(0,),
+        work=1 << 30,
+    )
+    sums_one = exchange(stats)
+    whole, token = kernel_call(
+        mix,
+        "mix",
+        [shape((world, -(-2 * hold // 8) * 8, LANES), BF), token_shape],
+        [bounds, stats_one, params, stats_two, sums_two, sums_one],
+        smem=1,
+    )
+    whole = exchange(whole)
+    (dx_b,) = kernel_call(
         first_delta,
         "first_delta",
-        [shape((so, mid), BF), shape((share * world, LANES), F32)],
-        [bounds, slope, c1_b, stats_one, params, sums_one, pad_b, taps_two],
-        scratch=[acc_scratch, own_scratch, in_scratch],
+        [shape(x_a.shape, BF)],
+        [bounds, slope, c1_b, stats_one, params, sums_one, weights, token],
+        scratch=[
+            mid_scratch,
+            pltpu.VMEM((so, mid), BF),
+            pltpu.VMEM((si, line), BF),
+            in_scratch,
+            band_scratch,
+            one_copy,
+        ],
         smem=1,
-        work=1 << 30,
-    )
-    (dx_b,) = kernel_call(
-        last_conv,
-        "last_conv",
-        [shape(x_a.shape, BF)],
-        [delta_one, back_one],
-        scratch=[pltpu.VMEM((si, line), BF)],
-        work=1 << 32,
+        far=(1,),
+        work=1 << 31,
     )
     y_a, grad_norm = kernel_call(
         out_a,
         "out_a",
         [shape(x_a.shape, BF), shape((4, chan), F32)],
-        [c2_a, sums_one, sums_two, params],
+        [c2_a, sums_one, sums_two, params, token],
         scratch=[pltpu.VMEM((si, line), BF)],
-        work=1 << 32,
-    )
-
-    part = exchange(taps.reshape(world, share, LANES))
-    (whole,) = kernel_call(mix, "mix", [shape(part.shape, BF)], [part, grad_norm])
-    whole = exchange(whole).reshape(world * share, LANES)
+        work=1 << 31,
+    )
     weight_shape = shape((3, 3, 3, chan, chan), F32)
-    grad_one, grad_two = kernel_call(last, "last", [weight_shape, weight_shape], [whole])
+    grad_one, grad_two = kernel_call(
+        last,
+        "last",
+        [weight_shape, weight_shape],
+        [whole],
+        scratch=[pltpu.VMEM((world * hold, LANES), F32)],
+    )
     return (y_a, dx_b, grad_one, grad_two, grad_norm)
 
 

time: 164 us -> 146 us (0.89)
  waiting for transfers between devices: 40.9 us -> 21.2 us
  local copies, waits for them, and re-layouts: 22.3 us -> 3.94 us
  blocking collectives: 0 us -> 16.9 us
  Pallas kernels: 42.2 us -> 57.2 us
  starting transfers between devices: 56.1 us -> 44.7 us
    all_to_all x6 -> x4, waiting for transfers between devices: 28.5 us -> 6.39 us  [exchange(): return lax.all_to_all(spread_rows, AXES, 0, 0)]
    unnamed x70 -> x18, local copies, waits for them, and re-layouts: 22.2 us -> 3.86 us
    all_to_all x0 -> x1, blocking collectives: none -> 16.9 us  [exchange(): return lax.all_to_all(spread_rows, AXES, 0, 0)]
    pallas_call x21 -> x20, Pallas kernels: 42.2 us -> 57.2 us  [kernel_call(): pl.pallas_call(body, out_shape=out_shape, in_specs=[SM if i < smem else H...]
    all_to_all x6 -> x4, starting transfers between devices: 27.7 us -> 20.3 us  [exchange(): return lax.all_to_all(spread_rows, AXES, 0, 0)]
    ppermute x2, starting transfers between devices: 10.2 us -> 6.5 us  [halo(): lax.ppermute(block, 'gx', forward_x)]
    ppermute x2, waiting for transfers between devices: 3.23 us -> 6.35 us  [halo(): lax.ppermute(mine, 'gx', backward_x)]
  transfers between devices with their start and end apart: 20 -> 18, of which waited for: 11 -> 8; matrix products, arithmetic and copies ran while one was open for 0% -> 0% of each run, Pallas kernels for 11% -> 21%
where the time goes in v3:
time: 146 us; the launch traced here: 145 us
  Pallas kernels  57.2 us (39%)
  starting transfers between devices  44.7 us (31%)
  waiting for transfers between devices  21.2 us (15%)
  blocking collectives  16.9 us (12%)
  local copies, waits for them, and re-layouts  3.94 us (3%)
    pallas_call x20, Pallas kernels, kernel_call(): pl.pallas_call(body, out_shape=out_shape, in_specs=[SM if i < smem else H...  57.2 us
    all_to_all x4, starting transfers between devices, exchange(): return lax.all_to_all(spread_rows, AXES, 0, 0)  20.3 us
    all_to_all x1, blocking collectives, exchange(): return lax.all_to_all(spread_rows, AXES, 0, 0)  16.9 us
    ppermute x2, starting transfers between devices, halo(): lax.ppermute(mine, 'gx', forward_x)  9.12 us
    ppermute x2, starting transfers between devices, halo(): lax.ppermute(block, 'gx', forward_x)  6.5 us
    all_to_all x4, waiting for transfers between devices, exchange(): return lax.all_to_all(spread_rows, AXES, 0, 0)  6.39 us
    ppermute x2, waiting for transfers between devices, halo(): lax.ppermute(mine, 'gx', backward_x)  6.35 us
    ppermute x2, waiting for transfers between devices, halo(): got_z = [lax.ppermute(tiles_z[0], 'gz', [(0, 1), (1, 0)])]  6.35 us
  transfers between devices with their start and end apart: 18, of which 8 were waited for; matrix products, arithmetic and copies ran while one was open for 0% of the time, Pallas kernels for 21%

profile of v3, /device:TPU:0, one launch (start us, length us, event | category | flops | bytes accessed | tf_op | source)
XLA Modules:
  0.0 145.0 jit_solution(4273632875900485843)
XLA Ops:
  0.8 2.5 %turn_in.1 = (bf16[512,512]{1,0:T(8,128)(2,1)S(1)}, bf16[1,64,512]{2,1,0:T(8,128)(2,1)S(1)}) custom-call(s32[9]{0:T(128)S(1)} %stack.39.bound, bf16[32,2,16,128]{3,2,1,0:T(8,128)(2,1)} %a_ref.1, bf16[32,2,16,128]{3,2,1,0:T(8,128)(2,1)} %b_ref.1), custom_call_target="tpu_custom_call" | custom-call | bytes 1048576 | tf_op jit(solution)/shard_map/turn_in/pallas_call | solution.py:29
  3.3 5.0 %collective-permute-start = (bf16[512,512]{1,0:T(8,128)(2,1)S(1)}, bf16[512,512]{1,0:T(8,128)(2,1)S(1)}, u32[]{:S(2)}, u32[]{:S(2)}) collective-permute-start(bf16[512,512]{1,0:T(8,128)(2,1)S(1)} %get-tuple-element.41.t_ref.refs_1_), channel_id=1, source_target_pairs={{0,8},{8,16},{16,24},{1,9},{9,17},{17,25},{2,10},{10,18},{18,26},{... | collective-permute-start | bytes 1572872 | tf_op jit(solution)/shard_map/ppermute | solution.py:396
  8.3 1.3 collective-permute-start.1
  9.6 1.6 %collective-permute-start.2 = (bf16[64,512]{1,0:T(8,128)(2,1)S(1)}, bf16[64,512]{1,0:T(8,128)(2,1)S(1)}, u32[]{:S(2)}, u32[]{:S(2)}) collective-permute-start(bf16[64,512]{1,0:T(8,128)(2,1)S(1)} %bitcast.15), channel_id=1, source_target_pairs={{0,1},{1,0},{2,3},{3,2},{4,5},{5,4},{6,7},{7,6},{8,9},{9,8},{10,11... | collective-permute-start | bytes 196616 | tf_op jit(solution)/shard_map/ppermute | solution.py:307
  11.2 2.7 %collective-permute-done.2.refs_0_ = bf16[64,512]{1,0:T(8,128)(2,1)S(1)} collective-permute-done((bf16[64,512]{1,0:T(8,128)(2,1)S(1)}, bf16[64,512]{1,0:T(8,128)(2,1)S(1)}, u32[]{:S(2)}, u32[]{:S(2)}) %collective-permute-start.2) | collective-permute-done | bytes 65568 | tf_op jit(solution)/shard_map/ppermute | solution.py:307
  13.9 0.6 edge.2
  14.6 0.7 collective-permute-start.4
  15.3 1.7 %prepare.1 = (bf16[1152,128]{1,0:T(8,128)(2,1)S(1)}, f32[8,128]{1,0:T(8,128)S(1)}) custom-call(bf16[3,3,3,32,32]{4,3,2,1,0:T(8,128)(2,1)} %w1_ref.1, bf16[3,3,3,32,32]{4,3,2,1,0:T(8,128)(2,1)} %w2_ref.1, f32[1,32]{1,0:T(1,128)} %bitcast.17, f32[1,32]{1,0:T(1,128)} %bitcast.18, f32[1,32]{1,0:T(1,128)} %bitcast.19, f32[1,32]{1,0:T(1,128)} %bitcast.20), custom_call_target="tpu_custom_call" | custom-call | flops 2147483648 | bytes 1048576 | tf_op jit(solution)/shard_map/prepare/pallas_call | solution.py:29
  17.0 0.6 strips.2.refs_4_
  17.6 4.6 %collective-permute-start.5 = (bf16[992,128]{1,0:T(8,128)(2,1)S(1)}, bf16[992,128]{1,0:T(8,128)(2,1)S(1)}, u32[]{:S(2)}, u32[]{:S(2)}) collective-permute-start(bf16[992,128]{1,0:T(8,128)(2,1)S(1)} %strips.2.refs_4_), channel_id=1, source_target_pairs={{0,8},{8,16},{16,24},{1,9},{9,17},{17,25},{2,10},{10,18},{18,26},{... | collective-permute-start | bytes 761864 | tf_op jit(solution)/shard_map/ppermute | solution.py:399
  22.1 1.3 collective-permute-start.6
  23.5 0.4 turn_cot.1.go_ref
  23.8 2.1 %collective-permute-done.5.refs_3_ = bf16[992,128]{1,0:T(8,128)(2,1)S(1)} collective-permute-done((bf16[992,128]{1,0:T(8,128)(2,1)S(1)}, bf16[992,128]{1,0:T(8,128)(2,1)S(1)}, u32[]{:S(2)}, u32[]{:S(2)}) %collective-permute-start.5) | collective-permute-done | bytes 253984 | tf_op jit(solution)/shard_map/ppermute | solution.py:399
  25.9 4.4 %collective-permute-done.6.refs_5_ = bf16[992,128]{1,0:T(8,128)(2,1)S(1)} collective-permute-done((bf16[992,128]{1,0:T(8,128)(2,1)S(1)}, bf16[992,128]{1,0:T(8,128)(2,1)S(1)}, u32[]{:S(2)}, u32[]{:S(2)}) %collective-permute-start.6) | collective-permute-done | bytes 253984 | tf_op jit(solution)/shard_map/ppermute | solution.py:401
  30.3 5.2 %first_conv_b.1 = (f32[592,640]{1,0:T(8,128)S(1)}, bf16[880,768]{1,0:T(8,128)(2,1)}, f32[32,1,128]{2,1,0:T(1,128)}, f32[8,128]{1,0:T(8,128)S(1)}) custom-call(bf16[1152,128]{1,0:T(8,128)(2,1)S(1)} %get-tuple-element.40.w_ref, bf16[512,512]{1,0:T(8,128)(2,1)S(1)} %collective-permute-done.refs_0_, bf16[512,512]{1,0:T(8,128)(2,1)S(1)} %get-tuple-element.41.t_ref.refs_1_, ...), custom_call_target="tpu_custom_call" | custom-call | flops 1073741824 | bytes 1048576 | tf_op jit(solution)/shard_map/first_conv_b/pallas_call | solution.py:29
  35.6 9.0 %all-to-all-start = ((f32[32,1,128]{2,1,0:T(1,128)}), f32[32,1,128]{2,1,0:T(1,128)S(1)}, u32[]{:S(2)}, u32[]{:S(2)}) async-start(f32[32,1,128]{2,1,0:T(1,128)} %get-tuple-element.50), calls=%async_computation | async-start | bytes 32768 | tf_op jit(solution)/shard_map/all_to_all | solution.py:46
  44.6 1.0 copy-done.2
  45.6 1.0 copy-done.4
  46.7 0.9 copy-done.6
  47.6 4.6 %first_conv_a.1 = (f32[592,640]{1,0:T(8,128)}, f32[8,128]{1,0:T(8,128)S(1)}) custom-call(bf16[1152,128]{1,0:T(8,128)(2,1)S(1)} %get-tuple-element.40.w_ref, f32[8,128]{1,0:T(8,128)S(1)} %get-tuple-element.47.after.m_ref, bf16[512,512]{1,0:T(8,128)(2,1)S(1)} %copy-done.2, bf16[512,512]{1,0:T(8,128)(2,1)S(1)} %get-tuple-element.41.t_ref.refs_1_, ...), custom_call_target="tpu_custom_call" | custom-call | flops 4294967296 | bytes 1048576 | tf_op jit(solution)/shard_map/first_conv_a/pallas_call | solution.py:29
  52.2 4.8 %second_conv_b.1 = (bf16[592,640]{1,0:T(8,128)(2,1)}, f32[304,512]{1,0:T(8,128)S(1)}, f32[32,3,128]{2,1,0:T(4,128)}, f32[8,128]{1,0:T(8,128)S(1)}) custom-call(s32[9]{0:T(128)S(1)} %stack.39.bound, f32[592,640]{1,0:T(8,128)S(1)} %get-tuple-element.49.c_ref, bf16[1152,128]{1,0:T(8,128)(2,1)S(1)} %get-tuple-element.40.w_ref, ...), custom_call_target="tpu_custom_call" | custom-call | flops 1073741824 | bytes 1048576 | tf_op jit(solution)/shard_map/second_conv_b/pallas_call | solution.py:29
  57.0 5.8 %all-to-all-start.1 = ((f32[32,3,128]{2,1,0:T(4,128)}), f32[32,3,128]{2,1,0:T(4,128)S(1)}, u32[]{:S(2)}, u32[]{:S(2)}) async-start(f32[32,3,128]{2,1,0:T(4,128)} %get-tuple-element.52), calls=%async_computation.1 | async-start | bytes 131072 | tf_op jit(solution)/shard_map/all_to_all | solution.py:46
  62.8 4.6 %early_taps.1.t_ref = f32[224,128]{1,0:T(8,128)S(1)} custom-call(f32[592,640]{1,0:T(8,128)S(1)} %get-tuple-element.49.c_ref, f32[32,1,128]{2,1,0:T(1,128)S(1)} %all-to-all-done.st_in, bf16[880,768]{1,0:T(8,128)(2,1)} %get-tuple-element.54.x_far, f32[8,128]{1,0:T(8,128)S(1)} %get-tuple-element.55.after), custom_call_target="tpu_custom_call" | custom-call | flops 4294967296 | bytes 1048576 | tf_op jit(solution)/shard_map/early_taps/pallas_call | solution.py:29
  67.5 3.0 %all-to-all-done.1.st_in.plain_ref = f32[32,3,128]{2,1,0:T(4,128)S(1)} async-done(((f32[32,3,128]{2,1,0:T(4,128)}), f32[32,3,128]{2,1,0:T(4,128)S(1)}, u32[]{:S(2)}, u32[]{:S(2)}) %all-to-all-start.1) | async-done | bytes 49184 | tf_op jit(solution)/shard_map/all_to_all | solution.py:46
  70.4 1.5 %second_slope.1 = (f32[32,8,128]{2,1,0:T(8,128)}, f32[8,128]{1,0:T(8,128)S(1)}) custom-call(f32[304,512]{1,0:T(8,128)S(1)} %get-tuple-element.53.c_ref, f32[32,3,128]{2,1,0:T(4,128)S(1)} %all-to-all-done.1.st_in.plain_ref, f32[8,128]{1,0:T(8,128)S(1)} %get-tuple-element.46.token_ref.p_ref, bf16[304,512]{1,0:T(8,128)(2,1)S(1)} %turn_cot.1.go_ref, ...), custom_call_target="tpu_custom_call" | custom-call | flops 134217728 | bytes 1048576 | tf_op jit(solution)/shard_map/second_slope/pallas_call | solution.py:29
  71.9 2.9 %all-to-all-start.2 = ((f32[32,8,128]{2,1,0:T(8,128)}), f32[32,8,128]{2,1,0:T(8,128)S(1)}, u32[]{:S(2)}, u32[]{:S(2)}) async-start(f32[32,8,128]{2,1,0:T(8,128)} %get-tuple-element.59), calls=%async_computation.2 | async-start | bytes 262144 | tf_op jit(solution)/shard_map/all_to_all | solution.py:46
  74.8 5.4 %second_conv_a.1 = (f32[304,512]{1,0:T(8,128)S(1)}, f32[8,128]{1,0:T(8,128)S(1)}) custom-call(s32[9]{0:T(128)S(1)} %stack.39.bound, f32[592,640]{1,0:T(8,128)} %get-tuple-element.48.c_far, bf16[1152,128]{1,0:T(8,128)(2,1)S(1)} %get-tuple-element.40.w_ref, f32[32,3,128]{2,1,0:T(4,128)S(1)} %all-to-all-done.1.st_in.plain_ref, ...), custom_call_target="tpu_custom_call" | custom-call | flops 4294967296 | bytes 1048576 | tf_op jit(solution)/shard_map/second_conv_a/pallas_call | solution.py:29
  80.2 0.8 copy-done.7
  81.0 2.4 %all-to-all-done.2.sums_in.early_ref.st_two = f32[32,8,128]{2,1,0:T(8,128)S(1)} async-done(((f32[32,8,128]{2,1,0:T(8,128)}), f32[32,8,128]{2,1,0:T(8,128)S(1)}, u32[]{:S(2)}, u32[]{:S(2)}) %all-to-all-start.2) | async-done | bytes 131104 | tf_op jit(solution)/shard_map/all_to_all | solution.py:46
  83.4 1.3 second_delta.1
  85.1 3.6 %collective-permute-done.9.refs_0_ = bf16[32,512]{1,0:T(8,128)(2,1)S(1)} collective-permute-done((bf16[32,512]{1,0:T(8,128)(2,1)S(1)}, bf16[32,512]{1,0:T(8,128)(2,1)S(1)}, u32[]{:S(2)}, u32[]{:S(2)}) %collective-permute-start.9) | collective-permute-done | bytes 32800 | tf_op jit(solution)/shard_map/ppermute | solution.py:307
  88.7 0.6 edge.3
  89.4 0.7 collective-permute-start.11
  90.0 1.5 %collective-permute-start.7 = (bf16[256,512]{1,0:T(8,128)(2,1)S(1)}, bf16[256,512]{1,0:T(8,128)(2,1)S(1)}, u32[]{:S(2)}, u32[]{:S(2)}) collective-permute-start(bf16[256,512]{1,0:T(8,128)(2,1)S(1)} %get-tuple-element.62.t_ref.refs_1_), channel_id=1, source_target_pairs={{0,8},{8,16},{16,24},{1,9},{9,17},{17,25},{2,10},{10,18},{18,26},{... | collective-permute-start | bytes 786440 | tf_op jit(solution)/shard_map/ppermute | solution.py:396
  91.5 1.3 collective-permute-start.8
  92.9 0.6 strips.3.refs_4_
  93.4 4.6 %collective-permute-start.12 = (bf16[496,128]{1,0:T(8,128)(2,1)S(1)}, bf16[496,128]{1,0:T(8,128)(2,1)S(1)}, u32[]{:S(2)}, u32[]{:S(2)}) collective-permute-start(bf16[496,128]{1,0:T(8,128)(2,1)S(1)} %strips.3.refs_4_), channel_id=1, source_target_pairs={{0,8},{8,16},{16,24},{1,9},{9,17},{17,25},{2,10},{10,18},{18,26},{... | collective-permute-start | bytes 380936 | tf_op jit(solution)/shard_map/ppermute | solution.py:399
  98.0 1.5 %collective-permute-start.13 = (bf16[496,128]{1,0:T(8,128)(2,1)S(1)}, bf16[496,128]{1,0:T(8,128)(2,1)S(1)}, u32[]{:S(2)}, u32[]{:S(2)}) collective-permute-start(bf16[496,128]{1,0:T(8,128)(2,1)S(1)} %strips.3.refs_4_), channel_id=1, source_target_pairs={{8,0},{16,8},{24,16},{9,1},{17,9},{25,17},{10,2},{18,10},{26,18},{... | collective-permute-start | bytes 380936 | tf_op jit(solution)/shard_map/ppermute | solution.py:401
  99.5 3.9 %second_taps.1.gw_two = f32[224,128]{1,0:T(8,128)S(1)} custom-call(bf16[304,512]{1,0:T(8,128)(2,1)S(1)} %get-tuple-element.60.d_ref, bf16[592,640]{1,0:T(8,128)(2,1)} %get-tuple-element.61.h_far), custom_call_target="tpu_custom_call" | custom-call | flops 4294967296 | bytes 1048576 | tf_op jit(solution)/shard_map/second_taps/pallas_call | solution.py:29
  103.4 1.9 %collective-permute-done.13.refs_5_ = bf16[496,128]{1,0:T(8,128)(2,1)S(1)} collective-permute-done((bf16[496,128]{1,0:T(8,128)(2,1)S(1)}, bf16[496,128]{1,0:T(8,128)(2,1)S(1)}, u32[]{:S(2)}, u32[]{:S(2)}) %collective-permute-start.13) | collective-permute-done | bytes 127008 | tf_op jit(solution)/shard_map/ppermute | solution.py:401
  105.4 9.0 %first_slope.1 = (f32[592,640]{1,0:T(8,128)}, f32[32,15,128]{2,1,0:T(8,128)S(1)}) custom-call(bf16[1152,128]{1,0:T(8,128)(2,1)S(1)} %get-tuple-element.40.w_ref, f32[592,640]{1,0:T(8,128)S(1)} %get-tuple-element.49.c_ref, f32[32,1,128]{2,1,0:T(1,128)S(1)} %all-to-all-done.st_in, f32[8,128]{1,0:T(8,128)S(1)} %get-tuple-element.46.token_ref.p_ref, ...), custom_call_target="tpu_custom_call" | custom-call | flops 1073741824 | bytes 1048576 | tf_op jit(solution)/shard_map/first_slope/pallas_call | solution.py:29
  114.4 16.9 %all_to_all.25.late_ref.st_in.sums_in = f32[32,15,128]{2,1,0:T(8,128)S(1)} all-to-all(f32[32,15,128]{2,1,0:T(8,128)S(1)} %get-tuple-element.67), channel_id=1, replica_groups=mesh['gx'=4,'gy'=4,'gz'=2] {'gx','gy','gz'}, dimensions={0} | all-to-all | bytes 491520 | tf_op jit(solution)/shard_map/all_to_all | solution.py:46
  131.3 1.5 %mix.1 = (bf16[32,16,128]{2,1,0:T(8,128)(2,1)}, f32[8,128]{1,0:T(8,128)S(1)}) custom-call(s32[9]{0:T(128)S(1)} %stack.39.bound, f32[32,1,128]{2,1,0:T(1,128)S(1)} %all-to-all-done.st_in, f32[8,128]{1,0:T(8,128)S(1)} %get-tuple-element.46.token_ref.p_ref, f32[32,3,128]{2,1,0:T(4,128)S(1)} %all-to-all-done.1.st_in.plain_ref, ...), custom_call_target="tpu_custom_call" | custom-call | bytes 1048576 | tf_op jit(solution)/shard_map/mix/pallas_call | solution.py:29
  132.8 2.6 %all-to-all-start.4 = ((bf16[32,16,128]{2,1,0:T(8,128)(2,1)}), bf16[32,16,128]{2,1,0:T(8,128)(2,1)S(1)}, u32[]{:S(2)}, u32[]{:S(2)}) async-start(bf16[32,16,128]{2,1,0:T(8,128)(2,1)} %get-tuple-element.71), calls=%async_computation.4 | async-start | bytes 262144 | tf_op jit(solution)/shard_map/all_to_all | solution.py:46
  135.4 5.8 %first_delta.1 = bf16[32,2,16,128]{3,2,1,0:T(8,128)(2,1)} custom-call(s32[9]{0:T(128)S(1)} %stack.39.bound, f32[592,640]{1,0:T(8,128)} %get-tuple-element.70.s_far, f32[592,640]{1,0:T(8,128)S(1)} %get-tuple-element.49.c_ref, f32[32,1,128]{2,1,0:T(1,128)S(1)} %all-to-all-done.st_in, f32[8,128]{1,0:T(8,128)S(1)} %get-tuple-element.46.token_ref.p_ref, ...), custom_call_target="tpu_custom_call" | custom-call | flops 2147483648 | bytes 1048576 | tf_op jit(solution)/shard_map/first_delta/pallas_call | solution.py:29
  141.2 1.7 %out_a.1 = (bf16[32,2,16,128]{3,2,1,0:T(8,128)(2,1)}, f32[4,32]{1,0:T(4,128)}) custom-call(f32[304,512]{1,0:T(8,128)S(1)} %copy-done.8, f32[32,15,128]{2,1,0:T(8,128)S(1)} %all_to_all.25.late_ref.st_in.sums_in, f32[32,8,128]{2,1,0:T(8,128)S(1)} %all-to-all-done.2.sums_in.early_ref.st_two, f32[8,128]{1,0:T(8,128)S(1)} %get-tuple-element.46.token_ref.p_ref, ...), custom_call_target="tpu_custom_call" | custom-call | flops 2147483648 | bytes 1048576 | tf_op jit(solution)/shard_map/out_a/pallas_call | solution.py:29
  142.9 1.0 all-to-all-done.4.got_ref
  144.0 1.1 last.1
  (28 shorter events, 0.7 us)
Async XLA Ops:
  3.3 27.0 %collective-permute-start = (bf16[512,512]{1,0:T(8,128)(2,1)S(1)}, bf16[512,512]{1,0:T(8,128)(2,1)S(1)}, u32[]{:S(2)}, u32[]{:S(2)}) collective-permute-start(bf16[512,512]{1,0:T(8,128)(2,1)S(1)} %get-tuple-element.41.t_ref.refs_1_), channel_id=1, source_target_pairs={{0,8},{8,16},{16,24},{1,9},{9,17},{17,25},{2,10},{10,18},{18,26},{... | collective-permute-start | bytes 1572872 | tf_op jit(solution)/shard_map/ppermute | solution.py:396
  8.3 22.1 %collective-permute-start.1 = (bf16[512,512]{1,0:T(8,128)(2,1)S(1)}, bf16[512,512]{1,0:T(8,128)(2,1)S(1)}, u32[]{:S(2)}, u32[]{:S(2)}) collective-permute-start(bf16[512,512]{1,0:T(8,128)(2,1)S(1)} %get-tuple-element.41.t_ref.refs_1_), channel_id=1, source_target_pairs={{8,0},{16,8},{24,16},{9,1},{17,9},{25,17},{10,2},{18,10},{26,18},{... | collective-permute-start | bytes 1572872 | tf_op jit(solution)/shard_map/ppermute | solution.py:398
  9.6 4.3 %collective-permute-start.2 = (bf16[64,512]{1,0:T(8,128)(2,1)S(1)}, bf16[64,512]{1,0:T(8,128)(2,1)S(1)}, u32[]{:S(2)}, u32[]{:S(2)}) collective-permute-start(bf16[64,512]{1,0:T(8,128)(2,1)S(1)} %bitcast.15), channel_id=1, source_target_pairs={{0,1},{1,0},{2,3},{3,2},{4,5},{5,4},{6,7},{7,6},{8,9},{9,8},{10,11... | collective-permute-start | bytes 196616 | tf_op jit(solution)/shard_map/ppermute | solution.py:307
  14.5 2.5 %collective-permute-start.3 = (bf16[608,128]{1,0:T(8,128)(2,1)S(1)}, bf16[608,128]{1,0:T(8,128)(2,1)S(1)}, u32[]{:S(2)}, u32[]{:S(2)}) collective-permute-start(bf16[608,128]{1,0:T(8,128)(2,1)S(1)} %get-tuple-element.43), channel_id=1, source_target_pairs={{0,2},{2,0},{4,6},{6,4},{1,3},{3,1},{5,7},{7,5},{8,10},{10,8},{12,... | collective-permute-start | bytes 466952 | tf_op jit(solution)/shard_map/ppermute | solution.py:370
  14.6 2.4 %collective-permute-start.4 = (bf16[608,128]{1,0:T(8,128)(2,1)S(1)}, bf16[608,128]{1,0:T(8,128)(2,1)S(1)}, u32[]{:S(2)}, u32[]{:S(2)}) collective-permute-start(bf16[608,128]{1,0:T(8,128)(2,1)S(1)} %get-tuple-element.44), channel_id=1, source_target_pairs={{2,4},{4,2},{3,5},{5,3},{10,12},{12,10},{11,13},{13,11},{18,20},{2... | collective-permute-start | bytes 466952 | tf_op jit(solution)/shard_map/ppermute | solution.py:371
  15.3 8.2 %copy-start = (bf16[32,2,16,128]{3,2,1,0:T(8,128)(2,1)S(1)}, bf16[32,2,16,128]{3,2,1,0:T(8,128)(2,1)}, u32[]{:S(2)}) copy-start(bf16[32,2,16,128]{3,2,1,0:T(8,128)(2,1)} %g_ref.1) | copy-start | bytes 786436
  17.6 8.3 %collective-permute-start.5 = (bf16[992,128]{1,0:T(8,128)(2,1)S(1)}, bf16[992,128]{1,0:T(8,128)(2,1)S(1)}, u32[]{:S(2)}, u32[]{:S(2)}) collective-permute-start(bf16[992,128]{1,0:T(8,128)(2,1)S(1)} %strips.2.refs_4_), channel_id=1, source_target_pairs={{0,8},{8,16},{16,24},{1,9},{9,17},{17,25},{2,10},{10,18},{18,26},{... | collective-permute-start | bytes 761864 | tf_op jit(solution)/shard_map/ppermute | solution.py:399
  22.1 8.2 %collective-permute-start.6 = (bf16[992,128]{1,0:T(8,128)(2,1)S(1)}, bf16[992,128]{1,0:T(8,128)(2,1)S(1)}, u32[]{:S(2)}, u32[]{:S(2)}) collective-permute-start(bf16[992,128]{1,0:T(8,128)(2,1)S(1)} %strips.2.refs_4_), channel_id=1, source_target_pairs={{8,0},{16,8},{24,16},{9,1},{17,9},{25,17},{10,2},{18,10},{26,18},{... | collective-permute-start | bytes 761864 | tf_op jit(solution)/shard_map/ppermute | solution.py:401
  30.3 5.2 %copy-start.5 = (bf16[992,128]{1,0:T(8,128)(2,1)}, bf16[992,128]{1,0:T(8,128)(2,1)S(1)}, u32[]{:S(2)}) copy-start(bf16[992,128]{1,0:T(8,128)(2,1)S(1)} %collective-permute-done.6.refs_5_) | copy-start | bytes 761860
  30.3 5.3 %copy-start.1 = (bf16[512,512]{1,0:T(8,128)(2,1)}, bf16[512,512]{1,0:T(8,128)(2,1)S(1)}, u32[]{:S(2)}) copy-start(bf16[512,512]{1,0:T(8,128)(2,1)S(1)} %collective-permute-done.refs_0_) | copy-start | bytes 1572868
  30.3 5.3 %copy-start.3 = (bf16[512,512]{1,0:T(8,128)(2,1)}, bf16[512,512]{1,0:T(8,128)(2,1)S(1)}, u32[]{:S(2)}) copy-start(bf16[512,512]{1,0:T(8,128)(2,1)S(1)} %collective-permute-done.1.refs_2_) | copy-start | bytes 1572868
  35.6 16.6 %all-to-all-start = ((f32[32,1,128]{2,1,0:T(1,128)}), f32[32,1,128]{2,1,0:T(1,128)S(1)}, u32[]{:S(2)}, u32[]{:S(2)}) async-start(f32[32,1,128]{2,1,0:T(1,128)} %get-tuple-element.50), calls=%async_computation | async-start | bytes 32768 | tf_op jit(solution)/shard_map/all_to_all | solution.py:46
  44.6 1.0 copy-start.2
  45.6 1.0 copy-start.4
  46.7 0.9 copy-start.6
  57.0 13.5 %all-to-all-start.1 = ((f32[32,3,128]{2,1,0:T(4,128)}), f32[32,3,128]{2,1,0:T(4,128)S(1)}, u32[]{:S(2)}, u32[]{:S(2)}) async-start(f32[32,3,128]{2,1,0:T(4,128)} %get-tuple-element.52), calls=%async_computation.1 | async-start | bytes 131072 | tf_op jit(solution)/shard_map/all_to_all | solution.py:46
  71.9 11.5 %all-to-all-start.2 = ((f32[32,8,128]{2,1,0:T(8,128)}), f32[32,8,128]{2,1,0:T(8,128)S(1)}, u32[]{:S(2)}, u32[]{:S(2)}) async-start(f32[32,8,128]{2,1,0:T(8,128)} %get-tuple-element.59), calls=%async_computation.2 | async-start | bytes 262144 | tf_op jit(solution)/shard_map/all_to_all | solution.py:46
  80.2 0.8 copy-start.7
  84.7 4.0 %collective-permute-start.9 = (bf16[32,512]{1,0:T(8,128)(2,1)S(1)}, bf16[32,512]{1,0:T(8,128)(2,1)S(1)}, u32[]{:S(2)}, u32[]{:S(2)}) collective-permute-start(bf16[32,512]{1,0:T(8,128)(2,1)S(1)} %bitcast.16), channel_id=1, source_target_pairs={{0,1},{1,0},{2,3},{3,2},{4,5},{5,4},{6,7},{7,6},{8,9},{9,8},{10,11... | collective-permute-start | bytes 98312 | tf_op jit(solution)/shard_map/ppermute | solution.py:307
  89.3 3.6 %collective-permute-start.10 = (bf16[304,128]{1,0:T(8,128)(2,1)S(1)}, bf16[304,128]{1,0:T(8,128)(2,1)S(1)}, u32[]{:S(2)}, u32[]{:S(2)}) collective-permute-start(bf16[304,128]{1,0:T(8,128)(2,1)S(1)} %get-tuple-element.64), channel_id=1, source_target_pairs={{0,2},{2,0},{4,6},{6,4},{1,3},{3,1},{5,7},{7,5},{8,10},{10,8},{12,... | collective-permute-start | bytes 233480 | tf_op jit(solution)/shard_map/ppermute | solution.py:370
  89.4 3.5 %collective-permute-start.11 = (bf16[304,128]{1,0:T(8,128)(2,1)S(1)}, bf16[304,128]{1,0:T(8,128)(2,1)S(1)}, u32[]{:S(2)}, u32[]{:S(2)}) collective-permute-start(bf16[304,128]{1,0:T(8,128)(2,1)S(1)} %get-tuple-element.65), channel_id=1, source_target_pairs={{2,4},{4,2},{3,5},{5,3},{10,12},{12,10},{11,13},{13,11},{18,20},{2... | collective-permute-start | bytes 233480 | tf_op jit(solution)/shard_map/ppermute | solution.py:371
  90.0 15.3 %collective-permute-start.7 = (bf16[256,512]{1,0:T(8,128)(2,1)S(1)}, bf16[256,512]{1,0:T(8,128)(2,1)S(1)}, u32[]{:S(2)}, u32[]{:S(2)}) collective-permute-start(bf16[256,512]{1,0:T(8,128)(2,1)S(1)} %get-tuple-element.62.t_ref.refs_1_), channel_id=1, source_target_pairs={{0,8},{8,16},{16,24},{1,9},{9,17},{17,25},{2,10},{10,18},{18,26},{... | collective-permute-start | bytes 786440 | tf_op jit(solution)/shard_map/ppermute | solution.py:396
  91.5 13.8 %collective-permute-start.8 = (bf16[256,512]{1,0:T(8,128)(2,1)S(1)}, bf16[256,512]{1,0:T(8,128)(2,1)S(1)}, u32[]{:S(2)}, u32[]{:S(2)}) collective-permute-start(bf16[256,512]{1,0:T(8,128)(2,1)S(1)} %get-tuple-element.62.t_ref.refs_1_), channel_id=1, source_target_pairs={{8,0},{16,8},{24,16},{9,1},{17,9},{25,17},{10,2},{18,10},{26,18},{... | collective-permute-start | bytes 786440 | tf_op jit(solution)/shard_map/ppermute | solution.py:398
  93.4 10.0 %collective-permute-start.12 = (bf16[496,128]{1,0:T(8,128)(2,1)S(1)}, bf16[496,128]{1,0:T(8,128)(2,1)S(1)}, u32[]{:S(2)}, u32[]{:S(2)}) collective-permute-start(bf16[496,128]{1,0:T(8,128)(2,1)S(1)} %strips.3.refs_4_), channel_id=1, source_target_pairs={{0,8},{8,16},{16,24},{1,9},{9,17},{17,25},{2,10},{10,18},{18,26},{... | collective-permute-start | bytes 380936 | tf_op jit(solution)/shard_map/ppermute | solution.py:399
  98.0 7.4 %collective-permute-start.13 = (bf16[496,128]{1,0:T(8,128)(2,1)S(1)}, bf16[496,128]{1,0:T(8,128)(2,1)S(1)}, u32[]{:S(2)}, u32[]{:S(2)}) collective-permute-start(bf16[496,128]{1,0:T(8,128)(2,1)S(1)} %strips.3.refs_4_), channel_id=1, source_target_pairs={{8,0},{16,8},{24,16},{9,1},{17,9},{25,17},{10,2},{18,10},{26,18},{... | collective-permute-start | bytes 380936 | tf_op jit(solution)/shard_map/ppermute | solution.py:401
  132.8 11.2 %all-to-all-start.4 = ((bf16[32,16,128]{2,1,0:T(8,128)(2,1)}), bf16[32,16,128]{2,1,0:T(8,128)(2,1)S(1)}, u32[]{:S(2)}, u32[]{:S(2)}) async-start(bf16[32,16,128]{2,1,0:T(8,128)(2,1)} %get-tuple-element.71), calls=%async_computation.4 | async-start | bytes 262144 | tf_op jit(solution)/shard_map/all_to_all | solution.py:46
  135.4 5.9 %copy-start.8 = (f32[304,512]{1,0:T(8,128)S(1)}, f32[304,512]{1,0:T(8,128)}, u32[]{:S(2)}) copy-start(f32[304,512]{1,0:T(8,128)} %copy-done.7) | copy-start | bytes 1867780

commit v4 on v3

v4 whole, which is shorter than its diff:
```python
import math

import jax
import jax.numpy as jnp
from jax import lax
from jax.experimental import pallas as pl
from jax.experimental.pallas import tpu as pltpu
from jax.sharding import PartitionSpec as P


EPSILON = 1e-05
AXES = ("gx", "gy", "gz")
LANES = 128
SEAM = 16
BF = jnp.bfloat16
F32 = jnp.float32
VM = pl.BlockSpec(memory_space=pltpu.VMEM)
SM = pl.BlockSpec(memory_space=pltpu.SMEM)
HB = pl.BlockSpec(memory_space=pltpu.HBM)


def kernel_call(body, out_shape, args, scratch=(), smem=0, work=0, far=(), far_out=(), home=()):
    args = [
        pltpu.with_memory_space_constraint(a, pltpu.HBM) if i in far else a
        for i, a in enumerate(args)
    ]
    out_shape = [
        pltpu.HBM(o.shape, o.dtype) if i in far_out or i in home else o
        for i, o in enumerate(out_shape)
    ]
    return pl.pallas_call(
        body,
        out_shape=out_shape,
        in_specs=[SM if i < smem else HB if i in far else VM for i in range(len(args))],
        out_specs=[HB if i in far_out else VM for i in range(len(out_shape))],
        scratch_shapes=list(scratch),
        cost_estimate=pl.CostEstimate(flops=work, bytes_accessed=1 << 20, transcendentals=0),
        compiler_params=pltpu.CompilerParams(vmem_limit_bytes=12 << 20),
    )(*args)


def shape(dims, kind):
    return jax.ShapeDtypeStruct(dims, kind)


def exchange(spread_rows):
    return lax.all_to_all(spread_rows, AXES, 0, 0)


def neighbours(axis):
    count = lax.axis_size(axis)
    forward = [(i, i + 1) for i in range(count - 1)]
    return forward, [(t, s) for s, t in forward]


def order_matrix(chan, rows, start, lanes):
    k = lax.broadcasted_iota(jnp.int32, (chan * rows, lanes), 0)
    n = lax.broadcasted_iota(jnp.int32, (chan * rows, lanes), 1)
    return (n == (k % rows) * chan + k // rows + start).astype(BF)


def lane_at(group):
    return pl.ds(pl.multiple_of(group * LANES, LANES), LANES)


def band_conv(src, weight, group, planes, pitch):
    size = planes * pitch + SEAM
    at = pl.multiple_of(group * LANES, LANES)
    parts = [src[pl.ds(d * pitch, size), pl.ds(at, 2 * LANES)] for d in range(3)]
    out = jnp.dot(jnp.concatenate(parts, axis=1), weight[...], preferred_element_type=F32)
    return (
        pltpu.roll(out[:, :LANES], 1, 0)
        + out[:, LANES : 2 * LANES]
        + pltpu.roll(out[:, 2 * LANES :], size - 1, 0)
    )


def tap_products(d_rows, h_ref, start, group, pitch, acc):
    size = d_rows.shape[0]
    three = jnp.concatenate(
        [pltpu.roll(d_rows, size - 1, 0), d_rows, pltpu.roll(d_rows, 1, 0)], axis=1
    )
    left = three.T.astype(BF)
    at = pl.multiple_of(group * LANES, LANES)
    for d in range(3):
        right = h_ref[pl.ds(start + d * pitch, size), pl.ds(at, 2 * LANES)]
        acc[d] = acc[d] + jnp.dot(left, right, preferred_element_type=F32)


def fold_taps(acc, out, first, chan, offset):
    per = LANES // chan
    for d in range(3):
        for t in range(3):
            rows = sum(
                acc[
                    d,
                    t * LANES + j * chan : t * LANES + (j + 1) * chan,
                    (j + offset) * chan : (j + offset + 3) * chan,
                ]
                for j in range(per)
            )
            for y in range(3):
                row, lane = divmod((d * 3 + y) * 3 + t, per)
                out[
                    first + row * chan : first + (row + 1) * chan, lane * chan : (lane + 1) * chan
                ] = rows[:, y * chan : (y + 1) * chan].astype(out.dtype)


def fold_lanes(value, chan):
    step = chan
    while step < LANES:
        value = value + pltpu.roll(value, step, 1)
        step *= 2
    return value


def packed(sums, chan):
    lane = lax.broadcasted_iota(jnp.int32, (1, LANES), 1)
    out = jnp.zeros((1, LANES), F32)
    for k, value in enumerate(sums):
        out = jnp.where(lane // chan == k, fold_lanes(value, chan), out)
    return out


def gathered(ref, k, chan):
    total = jnp.sum(ref[:, 0, :], axis=0, keepdims=True)
    lane = lax.broadcasted_iota(jnp.int32, (1, LANES), 1)
    return fold_lanes(jnp.where(lane // chan == k, total, 0.0), chan)


def sigmoid(value):
    return 0.5 + 0.5 * jnp.tanh(0.5 * value)


def body(x_a, x_b, w_first, w_second, gain_first, bias_first, gain_second, bias_second, grad_out):
    chan, span_x, span_y, span_z = x_a.shape
    world = lax.axis_size("gx") * lax.axis_size("gy") * lax.axis_size("gz")
    voxels = float(span_x * span_y * span_z * world)
    factor = 1.0 / math.sqrt(voxels)
    per = LANES // chan
    line = span_y * chan
    tiles = line // LANES
    pitch = span_z + SEAM
    inner_groups = span_y // per
    outer_groups = inner_groups + 1
    b_groups = inner_groups + 2
    wide = line + 3 * LANES
    begin = 2 * LANES
    mid = outer_groups * LANES
    mid_b = b_groups * LANES
    base_b, base_a, base_two, base_one = -5, -1, -2, -1
    po, pi = span_x + 2, span_x
    so, si, sw = po * pitch + SEAM, pi * pitch + SEAM, (span_x + 4) * pitch + SEAM
    flat_rows = span_x * span_z
    seams = (span_x + 1) * SEAM
    strip_at = (0, si + tiles * seams)
    strip_rows = strip_at[1] + 2 * si + tiles * seams
    swap = lax.axis_size("gz") == 2
    tap_rows = -(-27 // per) * chan
    hold = -(-tap_rows // world)
    edges = 1 if swap else 2

    def limits(axis, low, high, reach):
        at, count = lax.axis_index(axis), lax.axis_size(axis)
        return [
            jnp.where(at == 0, low, low - reach),
            jnp.where(at == count - 1, high, high + reach),
        ]

    bounds = jnp.stack(
        limits("gx", 1, span_x + 1, 1)
        + limits("gy", 0, span_y, 3)
        + limits("gz", 0, span_z, 3)
        + [lax.axis_index("gz"), lax.axis_index("gy") % 2, lax.axis_index(AXES)]
    ).astype(jnp.int32)


    def fill_inside(bound, ref, planes):
        row = lax.broadcasted_iota(jnp.int32, ref.shape, 0) + (pitch - SEAM + 4)
        plane = row // pitch - 1
        z = row % pitch - 4
        ok = (plane >= planes[0]) & (plane < planes[1]) & (z >= bound[4]) & (z < bound[5])
        ref[...] = ok.astype(F32)

    def inside(bound, ref, group, base):
        lane = lax.broadcasted_iota(jnp.int32, ref.shape, 1) + group * LANES
        y = lane // chan + base
        return (ref[...] > 0.5) & (y >= bound[2]) & (y < bound[3])

    def fill_own(ref):
        row = lax.broadcasted_iota(jnp.int32, (si, LANES), 0)
        ref[...] = ((row >= SEAM) & ((row - SEAM + pitch) % pitch < span_z)).astype(F32)

    def own(ref, group, base):
        lane = lax.broadcasted_iota(jnp.int32, (si, LANES), 1) + group * LANES
        y = lane // chan + base
        return (ref[...] > 0.5) & (y >= 0) & (y < span_y)

    own_scratch = pltpu.VMEM((si, LANES), F32)
    in_scratch = pltpu.VMEM((so, LANES), F32)


    def prepare(w1_ref, w2_ref, g1_ref, b1_ref, g2_ref, b2_ref, c_ref, p_ref, w1, w2, v, sems):
        copies = [
            pltpu.make_async_copy(source, dest, sems.at[i])
            for i, (source, dest) in enumerate(
                ((w1_ref, w1), (w2_ref, w2))
                + tuple((r, v.at[i : i + 1]) for i, r in enumerate((g1_ref, b1_ref, g2_ref, b2_ref)))
            )
        ]
        for copy in copies:
            copy.start()
        c_ref[...] = jnp.zeros(c_ref.shape, BF)
        p_ref[...] = jnp.zeros(p_ref.shape, F32)
        for copy in copies:
            copy.wait()
        for j in range(per):
            p_ref[0:4, j * chan : (j + 1) * chan] = v[0:4, 0:chan]
        for kind, (w, back) in enumerate(((w1, False), (w2, False), (w2, True), (w1, True))):
            for dx in range(3):
                for dy in range(3):
                    for dz in range(3):
                        if back:
                            block = w[2 - dx, 2 - dy, 2 - dz]
                        else:
                            block = w[dx, dy, dz].astype(F32).T.astype(BF)
                        row = ((kind * 3 + dx) * 3 + dy) * chan
                        c_ref[row : row + chan, dz * chan : (dz + 1) * chan] = block

    class Band:
        def __init__(self, band, part, sem, far, kind):
            self.band, self.part = band, part
            rows = 9 * chan
            self.copy = pltpu.make_async_copy(far.at[pl.ds(kind * rows, rows)], part, sem)
            self.copy.start()

        def fill(self, offset):
            self.band[...] = jnp.zeros(self.band.shape, BF)
            self.copy.wait()
            fill_band(self.band, self.part, offset)
            return self.band

    def fill_band(band, c_ref, offset):
        for dx in range(3):
            at = dx * 3 * chan
            for dz in range(3):
                block = c_ref[at : at + 3 * chan, dz * chan : (dz + 1) * chan]
                for j in range(per):
                    row = (dx * 2 * per + j + offset) * chan
                    lane = dz * LANES + j * chan
                    band[row : row + 3 * chan, lane : lane + chan] = block

    band_scratch = (
        pltpu.VMEM((6 * LANES, 3 * LANES), BF),
        pltpu.VMEM((9 * chan, LANES), BF),
        pltpu.SemaphoreType.DMA,
    )
    token_shape = shape((8, LANES), F32)
    vectors = (gain_first, bias_first, gain_second, bias_second)
    weights, params = kernel_call(
        prepare,
        [shape((4 * 9 * chan, LANES), BF), token_shape],
        [w_first, w_second] + [v.reshape(1, chan) for v in vectors],
        scratch=[
            pltpu.VMEM(w_first.shape, BF),
            pltpu.VMEM(w_second.shape, BF),
            pltpu.VMEM((8, chan), F32),
            pltpu.SemaphoreType.DMA((6,)),
        ],
        far=range(6),
        home=(0,),
        work=1 << 31,
    )


    def turned(block, order):
        return lax.dot_general(
            block.reshape(chan * span_y, span_z),
            order,
            (((0,), (0,)), ((), ())),
            preferred_element_type=F32,
        ).astype(BF)

    def native(value, order):
        return lax.dot_general(
            order, value, (((1,), (1,)), ((), ())), preferred_element_type=F32
        ).astype(BF).reshape(chan, span_y, span_z)

    def turn_in(bound, a_ref, b_ref, go_ref, t_ref, g_ref, z_ref, buf, sems):
        copies = [
            pltpu.make_async_copy(ref.at[:, x], buf.at[v * span_x + x], sems.at[v * span_x + x])
            for v, ref in enumerate((a_ref, b_ref, go_ref))
            for x in range(span_x)
        ]
        for copy in copies:
            copy.start()
        order = order_matrix(chan, span_y, 0, line)
        moved = order_matrix(chan, span_y, 2 * chan, mid)
        z_ref[...] = jnp.zeros(z_ref.shape, BF)
        for v in range(3):
            dest, lanes = (t_ref, line) if v < 2 else (g_ref, mid)
            for x in range(span_x):
                at = v * span_x + x
                row = (at % (2 * span_x)) * span_z
                copies[at].wait()
                dest[row : row + span_z, :] = turned(buf[at], order if v < 2 else moved)
                first = dest[row : row + SEAM, :]
                last = dest[row + span_z - SEAM : row + span_z, :]
                rows = slice(at * SEAM, (at + 1) * SEAM)
                if swap:
                    pick = jnp.full(first.shape, bound[6], jnp.int32) == 0
                    z_ref[0, rows, :lanes] = jnp.where(
                        pick, last.astype(F32), first.astype(F32)
                    ).astype(BF)
                else:
                    z_ref[0, rows, :lanes] = last
                    z_ref[1, rows, :lanes] = first


    def halo(block, cot_block, tiles_z, token):
        forward_x, backward_x = neighbours("gx")
        forward_z, backward_z = neighbours("gz")
        rows_y = lax.axis_size("gy")
        pairs_y = [
            [p for i in range(first, rows_y - 1, 2) for p in ((i, i + 1), (i + 1, i))]
            for first in range(2)
        ]
        if swap:
            got_z = [lax.ppermute(tiles_z[0], "gz", [(0, 1), (1, 0)])]
        else:
            got_z = [
                lax.ppermute(tiles_z[0], "gz", forward_z),
                lax.ppermute(tiles_z[1], "gz", backward_z),
            ]
        from_low = lax.ppermute(block, "gx", forward_x)
        from_high = lax.ppermute(block, "gx", backward_x)

        def edge(bound, t_ref, g_ref, *refs):
            got, (a_ref, b_ref, s_ref) = refs[:edges], refs[edges:]
            row = lax.broadcasted_iota(jnp.int32, (SEAM, mid), 0)
            even = jnp.full((SEAM, LANES), bound[7], jnp.int32) == 0
            even_block = jnp.full((span_z, LANES), bound[7], jnp.int32) == 0

            def choose(rows, low, high, ok):
                low, high = low.astype(F32), high.astype(F32)
                a_ref[rows, :] = jnp.where(ok, high, low).astype(BF)
                b_ref[rows, :] = jnp.where(ok, low, high).astype(BF)

            for v in range(3):
                source, lanes = (t_ref, line) if v < 2 else (g_ref, mid)
                for x in range(span_x + 1):
                    tile = jnp.zeros((SEAM, mid), F32)
                    if x < span_x:
                        at = (v * span_x + x) * SEAM
                        value = got[0][at : at + SEAM, :].astype(F32)
                        ok = row >= SEAM - 4
                        if swap:
                            ok = ok & (jnp.full(row.shape, bound[6], jnp.int32) == 1)
                        tile = jnp.where(ok, value, tile)
                    if x > 0:
                        at = (v * span_x + x - 1) * SEAM
                        value = got[-1][at : at + SEAM, :].astype(F32)
                        ok = row < 4
                        if swap:
                            ok = ok & (jnp.full(row.shape, bound[6], jnp.int32) == 0)
                        tile = jnp.where(ok, value, tile)
                    tile = tile.astype(BF)
                    s_ref[v * seams + x * SEAM : v * seams + (x + 1) * SEAM, :] = tile
                    base = v * si + x * pitch
                    choose(
                        slice(base, base + SEAM),
                        tile[:, :LANES],
                        tile[:, lanes - LANES : lanes],
                        even,
                    )
                    if x < span_x:
                        at = ((v * span_x + x) % (2 * span_x)) * span_z
                        own_rows = slice(at, at + span_z)
                        choose(
                            slice(base + SEAM, base + pitch),
                            source[own_rows, :LANES],
                            source[own_rows, lanes - LANES : lanes],
                            even_block,
                        )

        send_a, send_b, seam_rows = kernel_call(
            edge,
            [shape((3 * si, LANES), BF)] * 2 + [shape((3 * seams, mid), BF)],
            [bounds, block, cot_block] + got_z,
            smem=1,
        )
        got_a = lax.ppermute(send_a, "gy", pairs_y[0])
        got_b = lax.ppermute(send_b, "gy", pairs_y[1])

        def strips(bound, a_ref, b_ref, s_ref, g_ref, token_ref, o_ref, f_ref):
            del token_ref
            lane = lax.broadcasted_iota(jnp.int32, (si, LANES), 1)
            even = jnp.full(lane.shape, bound[7], jnp.int32) == 0

            def both(v):
                a = a_ref[v * si : (v + 1) * si, :].astype(F32)
                b = b_ref[v * si : (v + 1) * si, :].astype(F32)
                return jnp.where(even, b, a), jnp.where(even, a, b)

            low, high = both(0)
            o_ref[0:si, :] = jnp.where(lane < 2 * chan, high, low).astype(BF)
            low, high = both(1)
            at = strip_at[1]
            o_ref[at : at + si, :] = low.astype(BF)
            o_ref[at + si : at + 2 * si, :] = high.astype(BF)
            for v, first in enumerate((si, at + 2 * si)):
                for t in range(tiles):
                    o_ref[first + t * seams : first + (t + 1) * seams, :] = s_ref[
                        v * seams : (v + 1) * seams, t * LANES : (t + 1) * LANES
                    ]
            low, high = both(2)
            for x in range(span_x + 1):
                f_ref[x * pitch : x * pitch + SEAM, :] = s_ref[
                    2 * seams + x * SEAM : 2 * seams + (x + 1) * SEAM, :
                ]
                if x < span_x:
                    f_ref[x * pitch + SEAM : (x + 1) * pitch, :] = g_ref[
                        x * span_z : (x + 1) * span_z, :
                    ]
            f_ref[:, :LANES] = jnp.where(
                lane < 2 * chan, low, f_ref[:, :LANES].astype(F32)
            ).astype(BF)
            f_ref[:, mid - LANES :] = jnp.where(
                lane >= 2 * chan, high, f_ref[:, mid - LANES :].astype(F32)
            ).astype(BF)

        mine, cot_frame = kernel_call(
            strips,
            [shape((strip_rows, LANES), BF), shape((si, mid), BF)],
            [bounds, got_a, got_b, seam_rows, cot_block, token],
            smem=1,
        )
        return [
            from_low,
            block,
            from_high,
            lax.ppermute(mine, "gx", forward_x),
            mine,
            lax.ppermute(mine, "gx", backward_x),
        ], cot_frame

    def joiner(dest):
        waiting = {}

        def put(seam, columns, value):
            key = (seam, columns)
            if key in waiting:
                dest[seam : seam + SEAM, columns[0] : columns[1]] = waiting.pop(key) + value
            else:
                waiting[key] = value

        def finish():
            for (seam, columns), value in waiting.items():
                dest[seam : seam + SEAM, columns[0] : columns[1]] = value

        return put, finish

    def assemble(dest, v, pieces):
        blocks, strip_refs = pieces[:3], pieces[3:]
        lane = lax.broadcasted_iota(jnp.int32, (si, LANES), 1)
        put, finish = joiner(dest)
        dest[:, :LANES] = jnp.zeros((sw, LANES), BF)
        last = si - SEAM
        for b in range(3):
            base = b * span_x * pitch
            for x in range(span_x):
                at = base + SEAM + x * pitch
                rows = slice((v * span_x + x) * span_z, (v * span_x + x + 1) * span_z)
                dest[at : at + span_z, begin : begin + line] = blocks[b][rows, :]
            first = strip_at[v]
            if v == 0:
                ys = strip_refs[b][first : first + si, :].astype(F32)
                low = jnp.where(lane >= 2 * chan, ys, 0.0).astype(BF)
                high = jnp.where(lane < 2 * chan, ys, 0.0).astype(BF)
                first += si
            else:
                low = strip_refs[b][first : first + si, :]
                high = strip_refs[b][first + si : first + 2 * si, :]
                first += 2 * si
            for columns, value in (((LANES, begin), low), ((begin + line, wide), high)):
                dest[base + SEAM : base + last, columns[0] : columns[1]] = value[SEAM:last]
                put(base, columns, value[:SEAM])
                put(base + last, columns, value[last:])
            for t in range(tiles):
                at = first + t * seams
                columns = (begin + LANES * t, begin + LANES * (t + 1))
                for x in range(span_x + 1):
                    value = strip_refs[b][at + x * SEAM : at + (x + 1) * SEAM, :]
                    seam = base + x * pitch
                    if 0 < x < span_x:
                        dest[seam : seam + SEAM, columns[0] : columns[1]] = value
                    else:
                        put(seam, columns, value)
        finish()

    def assemble_delta(dest, frames):
        put, finish = joiner(dest)
        dest[:, mid:] = jnp.zeros((sw, LANES), BF)
        last = si - SEAM
        for b in range(3):
            base = b * span_x * pitch
            dest[base + SEAM : base + last, :mid] = frames[b][SEAM:last, :]
            put(base, (0, mid), frames[b][:SEAM, :])
            put(base + last, (0, mid), frames[b][last:, :])
        finish()


    def stat_shape(rows):
        return shape((world, rows, LANES), F32)

    def send(ref, sums, *parts):
        ref[:, 0:1, :] = jnp.broadcast_to(packed(sums, chan)[None], (world, 1, LANES))
        for i, part in enumerate(parts):
            for d in range(world):
                ref[d, 1 + i * hold : 1 + (i + 1) * hold, :] = part[d * hold : (d + 1) * hold, :]

    def moments(st_ref, row):
        mean = gathered(st_ref, row, chan) / voxels
        var = gathered(st_ref, row + 1, chan) / voxels - mean * mean
        return mean, lax.rsqrt(var + EPSILON)

    def add_up(sums, value, other):
        return (
            sums[0] + jnp.sum(value, axis=0, keepdims=True),
            sums[1] + jnp.sum(value * other, axis=0, keepdims=True),
        )

    def conv_one_of(first, groups, base, band, dest, c_ref, own_ref, to=None):
        fill_own(own_ref)
        band = band.fill(2)

        def step(g, sums):
            out = band_conv(dest, band, g + first, po, pitch)
            c_ref[:, lane_at(g)] = out
            if to is not None:
                column(c_ref, to[0], to[1], g).start()
            mine = jnp.where(own(own_ref, g, base), out[pitch : pitch + si], 0.0)
            return add_up(sums, mine, mine)

        return lax.fori_loop(0, groups, step, (zero(), zero()))

    def zero():
        return jnp.zeros((1, LANES), F32)

    def first_conv_b(w_ref, *refs):
        pieces, rest = refs[:6], refs[6:]
        c_ref, x_out, a_out, st_ref, m_ref, x_ref, a_ref, own_ref, *band, sems = rest
        band = Band(*band, w_ref, 0)
        copies = [
            pltpu.make_async_copy(a_ref, a_out, sems.at[0]),
            pltpu.make_async_copy(x_ref, x_out, sems.at[1]),
        ]
        assemble(a_ref, 0, pieces)
        copies[0].start()
        assemble(x_ref, 1, pieces)
        copies[1].start()
        send(st_ref, conv_one_of(0, b_groups, base_b, band, x_ref, c_ref, own_ref))
        plain_taps(x_ref, m_ref)
        for copy in copies:
            copy.wait()

    def first_conv_a(w_ref, after, x_far, c_out, st_ref, x_ref, c_ref, own_ref, band, part, wait, sem, sems):
        del after
        band = Band(band, part, wait, w_ref, 0)
        copy = pltpu.make_async_copy(x_far, x_ref, sem)
        copy.start()
        st_ref[...] = jnp.zeros(st_ref.shape, F32)
        copy.wait()
        to = (c_out, sems)
        rows = conv_one_of(1, outer_groups, base_a, band, x_ref, c_ref, own_ref, to)
        for k in range(2):
            st_ref[k : k + 1, :] = rows[k]
        columns(c_ref, c_out, sems)

    def column(source, dest, sems, g):
        return pltpu.make_async_copy(source.at[:, lane_at(g)], dest.at[:, lane_at(g)], sems.at[g])

    def columns(source, dest, sems):
        def wait(g, carry):
            column(source, dest, sems, g).wait()
            return carry

        lax.fori_loop(0, outer_groups, wait, 0)

    def conv_two_of(bound, c_ref, st_in, k, p_ref, h_ref, c2_ref, own_ref, in_ref, band, shifts, after=None):
        groups, base, out_groups, out_base, offset = shifts
        fill_own(own_ref)
        fill_inside(bound, in_ref, (bound[0], bound[1]))
        mean, rstd = moments(st_in, k)
        gain, bias = p_ref[0:1, :], p_ref[1:2, :]

        def act(g, carry):
            at = lane_at(g)
            z = gain * ((c_ref[:, at] - mean) * rstd) + bias
            h = jnp.where(inside(bound, in_ref, g, base), z * sigmoid(z), 0.0)
            h_ref[:, at] = h.astype(BF)
            return carry

        lax.fori_loop(0, groups, act, 0)
        if after is not None:
            after.start()
        band = band.fill(offset)

        def step(g, sums):
            out = band_conv(h_ref, band, g, pi, pitch)
            c2_ref[:, lane_at(g)] = out
            mine = jnp.where(own(own_ref, g, out_base), out, 0.0)
            return add_up(sums, mine, mine)

        return lax.fori_loop(0, out_groups, step, (zero(), zero()))

    def second_conv_b(bound, c_ref, w_ref, st_in, p_ref, more, m_ref, h_out, c2_ref, st_ref, token_ref, h_ref, own_ref, in_ref, band, part, wait, sem):
        band = Band(band, part, wait, w_ref, 1)
        token_ref[...] = jnp.zeros(token_ref.shape, F32)
        copy = pltpu.make_async_copy(h_ref, h_out, sem)
        shifts = (b_groups, base_b, outer_groups, base_two, 2)
        rows = conv_two_of(bound, c_ref, st_in, 0, p_ref, h_ref, c2_ref, own_ref, in_ref, band, shifts, copy)
        send(st_ref, list(rows) + [more[0:1, :], more[1:2, :]])
        for d in range(world):
            for k in range(2):
                row = min(d * hold // chan + k, m_ref.shape[0] - 1)
                st_ref[d, 1 + k : 2 + k, :] = m_ref[row : row + 1, :]
        copy.wait()

    def second_conv_a(bound, c_far, w_ref, st_in, p_ref, after, c2_ref, st_ref, c_ref, h_ref, own_ref, in_ref, band, part, wait, sem):
        del after
        band = Band(band, part, wait, w_ref, 1)
        shifts = (outer_groups, base_a, inner_groups, 0, 0)
        copy = pltpu.make_async_copy(c_far, c_ref, sem)
        copy.start()
        copy.wait()
        rows = conv_two_of(bound, c_ref, st_in, 2, p_ref, h_ref, c2_ref, own_ref, in_ref, band, shifts)
        st_ref[...] = jnp.concatenate(list(rows) + [jnp.zeros((6, LANES), F32)], axis=0)

    def early_taps(c_ref, st_in, x_far, after, t_ref, x_ref, acc, own_ref, sem):
        del after
        copy = pltpu.make_async_copy(x_far, x_ref, sem)
        copy.start()
        fill_own(own_ref)
        mean, rstd = moments(st_in, 0)
        acc[...] = jnp.zeros(acc.shape, F32)
        copy.wait()

        def step(g, carry):
            xhat = (c_ref[pl.ds(pitch, si), lane_at(g + 1)] - mean) * rstd
            mine = jnp.where(own(own_ref, g, base_one), xhat, 0.0)
            tap_products(mine, x_ref, pitch, g + 1, pitch, acc)
            return carry

        lax.fori_loop(0, outer_groups, step, 0)
        t_ref[...] = jnp.zeros(t_ref.shape, F32)
        fold_taps(acc, t_ref, 0, chan, 2)

    def plain_taps(x_ref, m_ref):
        m_ref[...] = jnp.zeros(m_ref.shape, F32)
        row = lax.broadcasted_iota(jnp.int32, (8, si), 0)
        at = lax.broadcasted_iota(jnp.int32, (8, si), 1)
        pick = jnp.zeros((8, si), F32)
        for x in range(span_x):
            for t in range(3):
                low = SEAM + x * pitch + t - 1
                pick = jnp.where((row == t) & (at >= low) & (at < low + span_z), 1.0, pick)
        pick = pick.astype(BF)
        for d in range(3):
            cols = jnp.dot(
                pick, x_ref[pl.ds((1 + d) * pitch, si), :], preferred_element_type=F32
            )
            for y in range(3):
                low = begin + (y - 1) * chan
                own_cols = cols[:, low : low + line]
                total = sum(own_cols[:, k * LANES : (k + 1) * LANES] for k in range(tiles))
                total = fold_lanes(total, chan)
                for t in range(3):
                    group, place = divmod((d * 3 + y) * 3 + t, per)
                    m_ref[group : group + 1, place * chan : (place + 1) * chan] = total[
                        t : t + 1, place * chan : (place + 1) * chan
                    ]

    def slope_two(c_ref, moment, p_ref, go_ref, at):
        mean, rstd = moment
        xhat = (c_ref[:, at] - mean) * rstd
        z = p_ref[2:3, :] * xhat + p_ref[3:4, :]
        s = sigmoid(z)
        d = go_ref[:, at].astype(F32) * (s * (1.0 + z * (1.0 - s)))
        return d, xhat

    def second_slope(c_ref, st_in, p_ref, go_ref, t_ref, st_ref, token_ref, own_ref):
        token_ref[...] = jnp.zeros(token_ref.shape, F32)
        fill_own(own_ref)
        moment = moments(st_in, 0)

        def step(g, sums):
            d, xhat = slope_two(c_ref, moment, p_ref, go_ref, lane_at(g))
            return add_up(sums, jnp.where(own(own_ref, g, base_two), d, 0.0), xhat)

        rows = lax.fori_loop(0, outer_groups, step, (zero(), zero()))
        send(st_ref, rows, t_ref)

    def second_delta(bound, c_ref, st_in, p_ref, go_ref, sums_in, after, d_ref, in_ref):
        del after
        fill_inside(bound, in_ref, (0, span_x))
        moment = moments(st_in, 0)
        scale = p_ref[2:3, :] * moment[1]
        sum_d, sum_x = gathered(sums_in, 0, chan) / voxels, gathered(sums_in, 1, chan) / voxels

        def step(g, carry):
            at = lane_at(g)
            d, xhat = slope_two(c_ref, moment, p_ref, go_ref, at)
            out = scale * (d - sum_d - xhat * sum_x)
            d_ref[:, at] = jnp.where(inside(bound, in_ref, g, base_two), out, 0.0).astype(BF)
            return carry

        lax.fori_loop(0, outer_groups, step, 0)

    def second_taps(d_ref, h_far, gw_ref, h_ref, acc, own_ref, sem):
        copy = pltpu.make_async_copy(h_far, h_ref, sem)
        copy.start()
        fill_own(own_ref)
        acc[...] = jnp.zeros(acc.shape, F32)
        gw_ref[...] = jnp.zeros(gw_ref.shape, F32)
        copy.wait()

        def taps(g, carry):
            mine = jnp.where(own(own_ref, g, base_two), d_ref[:, lane_at(g)].astype(F32), 0.0)
            tap_products(mine, h_ref, 0, g, pitch, acc)
            return carry

        lax.fori_loop(0, outer_groups, taps, 0)
        fold_taps(acc, gw_ref, 0, chan, 2)

    def first_slope(w_ref, c_ref, st_in, p_ref, more, gw_two, x_far, *refs):
        frames, rest = refs[:3], refs[3:]
        d1_out, st_ref, pad_ref, own_ref, *band, x_ref, acc, gw_ref, d1_ref, sem, sems = rest
        band = Band(*band, w_ref, 2)
        copy = pltpu.make_async_copy(x_far, x_ref, sem)
        copy.start()
        fill_own(own_ref)
        assemble_delta(pad_ref, frames)
        band = band.fill(0)
        mean, rstd = moments(st_in, 0)
        acc[...] = jnp.zeros(acc.shape, F32)
        gw_ref[...] = jnp.zeros(gw_ref.shape, F32)
        copy.wait()

        def step(g, sums):
            at = lane_at(g)
            xhat = (c_ref[:, lane_at(g + 1)] - mean) * rstd
            z = p_ref[0:1, :] * xhat + p_ref[1:2, :]
            s = sigmoid(z)
            d = band_conv(pad_ref, band, g, po, pitch) * (s * (1.0 + z * (1.0 - s)))
            d1_ref[:, at] = d
            column(d1_ref, d1_out, sems, g).start()
            mine = jnp.where(own(own_ref, g, base_one), d[pitch : pitch + si], 0.0)
            tap_products(mine, x_ref, pitch, g + 1, pitch, acc)
            return add_up(sums, mine, xhat[pitch : pitch + si])

        rows = lax.fori_loop(0, outer_groups, step, (zero(), zero()))
        fold_taps(acc, gw_ref, 0, chan, 2)
        send(st_ref, list(rows) + [more[0:1, :], more[1:2, :]], gw_ref, gw_two)
        columns(d1_ref, d1_out, sems)

    def first_delta(bound, s_far, c_ref, st_in, p_ref, sums_in, w_ref, after, dx_ref, s_ref, d_ref, o_ref, in_ref, band, part, wait, sem):
        del after
        band = Band(band, part, wait, w_ref, 3)
        copy = pltpu.make_async_copy(s_far, s_ref, sem)
        copy.start()
        fill_inside(bound, in_ref, (bound[0], bound[1]))
        band = band.fill(0)
        copy.wait()
        sum_d, sum_x = gathered(sums_in, 0, chan) / voxels, gathered(sums_in, 1, chan) / voxels
        mean, rstd = moments(st_in, 0)
        scale = p_ref[0:1, :] * rstd

        def step(g, carry):
            at = lane_at(g)
            xhat = (c_ref[:, lane_at(g + 1)] - mean) * rstd
            out = scale * (s_ref[:, at] - sum_d - xhat * sum_x)
            d_ref[:, at] = jnp.where(inside(bound, in_ref, g, base_one), out, 0.0).astype(BF)
            return carry

        lax.fori_loop(0, outer_groups, step, 0)

        def conv(g, carry):
            o_ref[:, lane_at(g)] = band_conv(d_ref, band, g, pi, pitch).astype(BF)
            return carry

        lax.fori_loop(0, inner_groups, conv, 0)
        order = order_matrix(chan, span_y, 0, line)
        for x in range(span_x):
            at = SEAM + x * pitch
            dx_ref[:, x] = native(o_ref[at : at + span_z, :], order)

    def mix(bound, st_in, p_ref, plain_ref, early_ref, late_ref, out_ref, token_ref):
        token_ref[...] = jnp.zeros(token_ref.shape, F32)
        sum_d, sum_x = gathered(late_ref, 0, chan) / voxels, gathered(late_ref, 1, chan) / voxels
        scale = p_ref[0:1, :] * moments(st_in, 0)[1]
        row = lax.broadcasted_iota(jnp.int32, (hold, LANES), 0) + bound[8] * hold
        lane = lax.broadcasted_iota(jnp.int32, (hold, LANES), 1)

        def of_row(value):
            return jnp.sum(jnp.where(lane == row % chan, value, 0.0), axis=1, keepdims=True)

        def part(ref, i):
            return jnp.sum(ref[:, 1 + i * hold : 1 + (i + 1) * hold, :], axis=0)

        plain = jnp.sum(plain_ref[:, 1:3, :], axis=0)
        plain = jnp.where(row // chan == bound[8] * hold // chan, plain[0:1, :], plain[1:2, :])
        one = of_row(scale) * (
            part(late_ref, 0) - of_row(sum_d) * plain - of_row(sum_x) * part(early_ref, 0)
        )
        out = jnp.concatenate([one, part(late_ref, 1)], axis=0) * factor
        spare = out_ref.shape[1] - out.shape[0]
        if spare:
            out = jnp.concatenate([out, jnp.zeros((spare, LANES), F32)], axis=0)
        out_ref[...] = jnp.broadcast_to(out.astype(BF)[None], out_ref.shape)

    def last(got_ref, one_ref, two_ref, flat):
        for i, out in enumerate((one_ref, two_ref)):
            for d in range(world):
                flat[d * hold : (d + 1) * hold, :] = got_ref[d, i * hold : (i + 1) * hold, :].astype(F32)
            for at in range(27):
                row, lane = divmod(at, per)
                block = flat[row * chan : (row + 1) * chan, lane * chan : (lane + 1) * chan]
                out[at // 9, at // 3 % 3, at % 3] = block

    def out_a(c_ref, st_in, st_two, p_ref, after, y_ref, n_ref, h_ref):
        del after
        for row, (ref, at) in enumerate(((st_in, 1), (st_in, 0), (st_two, 1), (st_two, 0))):
            n_ref[row : row + 1, :] = factor * gathered(ref, at, chan)[:, :chan]
        order = order_matrix(chan, span_y, 0, line)
        mean, rstd = moments(st_in, 2)

        def act(g, carry):
            at = lane_at(g)
            z = p_ref[2:3, :] * ((c_ref[:, at] - mean) * rstd) + p_ref[3:4, :]
            h_ref[:, at] = (z * sigmoid(z)).astype(BF)
            return carry

        lax.fori_loop(0, inner_groups, act, 0)
        for x in range(span_x):
            at = SEAM + x * pitch
            y_ref[:, x] = native(h_ref[at : at + span_z, :], order)


    vols, cot_block, tiles_z = kernel_call(
        turn_in,
        [
            shape((2 * flat_rows, line), BF),
            shape((flat_rows, mid), BF),
            shape((edges, 3 * span_x * SEAM, mid), BF),
        ],
        [bounds, x_a, x_b, grad_out],
        scratch=[
            pltpu.VMEM((3 * span_x, chan, span_y, span_z), BF),
            pltpu.SemaphoreType.DMA((3 * span_x,)),
        ],
        smem=1,
        far=(1, 2, 3),
    )
    pieces, cot = halo(vols, cot_block, tiles_z, params)
    wide_scratch = pltpu.VMEM((sw, wide), BF)
    one_copy = pltpu.SemaphoreType.DMA
    mid_scratch = pltpu.VMEM((so, mid), F32)
    group_copies = pltpu.SemaphoreType.DMA((outer_groups,))
    acc_scratch = pltpu.VMEM((3, 3 * LANES, 2 * LANES), F32)
    c1_b, pad_b, pad_a, stats, plain = kernel_call(
        first_conv_b,
        [shape((so, mid_b), F32)] + [shape((sw, wide), BF)] * 2 + [stat_shape(1), token_shape],
        [weights] + pieces,
        scratch=[
            wide_scratch,
            wide_scratch,
            own_scratch,
            *band_scratch,
            pltpu.SemaphoreType.DMA((2,)),
        ],
        far=(0,),
        far_out=(1, 2),
        home=(3,),
        work=1 << 30,
    )
    stats_one = exchange(stats)
    c1_a, local_a = kernel_call(
        first_conv_a,
        [shape((so, mid), F32), shape((8, LANES), F32)],
        [weights, plain, pad_a],
        scratch=[wide_scratch, mid_scratch, own_scratch, *band_scratch, one_copy, group_copies],
        far=(0, 2),
        far_out=(0,),
        work=1 << 32,
    )
    hidden_b, c2_b, stats, token = kernel_call(
        second_conv_b,
        [shape((so, mid_b), BF), shape((si, mid), F32), stat_shape(3), token_shape],
        [bounds, c1_b, weights, stats_one, params, local_a, plain],
        scratch=[pltpu.VMEM((so, mid_b), BF), own_scratch, in_scratch, *band_scratch, one_copy],
        smem=1,
        far_out=(0,),
        home=(2,),
        far=(2,),
        work=1 << 30,
    )
    stats_two = exchange(stats)
    (taps_early,) = kernel_call(
        early_taps,
        [shape((world * hold, LANES), F32)],
        [c1_b, stats_one, pad_b, token],
        scratch=[wide_scratch, acc_scratch, own_scratch, one_copy],
        far=(2,),
        work=1 << 32,
    )
    stats, token = kernel_call(
        second_slope,
        [stat_shape(1 + hold), token_shape],
        [c2_b, stats_two, params, cot, taps_early],
        scratch=[own_scratch],
        home=(0,),
        work=1 << 27,
    )
    sums_two = exchange(stats)
    c2_a, local_a = kernel_call(
        second_conv_a,
        [shape((si, line), F32), shape((8, LANES), F32)],
        [bounds, c1_a, weights, stats_two, params, token],
        scratch=[mid_scratch, pltpu.VMEM((so, mid), BF), own_scratch, in_scratch, *band_scratch, one_copy],
        smem=1,
        far=(1, 2),
        work=1 << 32,
    )
    (delta_two,) = kernel_call(
        second_delta,
        [shape((si, mid), BF)],
        [bounds, c2_b, stats_two, params, cot, sums_two, local_a],
        scratch=[pltpu.VMEM((si, LANES), F32)],
        smem=1,
        work=1 << 27,
    )
    (taps_two,) = kernel_call(
        second_taps,
        [shape((world * hold, LANES), F32)],
        [delta_two, hidden_b],
        scratch=[pltpu.VMEM((so, mid_b), BF), acc_scratch, own_scratch, one_copy],
        far=(1,),
        work=1 << 32,
    )
    forward_x, backward_x = neighbours("gx")
    frames = [
        lax.ppermute(delta_two, "gx", forward_x),
        delta_two,
        lax.ppermute(delta_two, "gx", backward_x),
    ]
    slope, stats = kernel_call(
        first_slope,
        [shape((so, mid), F32), stat_shape(1 + 2 * hold)],
        [weights, c1_b, stats_one, params, local_a, taps_two, pad_b] + frames,
        scratch=[
            pltpu.VMEM((sw, mid + LANES), BF),
            own_scratch,
            *band_scratch,
            wide_scratch,
            acc_scratch,
            pltpu.VMEM((world * hold, LANES), F32),
            mid_scratch,
            one_copy,
            group_copies,
        ],
        far=(0, 6),
        far_out=(0,),
        home=(1,),
        work=1 << 30,
    )
    sums_one = exchange(stats)
    whole, token = kernel_call(
        mix,
        [shape((world, -(-2 * hold // 8) * 8, LANES), BF), token_shape],
        [bounds, stats_one, params, stats_two, sums_two, sums_one],
        smem=1,
    )
    whole = exchange(whole)
    (dx_b,) = kernel_call(
        first_delta,
        [shape(x_a.shape, BF)],
        [bounds, slope, c1_b, stats_one, params, sums_one, weights, token],
        scratch=[
            mid_scratch,
            pltpu.VMEM((so, mid), BF),
            pltpu.VMEM((si, line), BF),
            in_scratch,
            *band_scratch,
            one_copy,
        ],
        smem=1,
        far=(1, 6),
        work=1 << 31,
    )
    y_a, grad_norm = kernel_call(
        out_a,
        [shape(x_a.shape, BF), shape((4, chan), F32)],
        [c2_a, sums_one, sums_two, params, token],
        scratch=[pltpu.VMEM((si, line), BF)],
        work=1 << 31,
    )
    weight_shape = shape((3, 3, 3, chan, chan), F32)
    grad_one, grad_two = kernel_call(
        last,
        [weight_shape, weight_shape],
        [whole],
        scratch=[pltpu.VMEM((world * hold, LANES), F32)],
    )
    return (y_a, dx_b, grad_one, grad_two, grad_norm)


def solution(mesh):
    block = P(None, "gx", "gy", "gz")
    placed = (block, block, P(), P(), P(), P(), P(), P(), block)

    return jax.shard_map(
        body,
        mesh=mesh,
        in_specs=placed,
        out_specs=(block, block, P(), P(), P()),
        check_vma=False,
    )
```

time: 146 us -> 143 us (0.979)
  starting transfers between devices: 44.7 us -> 39.9 us
  Pallas kernels: 57.2 us -> 61.8 us
  local copies, waits for them, and re-layouts: 3.94 us -> 0.91 us
    pallas_call x20 -> x17, Pallas kernels: 57.2 us -> 61.8 us  [kernel_call(): pl.pallas_call(body, out_shape=out_shape, in_specs=[SM if i < smem else H...]
    ppermute x2 -> x1, starting transfers between devices: 9.12 us -> 4.57 us  [halo(): lax.ppermute(mine, 'gx', forward_x)]
    ppermute x4, waiting for transfers between devices: 0.01 us -> 4.52 us  [the longest x1 1.87 us: body(): lax.ppermute(delta_two, 'gx', backward_x)]
    unnamed x18 -> x4, local copies, waits for them, and re-layouts: 3.86 us -> 0.83 us
    ppermute x2 -> x1, waiting for transfers between devices: 6.35 us -> 3.32 us  [halo(): got_z = [lax.ppermute(tiles_z[0], 'gz', [(0, 1), (1, 0)])]]
    ppermute x4, starting transfers between devices: 9.08 us -> 11.9 us  [the longest x1 4.75 us: body(): lax.ppermute(delta_two, 'gx', forward_x)]
    all_to_all x4, starting transfers between devices: 20.3 us -> 18.3 us  [exchange(): return lax.all_to_all(spread_rows, AXES, 0, 0)]
    ppermute x2 -> x1, starting transfers between devices: 2.76 us -> 1.29 us  [halo(): lax.ppermute(mine, 'gx', backward_x)]
  transfers between devices with their start and end apart: 18 -> 13, of which waited for: 8 -> 10; matrix products, arithmetic and copies ran while one was open for 0% -> 0% of each run, Pallas kernels for 21% -> 22%
where the time goes in v4:
time: 143 us; the launch traced here: 142 us
  Pallas kernels  61.8 us (43%)
  starting transfers between devices  39.9 us (28%)
  waiting for transfers between devices  22.5 us (16%)
  blocking collectives  15.8 us (11%)
    pallas_call x17, Pallas kernels, kernel_call(): pl.pallas_call(body, out_shape=out_shape, in_specs=[SM if i < smem else H...  61.8 us
    all_to_all x4, starting transfers between devices, exchange(): return lax.all_to_all(spread_rows, AXES, 0, 0)  18.3 us
    all_to_all x1, blocking collectives, exchange(): return lax.all_to_all(spread_rows, AXES, 0, 0)  15.8 us
    all_to_all x4, waiting for transfers between devices, exchange(): return lax.all_to_all(spread_rows, AXES, 0, 0)  7.59 us
    ppermute x1, waiting for transfers between devices, halo(): lax.ppermute(mine, 'gx', backward_x)  5.37 us
    ppermute x1, starting transfers between devices, body(): lax.ppermute(delta_two, 'gx', forward_x)  4.75 us
    ppermute x1, starting transfers between devices, halo(): from_low = lax.ppermute(block, 'gx', forward_x)  4.58 us
    ppermute x1, starting transfers between devices, halo(): lax.ppermute(mine, 'gx', forward_x)  4.57 us
  transfers between devices with their start and end apart: 13, of which 10 were waited for; matrix products, arithmetic and copies ran while one was open for 0% of the time, Pallas kernels for 22%

profile of v4, /device:TPU:0, one launch (start us, length us, event | category | flops | bytes accessed | tf_op | source)
XLA Modules:
  0.0 141.8 jit_solution(14288675070414382044)
XLA Ops:
  0.7 0.1 stack.39.bound
  0.8 3.1 %shard_map.129 = (bf16[512,512]{1,0:T(8,128)(2,1)S(1)}, bf16[256,640]{1,0:T(8,128)(2,1)S(1)}, bf16[1,96,640]{2,1,0:T(8,128)(2,1)S(1)}) custom-call(s32[9]{0:T(128)S(1)} %stack.39.bound, bf16[32,2,16,128]{3,2,1,0:T(8,128)(2,1)} %a_ref.1, bf16[32,2,16,128]{3,2,1,0:T(8,128)(2,1)} %b_ref.1, bf16[32,2,16,128]{3,2,1,0:T(8,128)(2,1)} %go_ref.1), custom_call_target="tpu_custom_call" | custom-call | bytes 1048576 | tf_op jit(solution)/shard_map/pallas_call | solution.py:31
  3.9 3.1 %collective-permute-start.2 = (bf16[96,640]{1,0:T(8,128)(2,1)S(1)}, bf16[96,640]{1,0:T(8,128)(2,1)S(1)}, u32[]{:S(2)}, u32[]{:S(2)}) collective-permute-start(bf16[96,640]{1,0:T(8,128)(2,1)S(1)} %bitcast.14), channel_id=1, source_target_pairs={{0,1},{1,0},{2,3},{3,2},{4,5},{5,4},{6,7},{7,6},{8,9},{9,8},{10,11... | collective-permute-start | bytes 368648 | tf_op jit(solution)/shard_map/ppermute | solution.py:329
  7.0 3.3 %collective-permute-done.2.refs_0_ = bf16[96,640]{1,0:T(8,128)(2,1)S(1)} collective-permute-done((bf16[96,640]{1,0:T(8,128)(2,1)S(1)}, bf16[96,640]{1,0:T(8,128)(2,1)S(1)}, u32[]{:S(2)}, u32[]{:S(2)}) %collective-permute-start.2) | collective-permute-done | bytes 122912 | tf_op jit(solution)/shard_map/ppermute | solution.py:329
  10.3 0.6 shard_map.130
  10.9 0.1 collective-permute-start.3
  11.0 0.7 collective-permute-start.4
  11.7 1.3 collective-permute-start.1
  13.0 4.6 %collective-permute-start = (bf16[512,512]{1,0:T(8,128)(2,1)S(1)}, bf16[512,512]{1,0:T(8,128)(2,1)S(1)}, u32[]{:S(2)}, u32[]{:S(2)}) collective-permute-start(bf16[512,512]{1,0:T(8,128)(2,1)S(1)} %get-tuple-element.39.t_ref.refs_1_), channel_id=1, source_target_pairs={{0,8},{8,16},{16,24},{1,9},{9,17},{17,25},{2,10},{10,18},{18,26},{... | collective-permute-start | bytes 1572872 | tf_op jit(solution)/shard_map/ppermute | solution.py:335
  17.6 2.3 %shard_map.128 = (bf16[1152,128]{1,0:T(8,128)(2,1)}, f32[8,128]{1,0:T(8,128)S(1)}) custom-call(bf16[3,3,3,32,32]{4,3,2,1,0:T(8,128)(2,1)} %w1_ref.1, bf16[3,3,3,32,32]{4,3,2,1,0:T(8,128)(2,1)} %w2_ref.1, f32[1,32]{1,0:T(1,128)} %bitcast.15, f32[1,32]{1,0:T(1,128)} %bitcast.16, f32[1,32]{1,0:T(1,128)} %bitcast.17, f32[1,32]{1,0:T(1,128)} %bitcast.18), custom_call_target="tpu_custom_call" | custom-call | flops 2147483648 | bytes 1048576 | tf_op jit(solution)/shard_map/pallas_call | solution.py:31
  19.9 0.0 collective-permute-done.3.a_ref
  19.9 0.0 collective-permute-done.4.b_ref
  19.9 0.7 shard_map.131
  20.7 1.3 collective-permute-start.6
  22.0 4.6 %collective-permute-start.5 = (bf16[1296,128]{1,0:T(8,128)(2,1)S(1)}, bf16[1296,128]{1,0:T(8,128)(2,1)S(1)}, u32[]{:S(2)}, u32[]{:S(2)}) collective-permute-start(bf16[1296,128]{1,0:T(8,128)(2,1)S(1)} %get-tuple-element.46.refs_4_), channel_id=1, source_target_pairs={{0,8},{8,16},{16,24},{1,9},{9,17},{17,25},{2,10},{10,18},{18,26},{... | collective-permute-start | bytes 995336 | tf_op jit(solution)/shard_map/ppermute | solution.py:442
  26.5 0.0 collective-permute-done.1.refs_2_
  26.6 1.5 %collective-permute-done.refs_0_ = bf16[512,512]{1,0:T(8,128)(2,1)S(1)} collective-permute-done((bf16[512,512]{1,0:T(8,128)(2,1)S(1)}, bf16[512,512]{1,0:T(8,128)(2,1)S(1)}, u32[]{:S(2)}, u32[]{:S(2)}) %collective-permute-start) | collective-permute-done | bytes 524320 | tf_op jit(solution)/shard_map/ppermute | solution.py:335
  28.0 5.4 %collective-permute-done.6.refs_5_ = bf16[1296,128]{1,0:T(8,128)(2,1)S(1)} collective-permute-done((bf16[1296,128]{1,0:T(8,128)(2,1)S(1)}, bf16[1296,128]{1,0:T(8,128)(2,1)S(1)}, u32[]{:S(2)}, u32[]{:S(2)}) %collective-permute-start.6) | collective-permute-done | bytes 331808 | tf_op jit(solution)/shard_map/ppermute | solution.py:444
  33.4 1.7 %collective-permute-done.5.refs_3_ = bf16[1296,128]{1,0:T(8,128)(2,1)S(1)} collective-permute-done((bf16[1296,128]{1,0:T(8,128)(2,1)S(1)}, bf16[1296,128]{1,0:T(8,128)(2,1)S(1)}, u32[]{:S(2)}, u32[]{:S(2)}) %collective-permute-start.5) | collective-permute-done | bytes 331808 | tf_op jit(solution)/shard_map/ppermute | solution.py:442
  35.1 6.6 %shard_map.132 = (f32[592,768]{1,0:T(8,128)S(1)}, bf16[880,896]{1,0:T(8,128)(2,1)}, bf16[880,896]{1,0:T(8,128)(2,1)}, f32[32,1,128]{2,1,0:T(1,128)}, f32[8,128]{1,0:T(8,128)S(1)}) custom-call(bf16[1152,128]{1,0:T(8,128)(2,1)} %get-tuple-element.38.w_ref, bf16[512,512]{1,0:T(8,128)(2,1)S(1)} %collective-permute-done.refs_0_, ...), custom_call_target="tpu_custom_call" | custom-call | flops 1073741824 | bytes 1048576 | tf_op jit(solution)/shard_map/pallas_call | solution.py:31
  41.8 8.1 %all-to-all-start = ((f32[32,1,128]{2,1,0:T(1,128)}), f32[32,1,128]{2,1,0:T(1,128)S(1)}, u32[]{:S(2)}, u32[]{:S(2)}) async-start(f32[32,1,128]{2,1,0:T(1,128)} %get-tuple-element.51), calls=%async_computation | async-start | bytes 32768 | tf_op jit(solution)/shard_map/all_to_all | solution.py:47
  49.8 6.0 %shard_map.133 = (f32[592,640]{1,0:T(8,128)}, f32[8,128]{1,0:T(8,128)S(1)}) custom-call(bf16[1152,128]{1,0:T(8,128)(2,1)} %get-tuple-element.38.w_ref, f32[8,128]{1,0:T(8,128)S(1)} %get-tuple-element.47.after.m_ref, bf16[880,896]{1,0:T(8,128)(2,1)} %get-tuple-element.48.x_far), custom_call_target="tpu_custom_call" | custom-call | flops 4294967296 | bytes 1048576 | tf_op jit(solution)/shard_map/pallas_call | solution.py:31
  55.8 1.2 all-to-all-done.st_in
  57.0 5.5 %shard_map.134 = (bf16[592,768]{1,0:T(8,128)(2,1)}, f32[304,640]{1,0:T(8,128)S(1)}, f32[32,3,128]{2,1,0:T(4,128)}, f32[8,128]{1,0:T(8,128)S(1)}) custom-call(s32[9]{0:T(128)S(1)} %stack.39.bound, f32[592,768]{1,0:T(8,128)S(1)} %get-tuple-element.50.c_ref, bf16[1152,128]{1,0:T(8,128)(2,1)} %get-tuple-element.38.w_ref, f32[32,1,128]{2,1,0:T(1,128)S(1)} %all-to-all-done.st_in, ...), custom_call_target="tpu_custom_call" | custom-call | flops 1073741824 | bytes 1048576 | tf_op jit(solution)/shard_map/pallas_call | solution.py:31
  62.4 4.7 %all-to-all-start.1 = ((f32[32,3,128]{2,1,0:T(4,128)}), f32[32,3,128]{2,1,0:T(4,128)S(1)}, u32[]{:S(2)}, u32[]{:S(2)}) async-start(f32[32,3,128]{2,1,0:T(4,128)} %get-tuple-element.53), calls=%async_computation.1 | async-start | bytes 131072 | tf_op jit(solution)/shard_map/all_to_all | solution.py:47
  67.1 4.7 %shard_map.135.t_ref = f32[224,128]{1,0:T(8,128)S(1)} custom-call(f32[592,768]{1,0:T(8,128)S(1)} %get-tuple-element.50.c_ref, f32[32,1,128]{2,1,0:T(1,128)S(1)} %all-to-all-done.st_in, bf16[880,896]{1,0:T(8,128)(2,1)} %get-tuple-element.56.x_far, f32[8,128]{1,0:T(8,128)S(1)} %get-tuple-element.57.after), custom_call_target="tpu_custom_call" | custom-call | flops 4294967296 | bytes 1048576 | tf_op jit(solution)/shard_map/pallas_call | solution.py:31
  71.9 2.9 %all-to-all-done.1.st_in.plain_ref = f32[32,3,128]{2,1,0:T(4,128)S(1)} async-done(((f32[32,3,128]{2,1,0:T(4,128)}), f32[32,3,128]{2,1,0:T(4,128)S(1)}, u32[]{:S(2)}, u32[]{:S(2)}) %all-to-all-start.1) | async-done | bytes 49184 | tf_op jit(solution)/shard_map/all_to_all | solution.py:47
  74.7 1.7 %shard_map.136 = (f32[32,8,128]{2,1,0:T(8,128)}, f32[8,128]{1,0:T(8,128)S(1)}) custom-call(f32[304,640]{1,0:T(8,128)S(1)} %get-tuple-element.54.c_ref, f32[32,3,128]{2,1,0:T(4,128)S(1)} %all-to-all-done.1.st_in.plain_ref, f32[8,128]{1,0:T(8,128)S(1)} %get-tuple-element.45.token_ref.p_ref, bf16[304,640]{1,0:T(8,128)(2,1)S(1)} %get-tuple-element.55.go_ref, ...), custom_call_target="tpu_custom_call" | custom-call | flops 134217728 | bytes 1048576 | tf_op jit(solution)/shard_map/pallas_call | solution.py:31
  76.4 3.0 %all-to-all-start.2 = ((f32[32,8,128]{2,1,0:T(8,128)}), f32[32,8,128]{2,1,0:T(8,128)S(1)}, u32[]{:S(2)}, u32[]{:S(2)}) async-start(f32[32,8,128]{2,1,0:T(8,128)} %get-tuple-element.61), calls=%async_computation.2 | async-start | bytes 262144 | tf_op jit(solution)/shard_map/all_to_all | solution.py:47
  79.4 5.5 %shard_map.137 = (f32[304,512]{1,0:T(8,128)S(1)}, f32[8,128]{1,0:T(8,128)S(1)}) custom-call(s32[9]{0:T(128)S(1)} %stack.39.bound, f32[592,640]{1,0:T(8,128)} %get-tuple-element.49.c_far, bf16[1152,128]{1,0:T(8,128)(2,1)} %get-tuple-element.38.w_ref, f32[32,3,128]{2,1,0:T(4,128)S(1)} %all-to-all-done.1.st_in.plain_ref, ...), custom_call_target="tpu_custom_call" | custom-call | flops 4294967296 | bytes 1048576 | tf_op jit(solution)/shard_map/pallas_call | solution.py:31
  84.9 0.0 copy-start
  84.9 0.8 copy-done
  85.7 2.3 %all-to-all-done.2.sums_in.early_ref.st_two = f32[32,8,128]{2,1,0:T(8,128)S(1)} async-done(((f32[32,8,128]{2,1,0:T(8,128)}), f32[32,8,128]{2,1,0:T(8,128)S(1)}, u32[]{:S(2)}, u32[]{:S(2)}) %all-to-all-start.2) | async-done | bytes 131104 | tf_op jit(solution)/shard_map/all_to_all | solution.py:47
  88.0 1.4 %shard_map.138.d_ref.refs_1_ = bf16[304,640]{1,0:T(8,128)(2,1)S(1)} custom-call(s32[9]{0:T(128)S(1)} %stack.39.bound, f32[304,640]{1,0:T(8,128)S(1)} %get-tuple-element.54.c_ref, f32[32,3,128]{2,1,0:T(4,128)S(1)} %all-to-all-done.1.st_in.plain_ref, f32[8,128]{1,0:T(8,128)S(1)} %get-tuple-element.45.token_ref.p_ref, ...), custom_call_target="tpu_custom_call" | custom-call | flops 134217728 | bytes 1048576 | tf_op jit(solution)/shard_map/pallas_call | solution.py:31
  89.4 1.3 collective-permute-start.8
  90.7 4.8 %collective-permute-start.7 = (bf16[304,640]{1,0:T(8,128)(2,1)S(1)}, bf16[304,640]{1,0:T(8,128)(2,1)S(1)}, u32[]{:S(2)}, u32[]{:S(2)}) collective-permute-start(bf16[304,640]{1,0:T(8,128)(2,1)S(1)} %shard_map.138.d_ref.refs_1_), channel_id=1, source_target_pairs={{0,8},{8,16},{16,24},{1,9},{9,17},{17,25},{2,10},{10,18},{18,26},{... | collective-permute-start | bytes 1167368 | tf_op jit(solution)/shard_map/ppermute | solution.py:953
  95.5 4.5 %shard_map.139.gw_two = f32[224,128]{1,0:T(8,128)S(1)} custom-call(bf16[304,640]{1,0:T(8,128)(2,1)S(1)} %shard_map.138.d_ref.refs_1_, bf16[592,768]{1,0:T(8,128)(2,1)} %get-tuple-element.62.h_far), custom_call_target="tpu_custom_call" | custom-call | flops 4294967296 | bytes 1048576 | tf_op jit(solution)/shard_map/pallas_call | solution.py:31
  99.9 1.9 %collective-permute-done.8.refs_2_ = bf16[304,640]{1,0:T(8,128)(2,1)S(1)} collective-permute-done((bf16[304,640]{1,0:T(8,128)(2,1)S(1)}, bf16[304,640]{1,0:T(8,128)(2,1)S(1)}, u32[]{:S(2)}, u32[]{:S(2)}) %collective-permute-start.8) | collective-permute-done | bytes 389152 | tf_op jit(solution)/shard_map/ppermute | solution.py:955
  101.8 1.2 collective-permute-done.7.refs_0_
  103.0 9.4 %shard_map.140 = (f32[592,640]{1,0:T(8,128)}, f32[32,15,128]{2,1,0:T(8,128)}) custom-call(bf16[1152,128]{1,0:T(8,128)(2,1)} %get-tuple-element.38.w_ref, f32[592,768]{1,0:T(8,128)S(1)} %get-tuple-element.50.c_ref, f32[32,1,128]{2,1,0:T(1,128)S(1)} %all-to-all-done.st_in, f32[8,128]{1,0:T(8,128)S(1)} %get-tuple-element.45.token_ref.p_ref, ...), custom_call_target="tpu_custom_call" | custom-call | flops 1073741824 | bytes 1048576 | tf_op jit(solution)/shard_map/pallas_call | solution.py:31
  112.3 15.8 %all_to_all.25.late_ref.st_in.sums_in = f32[32,15,128]{2,1,0:T(8,128)S(1)} all-to-all(f32[32,15,128]{2,1,0:T(8,128)} %get-tuple-element.63), channel_id=1, replica_groups=mesh['gx'=4,'gy'=4,'gz'=2] {'gx','gy','gz'}, dimensions={0} | all-to-all | bytes 491520 | tf_op jit(solution)/shard_map/all_to_all | solution.py:47
  128.1 1.5 %shard_map.141 = (bf16[32,16,128]{2,1,0:T(8,128)(2,1)}, f32[8,128]{1,0:T(8,128)S(1)}) custom-call(s32[9]{0:T(128)S(1)} %stack.39.bound, f32[32,1,128]{2,1,0:T(1,128)S(1)} %all-to-all-done.st_in, f32[8,128]{1,0:T(8,128)S(1)} %get-tuple-element.45.token_ref.p_ref, f32[32,3,128]{2,1,0:T(4,128)S(1)} %all-to-all-done.1.st_in.plain_ref, ...), custom_call_target="tpu_custom_call" | custom-call | bytes 1048576 | tf_op jit(solution)/shard_map/pallas_call | solution.py:31
  129.6 2.6 %all-to-all-start.4 = ((bf16[32,16,128]{2,1,0:T(8,128)(2,1)}), bf16[32,16,128]{2,1,0:T(8,128)(2,1)S(1)}, u32[]{:S(2)}, u32[]{:S(2)}) async-start(bf16[32,16,128]{2,1,0:T(8,128)(2,1)} %get-tuple-element.67), calls=%async_computation.4 | async-start | bytes 262144 | tf_op jit(solution)/shard_map/all_to_all | solution.py:47
  132.2 5.6 %shard_map.143 = bf16[32,2,16,128]{3,2,1,0:T(8,128)(2,1)} custom-call(s32[9]{0:T(128)S(1)} %stack.39.bound, f32[592,640]{1,0:T(8,128)} %get-tuple-element.66.s_far, f32[592,768]{1,0:T(8,128)S(1)} %get-tuple-element.50.c_ref, f32[32,1,128]{2,1,0:T(1,128)S(1)} %all-to-all-done.st_in, f32[8,128]{1,0:T(8,128)S(1)} %get-tuple-element.45.token_ref.p_ref, ...), custom_call_target="tpu_custom_call" | custom-call | flops 2147483648 | bytes 1048576 | tf_op jit(solution)/shard_map/pallas_call | solution.py:31
  137.8 0.0 copy-done.1
  137.8 1.7 %shard_map.142 = (bf16[32,2,16,128]{3,2,1,0:T(8,128)(2,1)}, f32[4,32]{1,0:T(4,128)}) custom-call(f32[304,512]{1,0:T(8,128)S(1)} %copy-done.1, f32[32,15,128]{2,1,0:T(8,128)S(1)} %all_to_all.25.late_ref.st_in.sums_in, f32[32,8,128]{2,1,0:T(8,128)S(1)} %all-to-all-done.2.sums_in.early_ref.st_two, f32[8,128]{1,0:T(8,128)S(1)} %get-tuple-element.45.token_ref.p_ref, ...), custom_call_target="tpu_custom_call" | custom-call | flops 2147483648 | bytes 1048576 | tf_op jit(solution)/shard_map/pallas_call | solution.py:31
  139.5 1.3 all-to-all-done.4.got_ref
  140.8 1.1 shard_map.144
  (1 shorter events, 0.0 us)
Async XLA Ops:
  3.9 6.4 %collective-permute-start.2 = (bf16[96,640]{1,0:T(8,128)(2,1)S(1)}, bf16[96,640]{1,0:T(8,128)(2,1)S(1)}, u32[]{:S(2)}, u32[]{:S(2)}) collective-permute-start(bf16[96,640]{1,0:T(8,128)(2,1)S(1)} %bitcast.14), channel_id=1, source_target_pairs={{0,1},{1,0},{2,3},{3,2},{4,5},{5,4},{6,7},{7,6},{8,9},{9,8},{10,11... | collective-permute-start | bytes 368648 | tf_op jit(solution)/shard_map/ppermute | solution.py:329
  10.9 9.0 %collective-permute-start.3 = (bf16[912,128]{1,0:T(8,128)(2,1)S(1)}, bf16[912,128]{1,0:T(8,128)(2,1)S(1)}, u32[]{:S(2)}, u32[]{:S(2)}) collective-permute-start(bf16[912,128]{1,0:T(8,128)(2,1)S(1)} %get-tuple-element.42), channel_id=1, source_target_pairs={{0,2},{2,0},{4,6},{6,4},{1,3},{3,1},{5,7},{7,5},{8,10},{10,8},{12,... | collective-permute-start | bytes 700424 | tf_op jit(solution)/shard_map/ppermute | solution.py:392
  11.0 8.9 %collective-permute-start.4 = (bf16[912,128]{1,0:T(8,128)(2,1)S(1)}, bf16[912,128]{1,0:T(8,128)(2,1)S(1)}, u32[]{:S(2)}, u32[]{:S(2)}) collective-permute-start(bf16[912,128]{1,0:T(8,128)(2,1)S(1)} %get-tuple-element.43), channel_id=1, source_target_pairs={{2,4},{4,2},{3,5},{5,3},{10,12},{12,10},{11,13},{13,11},{18,20},{2... | collective-permute-start | bytes 700424 | tf_op jit(solution)/shard_map/ppermute | solution.py:393
  11.7 14.9 %collective-permute-start.1 = (bf16[512,512]{1,0:T(8,128)(2,1)S(1)}, bf16[512,512]{1,0:T(8,128)(2,1)S(1)}, u32[]{:S(2)}, u32[]{:S(2)}) collective-permute-start(bf16[512,512]{1,0:T(8,128)(2,1)S(1)} %get-tuple-element.39.t_ref.refs_1_), channel_id=1, source_target_pairs={{8,0},{16,8},{24,16},{9,1},{17,9},{25,17},{10,2},{18,10},{26,18},{... | collective-permute-start | bytes 1572872 | tf_op jit(solution)/shard_map/ppermute | solution.py:336
  13.0 15.0 %collective-permute-start = (bf16[512,512]{1,0:T(8,128)(2,1)S(1)}, bf16[512,512]{1,0:T(8,128)(2,1)S(1)}, u32[]{:S(2)}, u32[]{:S(2)}) collective-permute-start(bf16[512,512]{1,0:T(8,128)(2,1)S(1)} %get-tuple-element.39.t_ref.refs_1_), channel_id=1, source_target_pairs={{0,8},{8,16},{16,24},{1,9},{9,17},{17,25},{2,10},{10,18},{18,26},{... | collective-permute-start | bytes 1572872 | tf_op jit(solution)/shard_map/ppermute | solution.py:335
  20.7 12.7 %collective-permute-start.6 = (bf16[1296,128]{1,0:T(8,128)(2,1)S(1)}, bf16[1296,128]{1,0:T(8,128)(2,1)S(1)}, u32[]{:S(2)}, u32[]{:S(2)}) collective-permute-start(bf16[1296,128]{1,0:T(8,128)(2,1)S(1)} %get-tuple-element.46.refs_4_), channel_id=1, source_target_pairs={{8,0},{16,8},{24,16},{9,1},{17,9},{25,17},{10,2},{18,10},{26,18},{... | collective-permute-start | bytes 995336 | tf_op jit(solution)/shard_map/ppermute | solution.py:444
  22.0 13.2 %collective-permute-start.5 = (bf16[1296,128]{1,0:T(8,128)(2,1)S(1)}, bf16[1296,128]{1,0:T(8,128)(2,1)S(1)}, u32[]{:S(2)}, u32[]{:S(2)}) collective-permute-start(bf16[1296,128]{1,0:T(8,128)(2,1)S(1)} %get-tuple-element.46.refs_4_), channel_id=1, source_target_pairs={{0,8},{8,16},{16,24},{1,9},{9,17},{17,25},{2,10},{10,18},{18,26},{... | collective-permute-start | bytes 995336 | tf_op jit(solution)/shard_map/ppermute | solution.py:442
  41.8 15.2 %all-to-all-start = ((f32[32,1,128]{2,1,0:T(1,128)}), f32[32,1,128]{2,1,0:T(1,128)S(1)}, u32[]{:S(2)}, u32[]{:S(2)}) async-start(f32[32,1,128]{2,1,0:T(1,128)} %get-tuple-element.51), calls=%async_computation | async-start | bytes 32768 | tf_op jit(solution)/shard_map/all_to_all | solution.py:47
  62.4 12.3 %all-to-all-start.1 = ((f32[32,3,128]{2,1,0:T(4,128)}), f32[32,3,128]{2,1,0:T(4,128)S(1)}, u32[]{:S(2)}, u32[]{:S(2)}) async-start(f32[32,3,128]{2,1,0:T(4,128)} %get-tuple-element.53), calls=%async_computation.1 | async-start | bytes 131072 | tf_op jit(solution)/shard_map/all_to_all | solution.py:47
  76.4 11.6 %all-to-all-start.2 = ((f32[32,8,128]{2,1,0:T(8,128)}), f32[32,8,128]{2,1,0:T(8,128)S(1)}, u32[]{:S(2)}, u32[]{:S(2)}) async-start(f32[32,8,128]{2,1,0:T(8,128)} %get-tuple-element.61), calls=%async_computation.2 | async-start | bytes 262144 | tf_op jit(solution)/shard_map/all_to_all | solution.py:47
  84.9 0.8 copy-start
  89.4 12.4 %collective-permute-start.8 = (bf16[304,640]{1,0:T(8,128)(2,1)S(1)}, bf16[304,640]{1,0:T(8,128)(2,1)S(1)}, u32[]{:S(2)}, u32[]{:S(2)}) collective-permute-start(bf16[304,640]{1,0:T(8,128)(2,1)S(1)} %shard_map.138.d_ref.refs_1_), channel_id=1, source_target_pairs={{8,0},{16,8},{24,16},{9,1},{17,9},{25,17},{10,2},{18,10},{26,18},{... | collective-permute-start | bytes 1167368 | tf_op jit(solution)/shard_map/ppermute | solution.py:955
  90.7 12.3 %collective-permute-start.7 = (bf16[304,640]{1,0:T(8,128)(2,1)S(1)}, bf16[304,640]{1,0:T(8,128)(2,1)S(1)}, u32[]{:S(2)}, u32[]{:S(2)}) collective-permute-start(bf16[304,640]{1,0:T(8,128)(2,1)S(1)} %shard_map.138.d_ref.refs_1_), channel_id=1, source_target_pairs={{0,8},{8,16},{16,24},{1,9},{9,17},{17,25},{2,10},{10,18},{18,26},{... | collective-permute-start | bytes 1167368 | tf_op jit(solution)/shard_map/ppermute | solution.py:953
  129.6 11.2 %all-to-all-start.4 = ((bf16[32,16,128]{2,1,0:T(8,128)(2,1)}), bf16[32,16,128]{2,1,0:T(8,128)(2,1)S(1)}, u32[]{:S(2)}, u32[]{:S(2)}) async-start(bf16[32,16,128]{2,1,0:T(8,128)(2,1)} %get-tuple-element.67), calls=%async_computation.4 | async-start | bytes 262144 | tf_op jit(solution)/shard_map/all_to_all | solution.py:47
  132.2 5.6 %copy-start.1 = (f32[304,512]{1,0:T(8,128)S(1)}, f32[304,512]{1,0:T(8,128)}, u32[]{:S(2)}) copy-start(f32[304,512]{1,0:T(8,128)} %copy-done) | copy-start | bytes 1867780

commit v5 on v4

--- a/solution.py
+++ b/solution.py
@@ -60,6 +60,8 @@
 
 
 def lane_at(group):
+    if isinstance(group, int):
+        return slice(group * LANES, (group + 1) * LANES)
     return pl.ds(pl.multiple_of(group * LANES, LANES), LANES)
 
 
@@ -75,16 +77,31 @@
     )
 
 
-def tap_products(d_rows, h_ref, start, group, pitch, acc):
-    size = d_rows.shape[0]
-    three = jnp.concatenate(
-        [pltpu.roll(d_rows, size - 1, 0), d_rows, pltpu.roll(d_rows, 1, 0)], axis=1
-    )
-    left = three.T.astype(BF)
-    at = pl.multiple_of(group * LANES, LANES)
-    for d in range(3):
-        right = h_ref[pl.ds(start + d * pitch, size), pl.ds(at, 2 * LANES)]
-        acc[d] = acc[d] + jnp.dot(left, right, preferred_element_type=F32)
+def tap_products(groups, h_ref, start, first, pitch):
+    size = groups[0].shape[0]
+    left, right = [], []
+    for g, rows in enumerate(groups):
+        left.append(
+            jnp.concatenate(
+                [pltpu.roll(rows, size - 1, 0), rows, pltpu.roll(rows, 1, 0)], axis=1
+            ).astype(BF)
+        )
+        at = (first + g) * LANES
+        right.append(
+            jnp.concatenate(
+                [
+                    h_ref[start + d * pitch : start + d * pitch + size, at : at + 2 * LANES]
+                    for d in range(3)
+                ],
+                axis=1,
+            )
+        )
+    return lax.dot_general(
+        jnp.concatenate(left, axis=0),
+        jnp.concatenate(right, axis=0),
+        (((0,), (0,)), ((), ())),
+        preferred_element_type=F32,
+    )
 
 
 def fold_taps(acc, out, first, chan, offset):
@@ -93,9 +110,8 @@
         for t in range(3):
             rows = sum(
                 acc[
-                    d,
                     t * LANES + j * chan : t * LANES + (j + 1) * chan,
-                    (j + offset) * chan : (j + offset + 3) * chan,
+                    d * 2 * LANES + (j + offset) * chan : d * 2 * LANES + (j + offset + 3) * chan,
                 ]
                 for j in range(per)
             )
@@ -153,8 +169,9 @@
     so, si, sw = po * pitch + SEAM, pi * pitch + SEAM, (span_x + 4) * pitch + SEAM
     flat_rows = span_x * span_z
     seams = (span_x + 1) * SEAM
-    strip_at = (0, si + tiles * seams)
-    strip_rows = strip_at[1] + 2 * si + tiles * seams
+    packs = span_x * SEAM
+    strip_at = (0, si + tiles * packs)
+    strip_rows = strip_at[1] + 2 * si + tiles * packs
     swap = lax.axis_size("gz") == 2
     tap_rows = -(-27 // per) * chan
     hold = -(-tap_rows // world)
@@ -346,46 +363,57 @@
                 a_ref[rows, :] = jnp.where(ok, high, low).astype(BF)
                 b_ref[rows, :] = jnp.where(ok, low, high).astype(BF)
 
-            for v in range(3):
-                source, lanes = (t_ref, line) if v < 2 else (g_ref, mid)
-                for x in range(span_x + 1):
-                    tile = jnp.zeros((SEAM, mid), F32)
-                    if x < span_x:
-                        at = (v * span_x + x) * SEAM
-                        value = got[0][at : at + SEAM, :].astype(F32)
-                        ok = row >= SEAM - 4
-                        if swap:
-                            ok = ok & (jnp.full(row.shape, bound[6], jnp.int32) == 1)
-                        tile = jnp.where(ok, value, tile)
-                    if x > 0:
-                        at = (v * span_x + x - 1) * SEAM
-                        value = got[-1][at : at + SEAM, :].astype(F32)
-                        ok = row < 4
-                        if swap:
-                            ok = ok & (jnp.full(row.shape, bound[6], jnp.int32) == 0)
-                        tile = jnp.where(ok, value, tile)
-                    tile = tile.astype(BF)
-                    s_ref[v * seams + x * SEAM : v * seams + (x + 1) * SEAM, :] = tile
-                    base = v * si + x * pitch
-                    choose(
-                        slice(base, base + SEAM),
-                        tile[:, :LANES],
-                        tile[:, lanes - LANES : lanes],
-                        even,
-                    )
-                    if x < span_x:
-                        at = ((v * span_x + x) % (2 * span_x)) * span_z
-                        own_rows = slice(at, at + span_z)
-                        choose(
-                            slice(base + SEAM, base + pitch),
-                            source[own_rows, :LANES],
-                            source[own_rows, lanes - LANES : lanes],
-                            even_block,
-                        )
+            def tile_of(v, x):
+                tile = jnp.zeros((SEAM, mid), F32)
+                if x < span_x:
+                    at = (v * span_x + x) * SEAM
+                    value = got[0][at : at + SEAM, :].astype(F32)
+                    ok = row >= SEAM - 4
+                    if swap:
+                        ok = ok & (jnp.full(row.shape, bound[6], jnp.int32) == 1)
+                    tile = jnp.where(ok, value, tile)
+                if x > 0:
+                    at = (v * span_x + x - 1) * SEAM
+                    value = got[-1][at : at + SEAM, :].astype(F32)
+                    ok = row < 4
+                    if swap:
+                        ok = ok & (jnp.full(row.shape, bound[6], jnp.int32) == 0)
+                    tile = jnp.where(ok, value, tile)
+                tile = tile.astype(BF)
+                s_ref[v * seams + x * SEAM : v * seams + (x + 1) * SEAM, :] = tile
+                return tile
+
+            def ends(value, v):
+                lanes = line if v < 2 else mid
+                return value[:, :LANES], value[:, lanes - LANES : lanes]
+
+            def shared(values):
+                (low, high), (cot_low, cot_high) = ends(values[0], 0), ends(values[1], 2)
+                lane = lax.broadcasted_iota(jnp.int32, low.shape, 1)
+                half = lane < 2 * chan
+                return (
+                    jnp.where(half, low.astype(F32), cot_low.astype(F32)),
+                    jnp.where(half, cot_high.astype(F32), high.astype(F32)),
+                )
+
+            for x in range(span_x + 1):
+                seam_tiles = [tile_of(v, x) for v in range(3)]
+                base = x * pitch
+                rows = slice(base, base + SEAM)
+                choose(rows, *shared((seam_tiles[0], seam_tiles[2])), even)
+                rows = slice(si + base, si + base + SEAM)
+                choose(rows, *ends(seam_tiles[1], 1), even)
+                if x < span_x:
+                    plane = slice(x * span_z, (x + 1) * span_z)
+                    rows = slice(base + SEAM, base + pitch)
+                    choose(rows, *shared((t_ref[plane, :], g_ref[plane, :])), even_block)
+                    plane = slice((span_x + x) * span_z, (span_x + x + 1) * span_z)
+                    rows = slice(si + base + SEAM, si + base + pitch)
+                    choose(rows, *ends(t_ref[plane, :], 1), even_block)
 
         send_a, send_b, seam_rows = kernel_call(
             edge,
-            [shape((3 * si, LANES), BF)] * 2 + [shape((3 * seams, mid), BF)],
+            [shape((2 * si, LANES), BF)] * 2 + [shape((3 * seams, mid), BF)],
             [bounds, block, cot_block] + got_z,
             smem=1,
         )
@@ -410,10 +438,16 @@
             o_ref[at + si : at + 2 * si, :] = high.astype(BF)
             for v, first in enumerate((si, at + 2 * si)):
                 for t in range(tiles):
-                    o_ref[first + t * seams : first + (t + 1) * seams, :] = s_ref[
-                        v * seams : (v + 1) * seams, t * LANES : (t + 1) * LANES
+                    lanes = slice(t * LANES, (t + 1) * LANES)
+                    at = first + t * packs
+                    o_ref[at : at + SEAM, :] = (
+                        s_ref[v * seams : v * seams + SEAM, lanes]
+                        + s_ref[(v + 1) * seams - SEAM : (v + 1) * seams, lanes]
+                    )
+                    o_ref[at + SEAM : at + packs, :] = s_ref[
+                        v * seams + SEAM : (v + 1) * seams - SEAM, lanes
                     ]
-            low, high = both(2)
+            low, high = both(0)
             for x in range(span_x + 1):
                 f_ref[x * pitch : x * pitch + SEAM, :] = s_ref[
                     2 * seams + x * SEAM : 2 * seams + (x + 1) * SEAM, :
@@ -487,10 +521,17 @@
                 put(base, columns, value[:SEAM])
                 put(base + last, columns, value[last:])
             for t in range(tiles):
-                at = first + t * seams
+                at = first + t * packs
                 columns = (begin + LANES * t, begin + LANES * (t + 1))
+                shared = strip_refs[b][at : at + SEAM, :].astype(F32)
+                row = lax.broadcasted_iota(jnp.int32, shared.shape, 0)
                 for x in range(span_x + 1):
-                    value = strip_refs[b][at + x * SEAM : at + (x + 1) * SEAM, :]
+                    if x == 0:
+                        value = jnp.where(row >= SEAM - 4, shared, 0.0).astype(BF)
+                    elif x == span_x:
+                        value = jnp.where(row < 4, shared, 0.0).astype(BF)
+                    else:
+                        value = strip_refs[b][at + x * SEAM : at + (x + 1) * SEAM, :]
                     seam = base + x * pitch
                     if 0 < x < span_x:
                         dest[seam : seam + SEAM, columns[0] : columns[1]] = value
@@ -542,7 +583,7 @@
             mine = jnp.where(own(own_ref, g, base), out[pitch : pitch + si], 0.0)
             return add_up(sums, mine, mine)
 
-        return lax.fori_loop(0, groups, step, (zero(), zero()))
+        return lax.fori_loop(0, groups, step, (zero(), zero()), unroll=True)
 
     def zero():
         return jnp.zeros((1, LANES), F32)
@@ -585,7 +626,7 @@
             column(source, dest, sems, g).wait()
             return carry
 
-        lax.fori_loop(0, outer_groups, wait, 0)
+        lax.fori_loop(0, outer_groups, wait, 0, unroll=True)
 
     def conv_two_of(bound, c_ref, st_in, k, p_ref, h_ref, c2_ref, own_ref, in_ref, band, shifts, after=None):
         groups, base, out_groups, out_base, offset = shifts
@@ -601,7 +642,7 @@
             h_ref[:, at] = h.astype(BF)
             return carry
 
-        lax.fori_loop(0, groups, act, 0)
+        lax.fori_loop(0, groups, act, 0, unroll=True)
         if after is not None:
             after.start()
         band = band.fill(offset)
@@ -612,7 +653,7 @@
             mine = jnp.where(own(own_ref, g, out_base), out, 0.0)
             return add_up(sums, mine, mine)
 
-        return lax.fori_loop(0, out_groups, step, (zero(), zero()))
+        return lax.fori_loop(0, out_groups, step, (zero(), zero()), unroll=True)
 
     def second_conv_b(bound, c_ref, w_ref, st_in, p_ref, more, m_ref, h_out, c2_ref, st_ref, token_ref, h_ref, own_ref, in_ref, band, part, wait, sem):
         band = Band(band, part, wait, w_ref, 1)
@@ -643,16 +684,12 @@
         copy.start()
         fill_own(own_ref)
         mean, rstd = moments(st_in, 0)
-        acc[...] = jnp.zeros(acc.shape, F32)
         copy.wait()
-
-        def step(g, carry):
+        groups = []
+        for g in range(outer_groups):
             xhat = (c_ref[pl.ds(pitch, si), lane_at(g + 1)] - mean) * rstd
-            mine = jnp.where(own(own_ref, g, base_one), xhat, 0.0)
-            tap_products(mine, x_ref, pitch, g + 1, pitch, acc)
-            return carry
-
-        lax.fori_loop(0, outer_groups, step, 0)
+            groups.append(jnp.where(own(own_ref, g, base_one), xhat, 0.0))
+        acc[...] = tap_products(groups, x_ref, pitch, 1, pitch)
         t_ref[...] = jnp.zeros(t_ref.shape, F32)
         fold_taps(acc, t_ref, 0, chan, 2)
 
@@ -698,7 +735,7 @@
             d, xhat = slope_two(c_ref, moment, p_ref, go_ref, lane_at(g))
             return add_up(sums, jnp.where(own(own_ref, g, base_two), d, 0.0), xhat)
 
-        rows = lax.fori_loop(0, outer_groups, step, (zero(), zero()))
+        rows = lax.fori_loop(0, outer_groups, step, (zero(), zero()), unroll=True)
         send(st_ref, rows, t_ref)
 
     def second_delta(bound, c_ref, st_in, p_ref, go_ref, sums_in, after, d_ref, in_ref):
@@ -715,22 +752,19 @@
             d_ref[:, at] = jnp.where(inside(bound, in_ref, g, base_two), out, 0.0).astype(BF)
             return carry
 
-        lax.fori_loop(0, outer_groups, step, 0)
+        lax.fori_loop(0, outer_groups, step, 0, unroll=True)
 
     def second_taps(d_ref, h_far, gw_ref, h_ref, acc, own_ref, sem):
         copy = pltpu.make_async_copy(h_far, h_ref, sem)
         copy.start()
         fill_own(own_ref)
-        acc[...] = jnp.zeros(acc.shape, F32)
         gw_ref[...] = jnp.zeros(gw_ref.shape, F32)
         copy.wait()
-
-        def taps(g, carry):
-            mine = jnp.where(own(own_ref, g, base_two), d_ref[:, lane_at(g)].astype(F32), 0.0)
-            tap_products(mine, h_ref, 0, g, pitch, acc)
-            return carry
-
-        lax.fori_loop(0, outer_groups, taps, 0)
+        groups = [
+            jnp.where(own(own_ref, g, base_two), d_ref[:, lane_at(g)].astype(F32), 0.0)
+            for g in range(outer_groups)
+        ]
+        acc[...] = tap_products(groups, h_ref, 0, 0, pitch)
         fold_taps(acc, gw_ref, 0, chan, 2)
 
     def first_slope(w_ref, c_ref, st_in, p_ref, more, gw_two, x_far, *refs):
@@ -743,9 +777,9 @@
         assemble_delta(pad_ref, frames)
         band = band.fill(0)
         mean, rstd = moments(st_in, 0)
-        acc[...] = jnp.zeros(acc.shape, F32)
         gw_ref[...] = jnp.zeros(gw_ref.shape, F32)
         copy.wait()
+        groups = []
 
         def step(g, sums):
             at = lane_at(g)
@@ -756,10 +790,13 @@
             d1_ref[:, at] = d
             column(d1_ref, d1_out, sems, g).start()
             mine = jnp.where(own(own_ref, g, base_one), d[pitch : pitch + si], 0.0)
-            tap_products(mine, x_ref, pitch, g + 1, pitch, acc)
+            groups.append(mine)
             return add_up(sums, mine, xhat[pitch : pitch + si])
 
-        rows = lax.fori_loop(0, outer_groups, step, (zero(), zero()))
+        rows = (zero(), zero())
+        for g in range(outer_groups):
+            rows = step(g, rows)
+        acc[...] = tap_products(groups, x_ref, pitch, 1, pitch)
         fold_taps(acc, gw_ref, 0, chan, 2)
         send(st_ref, list(rows) + [more[0:1, :], more[1:2, :]], gw_ref, gw_two)
         columns(d1_ref, d1_out, sems)
@@ -783,13 +820,13 @@
             d_ref[:, at] = jnp.where(inside(bound, in_ref, g, base_one), out, 0.0).astype(BF)
             return carry
 
-        lax.fori_loop(0, outer_groups, step, 0)
+        lax.fori_loop(0, outer_groups, step, 0, unroll=True)
 
         def conv(g, carry):
             o_ref[:, lane_at(g)] = band_conv(d_ref, band, g, pi, pitch).astype(BF)
             return carry
 
-        lax.fori_loop(0, inner_groups, conv, 0)
+        lax.fori_loop(0, inner_groups, conv, 0, unroll=True)
         order = order_matrix(chan, span_y, 0, line)
         for x in range(span_x):
             at = SEAM + x * pitch
@@ -841,7 +878,7 @@
             h_ref[:, at] = (z * sigmoid(z)).astype(BF)
             return carry
 
-        lax.fori_loop(0, inner_groups, act, 0)
+        lax.fori_loop(0, inner_groups, act, 0, unroll=True)
         for x in range(span_x):
             at = SEAM + x * pitch
             y_ref[:, x] = native(h_ref[at : at + span_z, :], order)
@@ -867,7 +904,7 @@
     one_copy = pltpu.SemaphoreType.DMA
     mid_scratch = pltpu.VMEM((so, mid), F32)
     group_copies = pltpu.SemaphoreType.DMA((outer_groups,))
-    acc_scratch = pltpu.VMEM((3, 3 * LANES, 2 * LANES), F32)
+    acc_scratch = pltpu.VMEM((3 * LANES, 6 * LANES), F32)
     c1_b, pad_b, pad_a, stats, plain = kernel_call(
         first_conv_b,
         [shape((so, mid_b), F32)] + [shape((sw, wide), BF)] * 2 + [stat_shape(1), token_shape],
@@ -930,6 +967,7 @@
         scratch=[mid_scratch, pltpu.VMEM((so, mid), BF), own_scratch, in_scratch, *band_scratch, one_copy],
         smem=1,
         far=(1, 2),
+        home=(0,),
         work=1 << 32,
     )
     (delta_two,) = kernel_call(

time: 143 us -> 130 us (0.909)
  Pallas kernels: 61.8 us -> 51.1 us
    pallas_call x17, Pallas kernels: 61.8 us -> 51.1 us  [kernel_call(): pl.pallas_call(body, out_shape=out_shape, in_specs=[SM if i < smem else H...]
    all_to_all x4, waiting for transfers between devices: 7.59 us -> 12.2 us  [exchange(): return lax.all_to_all(spread_rows, AXES, 0, 0)]
    ppermute x1, waiting for transfers between devices: 3.32 us -> 0.01 us  [halo(): got_z = [lax.ppermute(tiles_z[0], 'gz', [(0, 1), (1, 0)])]]
    ppermute x1, waiting for transfers between devices: 5.37 us -> 2.6 us  [halo(): lax.ppermute(mine, 'gx', backward_x)]
    ppermute x1, waiting for transfers between devices: 1.87 us -> 3.99 us  [body(): lax.ppermute(delta_two, 'gx', backward_x)]
  transfers between devices with their start and end apart: 13 -> 13, of which waited for: 10 -> 9; matrix products, arithmetic and copies ran while one was open for 0% -> 0% of each run, Pallas kernels for 22% -> 20%
where the time goes in v5:
time: 130 us; the launch traced here: 129 us
  Pallas kernels  51.1 us (39%)
  starting transfers between devices  39.9 us (31%)
  waiting for transfers between devices  21.8 us (17%)
  blocking collectives  15.1 us (12%)
    pallas_call x17, Pallas kernels, kernel_call(): pl.pallas_call(body, out_shape=out_shape, in_specs=[SM if i < smem else H...  51.1 us
    all_to_all x4, starting transfers between devices, exchange(): return lax.all_to_all(spread_rows, AXES, 0, 0)  18.5 us
    all_to_all x1, blocking collectives, exchange(): return lax.all_to_all(spread_rows, AXES, 0, 0)  15.1 us
    all_to_all x4, waiting for transfers between devices, exchange(): return lax.all_to_all(spread_rows, AXES, 0, 0)  12.2 us
    ppermute x1, starting transfers between devices, halo(): from_low = lax.ppermute(block, 'gx', forward_x)  4.58 us
    ppermute x1, starting transfers between devices, body(): lax.ppermute(delta_two, 'gx', forward_x)  4.57 us
    ppermute x1, starting transfers between devices, halo(): lax.ppermute(mine, 'gx', forward_x)  4.56 us
    ppermute x1, waiting for transfers between devices, body(): lax.ppermute(delta_two, 'gx', backward_x)  3.99 us
  transfers between devices with their start and end apart: 13, of which 9 were waited for; matrix products, arithmetic and copies ran while one was open for 0% of the time, Pallas kernels for 20%

profile of v5, /device:TPU:0, one launch (start us, length us, event | category | flops | bytes accessed | tf_op | source)
XLA Modules:
  0.0 128.8 jit_solution(3676438789774581542)
XLA Ops:
  0.7 0.1 stack.39.bound
  0.8 3.1 %shard_map.129 = (bf16[512,512]{1,0:T(8,128)(2,1)S(1)}, bf16[256,640]{1,0:T(8,128)(2,1)S(1)}, bf16[1,96,640]{2,1,0:T(8,128)(2,1)S(1)}) custom-call(s32[9]{0:T(128)S(1)} %stack.39.bound, bf16[32,2,16,128]{3,2,1,0:T(8,128)(2,1)} %a_ref.1, bf16[32,2,16,128]{3,2,1,0:T(8,128)(2,1)} %b_ref.1, bf16[32,2,16,128]{3,2,1,0:T(8,128)(2,1)} %go_ref.1), custom_call_target="tpu_custom_call" | custom-call | bytes 1048576 | tf_op jit(solution)/shard_map/pallas_call | solution.py:31
  3.9 3.1 %collective-permute-start.2 = (bf16[96,640]{1,0:T(8,128)(2,1)S(1)}, bf16[96,640]{1,0:T(8,128)(2,1)S(1)}, u32[]{:S(2)}, u32[]{:S(2)}) collective-permute-start(bf16[96,640]{1,0:T(8,128)(2,1)S(1)} %bitcast.14), channel_id=1, source_target_pairs={{0,1},{1,0},{2,3},{3,2},{4,5},{5,4},{6,7},{7,6},{8,9},{9,8},{10,11... | collective-permute-start | bytes 368648 | tf_op jit(solution)/shard_map/ppermute | solution.py:346
  7.0 1.3 collective-permute-start.1
  8.3 4.6 %collective-permute-start = (bf16[512,512]{1,0:T(8,128)(2,1)S(1)}, bf16[512,512]{1,0:T(8,128)(2,1)S(1)}, u32[]{:S(2)}, u32[]{:S(2)}) collective-permute-start(bf16[512,512]{1,0:T(8,128)(2,1)S(1)} %get-tuple-element.39.t_ref.refs_1_), channel_id=1, source_target_pairs={{0,8},{8,16},{16,24},{1,9},{9,17},{17,25},{2,10},{10,18},{18,26},{... | collective-permute-start | bytes 1572872 | tf_op jit(solution)/shard_map/ppermute | solution.py:352
  12.8 0.0 collective-permute-done.2.refs_0_
  12.9 0.6 shard_map.130
  13.5 0.1 collective-permute-start.3
  13.6 0.7 collective-permute-start.4
  14.2 2.3 %shard_map.128 = (bf16[1152,128]{1,0:T(8,128)(2,1)}, f32[8,128]{1,0:T(8,128)S(1)}) custom-call(bf16[3,3,3,32,32]{4,3,2,1,0:T(8,128)(2,1)} %w1_ref.1, bf16[3,3,3,32,32]{4,3,2,1,0:T(8,128)(2,1)} %w2_ref.1, f32[1,32]{1,0:T(1,128)} %bitcast.15, f32[1,32]{1,0:T(1,128)} %bitcast.16, f32[1,32]{1,0:T(1,128)} %bitcast.17, f32[1,32]{1,0:T(1,128)} %bitcast.18), custom_call_target="tpu_custom_call" | custom-call | flops 2147483648 | bytes 1048576 | tf_op jit(solution)/shard_map/pallas_call | solution.py:31
  16.6 0.0 collective-permute-done.3.a_ref
  16.6 0.0 collective-permute-done.4.b_ref
  16.6 0.7 shard_map.131
  17.3 1.3 %collective-permute-start.6 = (bf16[1168,128]{1,0:T(8,128)(2,1)S(1)}, bf16[1168,128]{1,0:T(8,128)(2,1)S(1)}, u32[]{:S(2)}, u32[]{:S(2)}) collective-permute-start(bf16[1168,128]{1,0:T(8,128)(2,1)S(1)} %get-tuple-element.46.refs_4_), channel_id=1, source_target_pairs={{8,0},{16,8},{24,16},{9,1},{17,9},{25,17},{10,2},{18,10},{26,18},{... | collective-permute-start | bytes 897032 | tf_op jit(solution)/shard_map/ppermute | solution.py:478
  18.6 4.6 %collective-permute-start.5 = (bf16[1168,128]{1,0:T(8,128)(2,1)S(1)}, bf16[1168,128]{1,0:T(8,128)(2,1)S(1)}, u32[]{:S(2)}, u32[]{:S(2)}) collective-permute-start(bf16[1168,128]{1,0:T(8,128)(2,1)S(1)} %get-tuple-element.46.refs_4_), channel_id=1, source_target_pairs={{0,8},{8,16},{16,24},{1,9},{9,17},{17,25},{2,10},{10,18},{18,26},{... | collective-permute-start | bytes 897032 | tf_op jit(solution)/shard_map/ppermute | solution.py:476
  23.2 0.0 collective-permute-done.1.refs_2_
  23.2 0.2 collective-permute-done.refs_0_
  23.4 2.6 %collective-permute-done.6.refs_5_ = bf16[1168,128]{1,0:T(8,128)(2,1)S(1)} collective-permute-done((bf16[1168,128]{1,0:T(8,128)(2,1)S(1)}, bf16[1168,128]{1,0:T(8,128)(2,1)S(1)}, u32[]{:S(2)}, u32[]{:S(2)}) %collective-permute-start.6) | collective-permute-done | bytes 299040 | tf_op jit(solution)/shard_map/ppermute | solution.py:478
  26.0 1.6 %collective-permute-done.5.refs_3_ = bf16[1168,128]{1,0:T(8,128)(2,1)S(1)} collective-permute-done((bf16[1168,128]{1,0:T(8,128)(2,1)S(1)}, bf16[1168,128]{1,0:T(8,128)(2,1)S(1)}, u32[]{:S(2)}, u32[]{:S(2)}) %collective-permute-start.5) | collective-permute-done | bytes 299040 | tf_op jit(solution)/shard_map/ppermute | solution.py:476
  27.6 5.6 %shard_map.132 = (f32[592,768]{1,0:T(8,128)S(1)}, bf16[880,896]{1,0:T(8,128)(2,1)}, bf16[880,896]{1,0:T(8,128)(2,1)}, f32[32,1,128]{2,1,0:T(1,128)}, f32[8,128]{1,0:T(8,128)S(1)}) custom-call(bf16[1152,128]{1,0:T(8,128)(2,1)} %get-tuple-element.38.w_ref, bf16[512,512]{1,0:T(8,128)(2,1)S(1)} %collective-permute-done.refs_0_, ...), custom_call_target="tpu_custom_call" | custom-call | flops 1073741824 | bytes 1048576 | tf_op jit(solution)/shard_map/pallas_call | solution.py:31
  33.2 9.1 %all-to-all-start = ((f32[32,1,128]{2,1,0:T(1,128)}), f32[32,1,128]{2,1,0:T(1,128)S(1)}, u32[]{:S(2)}, u32[]{:S(2)}) async-start(f32[32,1,128]{2,1,0:T(1,128)} %get-tuple-element.51), calls=%async_computation | async-start | bytes 32768 | tf_op jit(solution)/shard_map/all_to_all | solution.py:47
  42.4 5.1 %shard_map.133 = (f32[592,640]{1,0:T(8,128)}, f32[8,128]{1,0:T(8,128)S(1)}) custom-call(bf16[1152,128]{1,0:T(8,128)(2,1)} %get-tuple-element.38.w_ref, f32[8,128]{1,0:T(8,128)S(1)} %get-tuple-element.47.after.m_ref, bf16[880,896]{1,0:T(8,128)(2,1)} %get-tuple-element.48.x_far), custom_call_target="tpu_custom_call" | custom-call | flops 4294967296 | bytes 1048576 | tf_op jit(solution)/shard_map/pallas_call | solution.py:31
  47.5 2.0 %all-to-all-done.st_in = f32[32,1,128]{2,1,0:T(1,128)S(1)} async-done(((f32[32,1,128]{2,1,0:T(1,128)}), f32[32,1,128]{2,1,0:T(1,128)S(1)}, u32[]{:S(2)}, u32[]{:S(2)}) %all-to-all-start) | async-done | bytes 16416 | tf_op jit(solution)/shard_map/all_to_all | solution.py:47
  49.5 4.5 %shard_map.134 = (bf16[592,768]{1,0:T(8,128)(2,1)}, f32[304,640]{1,0:T(8,128)S(1)}, f32[32,3,128]{2,1,0:T(4,128)}, f32[8,128]{1,0:T(8,128)S(1)}) custom-call(s32[9]{0:T(128)S(1)} %stack.39.bound, f32[592,768]{1,0:T(8,128)S(1)} %get-tuple-element.50.c_ref, bf16[1152,128]{1,0:T(8,128)(2,1)} %get-tuple-element.38.w_ref, f32[32,1,128]{2,1,0:T(1,128)S(1)} %all-to-all-done.st_in, ...), custom_call_target="tpu_custom_call" | custom-call | flops 1073741824 | bytes 1048576 | tf_op jit(solution)/shard_map/pallas_call | solution.py:31
  54.1 4.0 %all-to-all-start.1 = ((f32[32,3,128]{2,1,0:T(4,128)}), f32[32,3,128]{2,1,0:T(4,128)S(1)}, u32[]{:S(2)}, u32[]{:S(2)}) async-start(f32[32,3,128]{2,1,0:T(4,128)} %get-tuple-element.53), calls=%async_computation.1 | async-start | bytes 131072 | tf_op jit(solution)/shard_map/all_to_all | solution.py:47
  58.1 2.8 %shard_map.135.t_ref = f32[224,128]{1,0:T(8,128)S(1)} custom-call(f32[592,768]{1,0:T(8,128)S(1)} %get-tuple-element.50.c_ref, f32[32,1,128]{2,1,0:T(1,128)S(1)} %all-to-all-done.st_in, bf16[880,896]{1,0:T(8,128)(2,1)} %get-tuple-element.56.x_far, f32[8,128]{1,0:T(8,128)S(1)} %get-tuple-element.57.after), custom_call_target="tpu_custom_call" | custom-call | flops 4294967296 | bytes 1048576 | tf_op jit(solution)/shard_map/pallas_call | solution.py:31
  60.9 4.7 %all-to-all-done.1.st_in.plain_ref = f32[32,3,128]{2,1,0:T(4,128)S(1)} async-done(((f32[32,3,128]{2,1,0:T(4,128)}), f32[32,3,128]{2,1,0:T(4,128)S(1)}, u32[]{:S(2)}, u32[]{:S(2)}) %all-to-all-start.1) | async-done | bytes 49184 | tf_op jit(solution)/shard_map/all_to_all | solution.py:47
  65.5 1.5 %shard_map.136 = (f32[32,8,128]{2,1,0:T(8,128)}, f32[8,128]{1,0:T(8,128)S(1)}) custom-call(f32[304,640]{1,0:T(8,128)S(1)} %get-tuple-element.54.c_ref, f32[32,3,128]{2,1,0:T(4,128)S(1)} %all-to-all-done.1.st_in.plain_ref, f32[8,128]{1,0:T(8,128)S(1)} %get-tuple-element.45.token_ref.p_ref, bf16[304,640]{1,0:T(8,128)(2,1)S(1)} %get-tuple-element.55.go_ref, ...), custom_call_target="tpu_custom_call" | custom-call | flops 134217728 | bytes 1048576 | tf_op jit(solution)/shard_map/pallas_call | solution.py:31
  67.0 2.6 %all-to-all-start.2 = ((f32[32,8,128]{2,1,0:T(8,128)}), f32[32,8,128]{2,1,0:T(8,128)S(1)}, u32[]{:S(2)}, u32[]{:S(2)}) async-start(f32[32,8,128]{2,1,0:T(8,128)} %get-tuple-element.61), calls=%async_computation.2 | async-start | bytes 262144 | tf_op jit(solution)/shard_map/all_to_all | solution.py:47
  69.6 5.6 %shard_map.137 = (f32[304,512]{1,0:T(8,128)}, f32[8,128]{1,0:T(8,128)S(1)}) custom-call(s32[9]{0:T(128)S(1)} %stack.39.bound, f32[592,640]{1,0:T(8,128)} %get-tuple-element.49.c_far, bf16[1152,128]{1,0:T(8,128)(2,1)} %get-tuple-element.38.w_ref, f32[32,3,128]{2,1,0:T(4,128)S(1)} %all-to-all-done.1.st_in.plain_ref, ...), custom_call_target="tpu_custom_call" | custom-call | flops 4294967296 | bytes 1048576 | tf_op jit(solution)/shard_map/pallas_call | solution.py:31
  75.2 3.0 %all-to-all-done.2.sums_in.early_ref.st_two = f32[32,8,128]{2,1,0:T(8,128)S(1)} async-done(((f32[32,8,128]{2,1,0:T(8,128)}), f32[32,8,128]{2,1,0:T(8,128)S(1)}, u32[]{:S(2)}, u32[]{:S(2)}) %all-to-all-start.2) | async-done | bytes 131104 | tf_op jit(solution)/shard_map/all_to_all | solution.py:47
  78.2 1.4 %shard_map.138.d_ref.refs_1_ = bf16[304,640]{1,0:T(8,128)(2,1)S(1)} custom-call(s32[9]{0:T(128)S(1)} %stack.39.bound, f32[304,640]{1,0:T(8,128)S(1)} %get-tuple-element.54.c_ref, f32[32,3,128]{2,1,0:T(4,128)S(1)} %all-to-all-done.1.st_in.plain_ref, f32[8,128]{1,0:T(8,128)S(1)} %get-tuple-element.45.token_ref.p_ref, ...), custom_call_target="tpu_custom_call" | custom-call | flops 134217728 | bytes 1048576 | tf_op jit(solution)/shard_map/pallas_call | solution.py:31
  79.6 1.3 %collective-permute-start.8 = (bf16[304,640]{1,0:T(8,128)(2,1)S(1)}, bf16[304,640]{1,0:T(8,128)(2,1)S(1)}, u32[]{:S(2)}, u32[]{:S(2)}) collective-permute-start(bf16[304,640]{1,0:T(8,128)(2,1)S(1)} %shard_map.138.d_ref.refs_1_), channel_id=1, source_target_pairs={{8,0},{16,8},{24,16},{9,1},{17,9},{25,17},{10,2},{18,10},{26,18},{... | collective-permute-start | bytes 1167368 | tf_op jit(solution)/shard_map/ppermute | solution.py:993
  80.9 4.6 %collective-permute-start.7 = (bf16[304,640]{1,0:T(8,128)(2,1)S(1)}, bf16[304,640]{1,0:T(8,128)(2,1)S(1)}, u32[]{:S(2)}, u32[]{:S(2)}) collective-permute-start(bf16[304,640]{1,0:T(8,128)(2,1)S(1)} %shard_map.138.d_ref.refs_1_), channel_id=1, source_target_pairs={{0,8},{8,16},{16,24},{1,9},{9,17},{17,25},{2,10},{10,18},{18,26},{... | collective-permute-start | bytes 1167368 | tf_op jit(solution)/shard_map/ppermute | solution.py:991
  85.5 2.5 %shard_map.139.gw_two = f32[224,128]{1,0:T(8,128)S(1)} custom-call(bf16[304,640]{1,0:T(8,128)(2,1)S(1)} %shard_map.138.d_ref.refs_1_, bf16[592,768]{1,0:T(8,128)(2,1)} %get-tuple-element.62.h_far), custom_call_target="tpu_custom_call" | custom-call | flops 4294967296 | bytes 1048576 | tf_op jit(solution)/shard_map/pallas_call | solution.py:31
  88.0 4.0 %collective-permute-done.8.refs_2_ = bf16[304,640]{1,0:T(8,128)(2,1)S(1)} collective-permute-done((bf16[304,640]{1,0:T(8,128)(2,1)S(1)}, bf16[304,640]{1,0:T(8,128)(2,1)S(1)}, u32[]{:S(2)}, u32[]{:S(2)}) %collective-permute-start.8) | collective-permute-done | bytes 389152 | tf_op jit(solution)/shard_map/ppermute | solution.py:993
  92.0 1.2 collective-permute-done.7.refs_0_
  93.2 6.8 %shard_map.140 = (f32[592,640]{1,0:T(8,128)}, f32[32,15,128]{2,1,0:T(8,128)}) custom-call(bf16[1152,128]{1,0:T(8,128)(2,1)} %get-tuple-element.38.w_ref, f32[592,768]{1,0:T(8,128)S(1)} %get-tuple-element.50.c_ref, f32[32,1,128]{2,1,0:T(1,128)S(1)} %all-to-all-done.st_in, f32[8,128]{1,0:T(8,128)S(1)} %get-tuple-element.45.token_ref.p_ref, ...), custom_call_target="tpu_custom_call" | custom-call | flops 1073741824 | bytes 1048576 | tf_op jit(solution)/shard_map/pallas_call | solution.py:31
  100.1 15.1 %all_to_all.25.late_ref.st_in.sums_in = f32[32,15,128]{2,1,0:T(8,128)S(1)} all-to-all(f32[32,15,128]{2,1,0:T(8,128)} %get-tuple-element.63), channel_id=1, replica_groups=mesh['gx'=4,'gy'=4,'gz'=2] {'gx','gy','gz'}, dimensions={0} | all-to-all | bytes 491520 | tf_op jit(solution)/shard_map/all_to_all | solution.py:47
  115.1 1.5 %shard_map.141 = (bf16[32,16,128]{2,1,0:T(8,128)(2,1)}, f32[8,128]{1,0:T(8,128)S(1)}) custom-call(s32[9]{0:T(128)S(1)} %stack.39.bound, f32[32,1,128]{2,1,0:T(1,128)S(1)} %all-to-all-done.st_in, f32[8,128]{1,0:T(8,128)S(1)} %get-tuple-element.45.token_ref.p_ref, f32[32,3,128]{2,1,0:T(4,128)S(1)} %all-to-all-done.1.st_in.plain_ref, ...), custom_call_target="tpu_custom_call" | custom-call | bytes 1048576 | tf_op jit(solution)/shard_map/pallas_call | solution.py:31
  116.6 2.8 %all-to-all-start.4 = ((bf16[32,16,128]{2,1,0:T(8,128)(2,1)}), bf16[32,16,128]{2,1,0:T(8,128)(2,1)S(1)}, u32[]{:S(2)}, u32[]{:S(2)}) async-start(bf16[32,16,128]{2,1,0:T(8,128)(2,1)} %get-tuple-element.67), calls=%async_computation.4 | async-start | bytes 262144 | tf_op jit(solution)/shard_map/all_to_all | solution.py:47
  119.4 0.0 copy-start
  119.4 4.4 %shard_map.143 = bf16[32,2,16,128]{3,2,1,0:T(8,128)(2,1)} custom-call(s32[9]{0:T(128)S(1)} %stack.39.bound, f32[592,640]{1,0:T(8,128)} %get-tuple-element.66.s_far, f32[592,768]{1,0:T(8,128)S(1)} %get-tuple-element.50.c_ref, f32[32,1,128]{2,1,0:T(1,128)S(1)} %all-to-all-done.st_in, f32[8,128]{1,0:T(8,128)S(1)} %get-tuple-element.45.token_ref.p_ref, ...), custom_call_target="tpu_custom_call" | custom-call | flops 2147483648 | bytes 1048576 | tf_op jit(solution)/shard_map/pallas_call | solution.py:31
  123.8 0.0 copy-done
  123.8 1.5 %shard_map.142 = (bf16[32,2,16,128]{3,2,1,0:T(8,128)(2,1)}, f32[4,32]{1,0:T(4,128)}) custom-call(f32[304,512]{1,0:T(8,128)S(1)} %copy-done, f32[32,15,128]{2,1,0:T(8,128)S(1)} %all_to_all.25.late_ref.st_in.sums_in, f32[32,8,128]{2,1,0:T(8,128)S(1)} %all-to-all-done.2.sums_in.early_ref.st_two, f32[8,128]{1,0:T(8,128)S(1)} %get-tuple-element.45.token_ref.p_ref, ...), custom_call_target="tpu_custom_call" | custom-call | flops 2147483648 | bytes 1048576 | tf_op jit(solution)/shard_map/pallas_call | solution.py:31
  125.3 2.5 %all-to-all-done.4.got_ref = bf16[32,16,128]{2,1,0:T(8,128)(2,1)S(1)} async-done(((bf16[32,16,128]{2,1,0:T(8,128)(2,1)}), bf16[32,16,128]{2,1,0:T(8,128)(2,1)S(1)}, u32[]{:S(2)}, u32[]{:S(2)}) %all-to-all-start.4) | async-done | bytes 131104 | tf_op jit(solution)/shard_map/all_to_all | solution.py:47
  127.8 1.1 shard_map.144
Async XLA Ops:
  3.9 8.9 %collective-permute-start.2 = (bf16[96,640]{1,0:T(8,128)(2,1)S(1)}, bf16[96,640]{1,0:T(8,128)(2,1)S(1)}, u32[]{:S(2)}, u32[]{:S(2)}) collective-permute-start(bf16[96,640]{1,0:T(8,128)(2,1)S(1)} %bitcast.14), channel_id=1, source_target_pairs={{0,1},{1,0},{2,3},{3,2},{4,5},{5,4},{6,7},{7,6},{8,9},{9,8},{10,11... | collective-permute-start | bytes 368648 | tf_op jit(solution)/shard_map/ppermute | solution.py:346
  7.0 16.3 %collective-permute-start.1 = (bf16[512,512]{1,0:T(8,128)(2,1)S(1)}, bf16[512,512]{1,0:T(8,128)(2,1)S(1)}, u32[]{:S(2)}, u32[]{:S(2)}) collective-permute-start(bf16[512,512]{1,0:T(8,128)(2,1)S(1)} %get-tuple-element.39.t_ref.refs_1_), channel_id=1, source_target_pairs={{8,0},{16,8},{24,16},{9,1},{17,9},{25,17},{10,2},{18,10},{26,18},{... | collective-permute-start | bytes 1572872 | tf_op jit(solution)/shard_map/ppermute | solution.py:353
  8.3 15.2 %collective-permute-start = (bf16[512,512]{1,0:T(8,128)(2,1)S(1)}, bf16[512,512]{1,0:T(8,128)(2,1)S(1)}, u32[]{:S(2)}, u32[]{:S(2)}) collective-permute-start(bf16[512,512]{1,0:T(8,128)(2,1)S(1)} %get-tuple-element.39.t_ref.refs_1_), channel_id=1, source_target_pairs={{0,8},{8,16},{16,24},{1,9},{9,17},{17,25},{2,10},{10,18},{18,26},{... | collective-permute-start | bytes 1572872 | tf_op jit(solution)/shard_map/ppermute | solution.py:352
  13.5 3.1 %collective-permute-start.3 = (bf16[608,128]{1,0:T(8,128)(2,1)S(1)}, bf16[608,128]{1,0:T(8,128)(2,1)S(1)}, u32[]{:S(2)}, u32[]{:S(2)}) collective-permute-start(bf16[608,128]{1,0:T(8,128)(2,1)S(1)} %get-tuple-element.42), channel_id=1, source_target_pairs={{0,2},{2,0},{4,6},{6,4},{1,3},{3,1},{5,7},{7,5},{8,10},{10,8},{12,... | collective-permute-start | bytes 466952 | tf_op jit(solution)/shard_map/ppermute | solution.py:420
  13.6 3.0 %collective-permute-start.4 = (bf16[608,128]{1,0:T(8,128)(2,1)S(1)}, bf16[608,128]{1,0:T(8,128)(2,1)S(1)}, u32[]{:S(2)}, u32[]{:S(2)}) collective-permute-start(bf16[608,128]{1,0:T(8,128)(2,1)S(1)} %get-tuple-element.43), channel_id=1, source_target_pairs={{2,4},{4,2},{3,5},{5,3},{10,12},{12,10},{11,13},{13,11},{18,20},{2... | collective-permute-start | bytes 466952 | tf_op jit(solution)/shard_map/ppermute | solution.py:421
  17.3 8.7 %collective-permute-start.6 = (bf16[1168,128]{1,0:T(8,128)(2,1)S(1)}, bf16[1168,128]{1,0:T(8,128)(2,1)S(1)}, u32[]{:S(2)}, u32[]{:S(2)}) collective-permute-start(bf16[1168,128]{1,0:T(8,128)(2,1)S(1)} %get-tuple-element.46.refs_4_), channel_id=1, source_target_pairs={{8,0},{16,8},{24,16},{9,1},{17,9},{25,17},{10,2},{18,10},{26,18},{... | collective-permute-start | bytes 897032 | tf_op jit(solution)/shard_map/ppermute | solution.py:478
  18.6 9.0 %collective-permute-start.5 = (bf16[1168,128]{1,0:T(8,128)(2,1)S(1)}, bf16[1168,128]{1,0:T(8,128)(2,1)S(1)}, u32[]{:S(2)}, u32[]{:S(2)}) collective-permute-start(bf16[1168,128]{1,0:T(8,128)(2,1)S(1)} %get-tuple-element.46.refs_4_), channel_id=1, source_target_pairs={{0,8},{8,16},{16,24},{1,9},{9,17},{17,25},{2,10},{10,18},{18,26},{... | collective-permute-start | bytes 897032 | tf_op jit(solution)/shard_map/ppermute | solution.py:476
  33.2 16.3 %all-to-all-start = ((f32[32,1,128]{2,1,0:T(1,128)}), f32[32,1,128]{2,1,0:T(1,128)S(1)}, u32[]{:S(2)}, u32[]{:S(2)}) async-start(f32[32,1,128]{2,1,0:T(1,128)} %get-tuple-element.51), calls=%async_computation | async-start | bytes 32768 | tf_op jit(solution)/shard_map/all_to_all | solution.py:47
  54.1 11.4 %all-to-all-start.1 = ((f32[32,3,128]{2,1,0:T(4,128)}), f32[32,3,128]{2,1,0:T(4,128)S(1)}, u32[]{:S(2)}, u32[]{:S(2)}) async-start(f32[32,3,128]{2,1,0:T(4,128)} %get-tuple-element.53), calls=%async_computation.1 | async-start | bytes 131072 | tf_op jit(solution)/shard_map/all_to_all | solution.py:47
  67.0 11.2 %all-to-all-start.2 = ((f32[32,8,128]{2,1,0:T(8,128)}), f32[32,8,128]{2,1,0:T(8,128)S(1)}, u32[]{:S(2)}, u32[]{:S(2)}) async-start(f32[32,8,128]{2,1,0:T(8,128)} %get-tuple-element.61), calls=%async_computation.2 | async-start | bytes 262144 | tf_op jit(solution)/shard_map/all_to_all | solution.py:47
  79.6 12.4 %collective-permute-start.8 = (bf16[304,640]{1,0:T(8,128)(2,1)S(1)}, bf16[304,640]{1,0:T(8,128)(2,1)S(1)}, u32[]{:S(2)}, u32[]{:S(2)}) collective-permute-start(bf16[304,640]{1,0:T(8,128)(2,1)S(1)} %shard_map.138.d_ref.refs_1_), channel_id=1, source_target_pairs={{8,0},{16,8},{24,16},{9,1},{17,9},{25,17},{10,2},{18,10},{26,18},{... | collective-permute-start | bytes 1167368 | tf_op jit(solution)/shard_map/ppermute | solution.py:993
  80.9 12.3 %collective-permute-start.7 = (bf16[304,640]{1,0:T(8,128)(2,1)S(1)}, bf16[304,640]{1,0:T(8,128)(2,1)S(1)}, u32[]{:S(2)}, u32[]{:S(2)}) collective-permute-start(bf16[304,640]{1,0:T(8,128)(2,1)S(1)} %shard_map.138.d_ref.refs_1_), channel_id=1, source_target_pairs={{0,8},{8,16},{16,24},{1,9},{9,17},{17,25},{2,10},{10,18},{18,26},{... | collective-permute-start | bytes 1167368 | tf_op jit(solution)/shard_map/ppermute | solution.py:991
  116.6 11.2 %all-to-all-start.4 = ((bf16[32,16,128]{2,1,0:T(8,128)(2,1)}), bf16[32,16,128]{2,1,0:T(8,128)(2,1)S(1)}, u32[]{:S(2)}, u32[]{:S(2)}) async-start(bf16[32,16,128]{2,1,0:T(8,128)(2,1)} %get-tuple-element.67), calls=%async_computation.4 | async-start | bytes 262144 | tf_op jit(solution)/shard_map/all_to_all | solution.py:47
  119.4 4.4 %copy-start = (f32[304,512]{1,0:T(8,128)S(1)}, f32[304,512]{1,0:T(8,128)}, u32[]{:S(2)}) copy-start(f32[304,512]{1,0:T(8,128)} %get-tuple-element.59.c_ref) | copy-start | bytes 1867780

commit v6 on v5

--- a/solution.py
+++ b/solution.py
@@ -193,25 +193,36 @@
 
 
     def fill_inside(bound, ref, planes):
-        row = lax.broadcasted_iota(jnp.int32, ref.shape, 0) + (pitch - SEAM + 4)
-        plane = row // pitch - 1
-        z = row % pitch - 4
-        ok = (plane >= planes[0]) & (plane < planes[1]) & (z >= bound[4]) & (z < bound[5])
-        ref[...] = ok.astype(F32)
+        row = lax.broadcasted_iota(jnp.int32, (pitch, LANES), 0)
+        near = ((row >= SEAM - 4) & (row >= bound[4] + SEAM)).astype(F32)
+        far = ((row < SEAM - 4) & (row < bound[5] - span_z)).astype(F32)
+        count = ref.shape[0] // pitch
+
+        def valid(p):
+            if p < 0 or p >= count:
+                return jnp.float32(0.0)
+            return jnp.where((p >= planes[0]) & (p < planes[1]), 1.0, 0.0).astype(F32)
+
+        for p in range(count):
+            ref[p * pitch : (p + 1) * pitch, :] = near * valid(p) + far * valid(p - 1)
+        ref[count * pitch :, :] = far[:SEAM] * valid(count - 1)
+
+    def rows_of(group, base):
+        return (lax.broadcasted_iota(jnp.int32, (1, LANES), 1) + group * LANES) // chan + base
 
     def inside(bound, ref, group, base):
-        lane = lax.broadcasted_iota(jnp.int32, ref.shape, 1) + group * LANES
-        y = lane // chan + base
-        return (ref[...] > 0.5) & (y >= bound[2]) & (y < bound[3])
+        y = rows_of(group, base)
+        return ref[...] * ((y >= bound[2]) & (y < bound[3])).astype(F32) > 0.5
 
     def fill_own(ref):
-        row = lax.broadcasted_iota(jnp.int32, (si, LANES), 0)
-        ref[...] = ((row >= SEAM) & ((row - SEAM + pitch) % pitch < span_z)).astype(F32)
+        ref[...] = jnp.zeros(ref.shape, F32)
+        for x in range(span_x):
+            at = SEAM + x * pitch
+            ref[at : at + span_z, :] = jnp.ones((span_z, LANES), F32)
 
     def own(ref, group, base):
-        lane = lax.broadcasted_iota(jnp.int32, (si, LANES), 1) + group * LANES
-        y = lane // chan + base
-        return (ref[...] > 0.5) & (y >= 0) & (y < span_y)
+        y = rows_of(group, base)
+        return ref[...] * ((y >= 0) & (y < span_y)).astype(F32) > 0.5
 
     own_scratch = pltpu.VMEM((si, LANES), F32)
     in_scratch = pltpu.VMEM((so, LANES), F32)
@@ -290,9 +301,9 @@
     )
 
 
-    def turned(block, order):
+    def turned(planes, order):
         return lax.dot_general(
-            block.reshape(chan * span_y, span_z),
+            jnp.concatenate([p.reshape(chan * span_y, span_z) for p in planes], axis=1),
             order,
             (((0,), (0,)), ((), ())),
             preferred_element_type=F32,
@@ -314,13 +325,16 @@
         order = order_matrix(chan, span_y, 0, line)
         moved = order_matrix(chan, span_y, 2 * chan, mid)
         z_ref[...] = jnp.zeros(z_ref.shape, BF)
-        for v in range(3):
-            dest, lanes = (t_ref, line) if v < 2 else (g_ref, mid)
-            for x in range(span_x):
-                at = v * span_x + x
+        for planes, dest, matrix in (
+            (range(2 * span_x), t_ref, order),
+            (range(2 * span_x, 3 * span_x), g_ref, moved),
+        ):
+            for at in planes:
+                copies[at].wait()
+            dest[...] = turned([buf[at] for at in planes], matrix)
+            lanes = dest.shape[1]
+            for at in planes:
                 row = (at % (2 * span_x)) * span_z
-                copies[at].wait()
-                dest[row : row + span_z, :] = turned(buf[at], order if v < 2 else moved)
                 first = dest[row : row + SEAM, :]
                 last = dest[row + span_z - SEAM : row + span_z, :]
                 rows = slice(at * SEAM, (at + 1) * SEAM)
@@ -539,16 +553,38 @@
                         put(seam, columns, value)
         finish()
 
-    def assemble_delta(dest, frames):
-        put, finish = joiner(dest)
-        dest[:, mid:] = jnp.zeros((sw, LANES), BF)
-        last = si - SEAM
-        for b in range(3):
-            base = b * span_x * pitch
-            dest[base + SEAM : base + last, :mid] = frames[b][SEAM:last, :]
-            put(base, (0, mid), frames[b][:SEAM, :])
-            put(base + last, (0, mid), frames[b][last:, :])
-        finish()
+    def below(frame, band, group):
+        now, later = windows(frame, group)
+        zeros = jnp.zeros((si - (later.shape[0] - pitch), 2 * LANES), BF)
+        lhs = jnp.concatenate([now, jnp.concatenate([later[pitch:], zeros], axis=0)], axis=1)
+        return spread_dz(jnp.dot(lhs, band[0 : 4 * LANES, :], preferred_element_type=F32))
+
+    def above(frame, band, group):
+        now, later = windows(frame, group)
+        zeros = jnp.zeros((pitch, 2 * LANES), BF)
+        lhs = jnp.concatenate([jnp.concatenate([zeros, later[: si - pitch]], axis=0), now], axis=1)
+        return spread_dz(jnp.dot(lhs, band[2 * LANES :, :], preferred_element_type=F32))
+
+    def windows(frame, group):
+        value = frame[:, lane_at(group)]
+        if (group + 1) * LANES < mid:
+            more = frame[:, lane_at(group + 1)]
+        else:
+            more = jnp.zeros(value.shape, BF)
+        value = jnp.concatenate([value, more], axis=1)
+        return value, value
+
+    def spread_dz(out):
+        size = out.shape[0]
+        return (
+            pltpu.roll(out[:, :LANES], 1, 0)
+            + out[:, LANES : 2 * LANES]
+            + pltpu.roll(out[:, 2 * LANES :], size - 1, 0)
+        )
+
+    def halves(first, second):
+        cut = si - SEAM // 2
+        return jnp.concatenate([first[:cut], second[SEAM // 2 :]], axis=0)
 
 
     def stat_shape(rows):
@@ -767,14 +803,18 @@
         acc[...] = tap_products(groups, h_ref, 0, 0, pitch)
         fold_taps(acc, gw_ref, 0, chan, 2)
 
-    def first_slope(w_ref, c_ref, st_in, p_ref, more, gw_two, x_far, *refs):
-        frames, rest = refs[:3], refs[3:]
-        d1_out, st_ref, pad_ref, own_ref, *band, x_ref, acc, gw_ref, d1_ref, sem, sems = rest
+    def own_upstream(w_ref, d_ref, after, e_ref, band, part, wait):
+        del after
+        band = Band(band, part, wait, w_ref, 2).fill(0)
+        for g in range(outer_groups):
+            e_ref[:, lane_at(g)] = halves(above(d_ref, band, g), below(d_ref, band, g))
+
+    def first_slope(w_ref, c_ref, st_in, p_ref, more, gw_two, x_far, low_ref, high_ref, e_ref, *rest):
+        d1_out, st_ref, own_ref, *band, x_ref, acc, gw_ref, d1_ref, sem, sems = rest
         band = Band(*band, w_ref, 2)
         copy = pltpu.make_async_copy(x_far, x_ref, sem)
         copy.start()
         fill_own(own_ref)
-        assemble_delta(pad_ref, frames)
         band = band.fill(0)
         mean, rstd = moments(st_in, 0)
         gw_ref[...] = jnp.zeros(gw_ref.shape, F32)
@@ -786,7 +826,8 @@
             xhat = (c_ref[:, lane_at(g + 1)] - mean) * rstd
             z = p_ref[0:1, :] * xhat + p_ref[1:2, :]
             s = sigmoid(z)
-            d = band_conv(pad_ref, band, g, po, pitch) * (s * (1.0 + z * (1.0 - s)))
+            e = e_ref[:, at] + halves(below(low_ref, band, g), above(high_ref, band, g))
+            d = e * (s * (1.0 + z * (1.0 - s)))
             d1_ref[:, at] = d
             column(d1_ref, d1_out, sems, g).start()
             mine = jnp.where(own(own_ref, g, base_one), d[pitch : pitch + si], 0.0)
@@ -989,15 +1030,21 @@
     forward_x, backward_x = neighbours("gx")
     frames = [
         lax.ppermute(delta_two, "gx", forward_x),
-        delta_two,
         lax.ppermute(delta_two, "gx", backward_x),
     ]
+    (upstream,) = kernel_call(
+        own_upstream,
+        [shape((so, mid), F32)],
+        [weights, delta_two, taps_two],
+        scratch=list(band_scratch),
+        far=(0,),
+        work=1 << 32,
+    )
     slope, stats = kernel_call(
         first_slope,
         [shape((so, mid), F32), stat_shape(1 + 2 * hold)],
-        [weights, c1_b, stats_one, params, local_a, taps_two, pad_b] + frames,
+        [weights, c1_b, stats_one, params, local_a, taps_two, pad_b] + frames + [upstream],
         scratch=[
-            pltpu.VMEM((sw, mid + LANES), BF),
             own_scratch,
             *band_scratch,
             wide_scratch,

time: 130 us -> 127 us (0.977)
  waiting for transfers between devices: 21.8 us -> 19.4 us
    ppermute x1, waiting for transfers between devices: 3.99 us -> 0.97 us  [body(): lax.ppermute(delta_two, 'gx', backward_x)]
    pallas_call x17 -> x18, Pallas kernels: 51.1 us -> 51 us  [kernel_call(): pl.pallas_call(body, out_shape=out_shape, in_specs=[SM if i < smem else H...]
  transfers between devices with their start and end apart: 13 -> 13, of which waited for: 9 -> 9; matrix products, arithmetic and copies ran while one was open for 0% -> 0% of each run, Pallas kernels for 20% -> 22%
where the time goes in v6:
time: 127 us; the launch traced here: 126 us
  Pallas kernels  51 us (40%)
  starting transfers between devices  39.6 us (31%)
  waiting for transfers between devices  19.4 us (15%)
  blocking collectives  14.8 us (12%)
    pallas_call x18, Pallas kernels, kernel_call(): pl.pallas_call(body, out_shape=out_shape, in_specs=[SM if i < smem else H...  51 us
    all_to_all x4, starting transfers between devices, exchange(): return lax.all_to_all(spread_rows, AXES, 0, 0)  18.2 us
    all_to_all x1, blocking collectives, exchange(): return lax.all_to_all(spread_rows, AXES, 0, 0)  14.8 us
    all_to_all x4, waiting for transfers between devices, exchange(): return lax.all_to_all(spread_rows, AXES, 0, 0)  12.8 us
    ppermute x1, starting transfers between devices, halo(): from_low = lax.ppermute(block, 'gx', forward_x)  4.58 us
    ppermute x1, starting transfers between devices, body(): lax.ppermute(delta_two, 'gx', forward_x)  4.57 us
    ppermute x1, starting transfers between devices, halo(): lax.ppermute(mine, 'gx', forward_x)  4.56 us
    ppermute x1, starting transfers between devices, halo(): got_z = [lax.ppermute(tiles_z[0], 'gz', [(0, 1), (1, 0)])]  3.07 us
  transfers between devices with their start and end apart: 13, of which 9 were waited for; matrix products, arithmetic and copies ran while one was open for 0% of the time, Pallas kernels for 22%

profile of v6, /device:TPU:0, one launch (start us, length us, event | category | flops | bytes accessed | tf_op | source)
XLA Modules:
  0.0 125.7 jit_solution(14656936047037409165)
XLA Ops:
  0.7 0.1 stack.39.bound
  0.8 2.6 %shard_map.129 = (bf16[512,512]{1,0:T(8,128)(2,1)S(1)}, bf16[256,640]{1,0:T(8,128)(2,1)S(1)}, bf16[1,96,640]{2,1,0:T(8,128)(2,1)S(1)}) custom-call(s32[9]{0:T(128)S(1)} %stack.39.bound, bf16[32,2,16,128]{3,2,1,0:T(8,128)(2,1)} %a_ref.1, bf16[32,2,16,128]{3,2,1,0:T(8,128)(2,1)} %b_ref.1, bf16[32,2,16,128]{3,2,1,0:T(8,128)(2,1)} %go_ref.1), custom_call_target="tpu_custom_call" | custom-call | bytes 1048576 | tf_op jit(solution)/shard_map/pallas_call | solution.py:31
  3.3 3.1 %collective-permute-start.2 = (bf16[96,640]{1,0:T(8,128)(2,1)S(1)}, bf16[96,640]{1,0:T(8,128)(2,1)S(1)}, u32[]{:S(2)}, u32[]{:S(2)}) collective-permute-start(bf16[96,640]{1,0:T(8,128)(2,1)S(1)} %bitcast.14), channel_id=1, source_target_pairs={{0,1},{1,0},{2,3},{3,2},{4,5},{5,4},{6,7},{7,6},{8,9},{9,8},{10,11... | collective-permute-start | bytes 368648 | tf_op jit(solution)/shard_map/ppermute | solution.py:360
  6.4 1.3 %collective-permute-start.1 = (bf16[512,512]{1,0:T(8,128)(2,1)S(1)}, bf16[512,512]{1,0:T(8,128)(2,1)S(1)}, u32[]{:S(2)}, u32[]{:S(2)}) collective-permute-start(bf16[512,512]{1,0:T(8,128)(2,1)S(1)} %get-tuple-element.39.t_ref.refs_1_), channel_id=1, source_target_pairs={{8,0},{16,8},{24,16},{9,1},{17,9},{25,17},{10,2},{18,10},{26,18},{... | collective-permute-start | bytes 1572872 | tf_op jit(solution)/shard_map/ppermute | solution.py:367
  7.7 4.6 %collective-permute-start = (bf16[512,512]{1,0:T(8,128)(2,1)S(1)}, bf16[512,512]{1,0:T(8,128)(2,1)S(1)}, u32[]{:S(2)}, u32[]{:S(2)}) collective-permute-start(bf16[512,512]{1,0:T(8,128)(2,1)S(1)} %get-tuple-element.39.t_ref.refs_1_), channel_id=1, source_target_pairs={{0,8},{8,16},{16,24},{1,9},{9,17},{17,25},{2,10},{10,18},{18,26},{... | collective-permute-start | bytes 1572872 | tf_op jit(solution)/shard_map/ppermute | solution.py:366
  12.3 0.0 collective-permute-done.2.refs_0_
  12.3 0.6 shard_map.130
  12.9 0.1 collective-permute-start.3
  13.0 0.7 collective-permute-start.4
  13.7 2.3 %shard_map.128 = (bf16[1152,128]{1,0:T(8,128)(2,1)}, f32[8,128]{1,0:T(8,128)S(1)}) custom-call(bf16[3,3,3,32,32]{4,3,2,1,0:T(8,128)(2,1)} %w1_ref.1, bf16[3,3,3,32,32]{4,3,2,1,0:T(8,128)(2,1)} %w2_ref.1, f32[1,32]{1,0:T(1,128)} %bitcast.15, f32[1,32]{1,0:T(1,128)} %bitcast.16, f32[1,32]{1,0:T(1,128)} %bitcast.17, f32[1,32]{1,0:T(1,128)} %bitcast.18), custom_call_target="tpu_custom_call" | custom-call | flops 2147483648 | bytes 1048576 | tf_op jit(solution)/shard_map/pallas_call | solution.py:31
  16.0 0.0 collective-permute-done.3.a_ref
  16.0 0.0 collective-permute-done.4.b_ref
  16.1 0.7 shard_map.131
  16.8 1.3 %collective-permute-start.6 = (bf16[1168,128]{1,0:T(8,128)(2,1)S(1)}, bf16[1168,128]{1,0:T(8,128)(2,1)S(1)}, u32[]{:S(2)}, u32[]{:S(2)}) collective-permute-start(bf16[1168,128]{1,0:T(8,128)(2,1)S(1)} %get-tuple-element.46.refs_4_), channel_id=1, source_target_pairs={{8,0},{16,8},{24,16},{9,1},{17,9},{25,17},{10,2},{18,10},{26,18},{... | collective-permute-start | bytes 897032 | tf_op jit(solution)/shard_map/ppermute | solution.py:492
  18.1 4.6 %collective-permute-start.5 = (bf16[1168,128]{1,0:T(8,128)(2,1)S(1)}, bf16[1168,128]{1,0:T(8,128)(2,1)S(1)}, u32[]{:S(2)}, u32[]{:S(2)}) collective-permute-start(bf16[1168,128]{1,0:T(8,128)(2,1)S(1)} %get-tuple-element.46.refs_4_), channel_id=1, source_target_pairs={{0,8},{8,16},{16,24},{1,9},{9,17},{17,25},{2,10},{10,18},{18,26},{... | collective-permute-start | bytes 897032 | tf_op jit(solution)/shard_map/ppermute | solution.py:490
  22.7 0.0 collective-permute-done.1.refs_2_
  22.7 0.2 collective-permute-done.refs_0_
  22.8 2.6 %collective-permute-done.6.refs_5_ = bf16[1168,128]{1,0:T(8,128)(2,1)S(1)} collective-permute-done((bf16[1168,128]{1,0:T(8,128)(2,1)S(1)}, bf16[1168,128]{1,0:T(8,128)(2,1)S(1)}, u32[]{:S(2)}, u32[]{:S(2)}) %collective-permute-start.6) | collective-permute-done | bytes 299040 | tf_op jit(solution)/shard_map/ppermute | solution.py:492
  25.4 1.6 %collective-permute-done.5.refs_3_ = bf16[1168,128]{1,0:T(8,128)(2,1)S(1)} collective-permute-done((bf16[1168,128]{1,0:T(8,128)(2,1)S(1)}, bf16[1168,128]{1,0:T(8,128)(2,1)S(1)}, u32[]{:S(2)}, u32[]{:S(2)}) %collective-permute-start.5) | collective-permute-done | bytes 299040 | tf_op jit(solution)/shard_map/ppermute | solution.py:490
  27.1 5.4 %shard_map.132 = (f32[592,768]{1,0:T(8,128)S(1)}, bf16[880,896]{1,0:T(8,128)(2,1)}, bf16[880,896]{1,0:T(8,128)(2,1)}, f32[32,1,128]{2,1,0:T(1,128)}, f32[8,128]{1,0:T(8,128)S(1)}) custom-call(bf16[1152,128]{1,0:T(8,128)(2,1)} %get-tuple-element.38.w_ref, bf16[512,512]{1,0:T(8,128)(2,1)S(1)} %collective-permute-done.refs_0_, ...), custom_call_target="tpu_custom_call" | custom-call | flops 1073741824 | bytes 1048576 | tf_op jit(solution)/shard_map/pallas_call | solution.py:31
  32.5 9.1 %all-to-all-start = ((f32[32,1,128]{2,1,0:T(1,128)}), f32[32,1,128]{2,1,0:T(1,128)S(1)}, u32[]{:S(2)}, u32[]{:S(2)}) async-start(f32[32,1,128]{2,1,0:T(1,128)} %get-tuple-element.51), calls=%async_computation | async-start | bytes 32768 | tf_op jit(solution)/shard_map/all_to_all | solution.py:47
  41.7 5.1 %shard_map.133 = (f32[592,640]{1,0:T(8,128)}, f32[8,128]{1,0:T(8,128)S(1)}) custom-call(bf16[1152,128]{1,0:T(8,128)(2,1)} %get-tuple-element.38.w_ref, f32[8,128]{1,0:T(8,128)S(1)} %get-tuple-element.47.after.m_ref, bf16[880,896]{1,0:T(8,128)(2,1)} %get-tuple-element.48.x_far), custom_call_target="tpu_custom_call" | custom-call | flops 4294967296 | bytes 1048576 | tf_op jit(solution)/shard_map/pallas_call | solution.py:31
  46.7 2.1 %all-to-all-done.st_in = f32[32,1,128]{2,1,0:T(1,128)S(1)} async-done(((f32[32,1,128]{2,1,0:T(1,128)}), f32[32,1,128]{2,1,0:T(1,128)S(1)}, u32[]{:S(2)}, u32[]{:S(2)}) %all-to-all-start) | async-done | bytes 16416 | tf_op jit(solution)/shard_map/all_to_all | solution.py:47
  48.8 4.3 %shard_map.134 = (bf16[592,768]{1,0:T(8,128)(2,1)}, f32[304,640]{1,0:T(8,128)S(1)}, f32[32,3,128]{2,1,0:T(4,128)}, f32[8,128]{1,0:T(8,128)S(1)}) custom-call(s32[9]{0:T(128)S(1)} %stack.39.bound, f32[592,768]{1,0:T(8,128)S(1)} %get-tuple-element.50.c_ref, bf16[1152,128]{1,0:T(8,128)(2,1)} %get-tuple-element.38.w_ref, f32[32,1,128]{2,1,0:T(1,128)S(1)} %all-to-all-done.st_in, ...), custom_call_target="tpu_custom_call" | custom-call | flops 1073741824 | bytes 1048576 | tf_op jit(solution)/shard_map/pallas_call | solution.py:31
  53.1 3.9 %all-to-all-start.1 = ((f32[32,3,128]{2,1,0:T(4,128)}), f32[32,3,128]{2,1,0:T(4,128)S(1)}, u32[]{:S(2)}, u32[]{:S(2)}) async-start(f32[32,3,128]{2,1,0:T(4,128)} %get-tuple-element.53), calls=%async_computation.1 | async-start | bytes 131072 | tf_op jit(solution)/shard_map/all_to_all | solution.py:47
  57.0 2.7 %shard_map.135.t_ref = f32[224,128]{1,0:T(8,128)S(1)} custom-call(f32[592,768]{1,0:T(8,128)S(1)} %get-tuple-element.50.c_ref, f32[32,1,128]{2,1,0:T(1,128)S(1)} %all-to-all-done.st_in, bf16[880,896]{1,0:T(8,128)(2,1)} %get-tuple-element.56.x_far, f32[8,128]{1,0:T(8,128)S(1)} %get-tuple-element.57.after), custom_call_target="tpu_custom_call" | custom-call | flops 4294967296 | bytes 1048576 | tf_op jit(solution)/shard_map/pallas_call | solution.py:31
  59.8 4.7 %all-to-all-done.1.st_in.plain_ref = f32[32,3,128]{2,1,0:T(4,128)S(1)} async-done(((f32[32,3,128]{2,1,0:T(4,128)}), f32[32,3,128]{2,1,0:T(4,128)S(1)}, u32[]{:S(2)}, u32[]{:S(2)}) %all-to-all-start.1) | async-done | bytes 49184 | tf_op jit(solution)/shard_map/all_to_all | solution.py:47
  64.5 1.4 %shard_map.136 = (f32[32,8,128]{2,1,0:T(8,128)}, f32[8,128]{1,0:T(8,128)S(1)}) custom-call(f32[304,640]{1,0:T(8,128)S(1)} %get-tuple-element.54.c_ref, f32[32,3,128]{2,1,0:T(4,128)S(1)} %all-to-all-done.1.st_in.plain_ref, f32[8,128]{1,0:T(8,128)S(1)} %get-tuple-element.45.token_ref.p_ref, bf16[304,640]{1,0:T(8,128)(2,1)S(1)} %get-tuple-element.55.go_ref, ...), custom_call_target="tpu_custom_call" | custom-call | flops 134217728 | bytes 1048576 | tf_op jit(solution)/shard_map/pallas_call | solution.py:31
  65.9 2.6 %all-to-all-start.2 = ((f32[32,8,128]{2,1,0:T(8,128)}), f32[32,8,128]{2,1,0:T(8,128)S(1)}, u32[]{:S(2)}, u32[]{:S(2)}) async-start(f32[32,8,128]{2,1,0:T(8,128)} %get-tuple-element.61), calls=%async_computation.2 | async-start | bytes 262144 | tf_op jit(solution)/shard_map/all_to_all | solution.py:47
  68.5 5.3 %shard_map.137 = (f32[304,512]{1,0:T(8,128)}, f32[8,128]{1,0:T(8,128)S(1)}) custom-call(s32[9]{0:T(128)S(1)} %stack.39.bound, f32[592,640]{1,0:T(8,128)} %get-tuple-element.49.c_far, bf16[1152,128]{1,0:T(8,128)(2,1)} %get-tuple-element.38.w_ref, f32[32,3,128]{2,1,0:T(4,128)S(1)} %all-to-all-done.1.st_in.plain_ref, ...), custom_call_target="tpu_custom_call" | custom-call | flops 4294967296 | bytes 1048576 | tf_op jit(solution)/shard_map/pallas_call | solution.py:31
  73.8 3.3 %all-to-all-done.2.sums_in.early_ref.st_two = f32[32,8,128]{2,1,0:T(8,128)S(1)} async-done(((f32[32,8,128]{2,1,0:T(8,128)}), f32[32,8,128]{2,1,0:T(8,128)S(1)}, u32[]{:S(2)}, u32[]{:S(2)}) %all-to-all-start.2) | async-done | bytes 131104 | tf_op jit(solution)/shard_map/all_to_all | solution.py:47
  77.1 1.3 %shard_map.138.d_ref = bf16[304,640]{1,0:T(8,128)(2,1)S(1)} custom-call(s32[9]{0:T(128)S(1)} %stack.39.bound, f32[304,640]{1,0:T(8,128)S(1)} %get-tuple-element.54.c_ref, f32[32,3,128]{2,1,0:T(4,128)S(1)} %all-to-all-done.1.st_in.plain_ref, f32[8,128]{1,0:T(8,128)S(1)} %get-tuple-element.45.token_ref.p_ref, bf16[304,640]{1,0:T(8,128)(2,1)S(1)} %get-tuple-element.55.go_ref, ...), custom_call_target="tpu_custom_call" | custom-call | flops 134217728 | bytes 1048576 | tf_op jit(solution)/shard_map/pallas_call | solution.py:31
  78.4 1.3 %collective-permute-start.8 = (bf16[304,640]{1,0:T(8,128)(2,1)S(1)}, bf16[304,640]{1,0:T(8,128)(2,1)S(1)}, u32[]{:S(2)}, u32[]{:S(2)}) collective-permute-start(bf16[304,640]{1,0:T(8,128)(2,1)S(1)} %shard_map.138.d_ref), channel_id=1, source_target_pairs={{8,0},{16,8},{24,16},{9,1},{17,9},{25,17},{10,2},{18,10},{26,18},{... | collective-permute-start | bytes 1167368 | tf_op jit(solution)/shard_map/ppermute | solution.py:1033
  79.7 4.6 %collective-permute-start.7 = (bf16[304,640]{1,0:T(8,128)(2,1)S(1)}, bf16[304,640]{1,0:T(8,128)(2,1)S(1)}, u32[]{:S(2)}, u32[]{:S(2)}) collective-permute-start(bf16[304,640]{1,0:T(8,128)(2,1)S(1)} %shard_map.138.d_ref), channel_id=1, source_target_pairs={{0,8},{8,16},{16,24},{1,9},{9,17},{17,25},{2,10},{10,18},{18,26},{... | collective-permute-start | bytes 1167368 | tf_op jit(solution)/shard_map/ppermute | solution.py:1032
  84.3 2.5 %shard_map.139.after.gw_two = f32[224,128]{1,0:T(8,128)S(1)} custom-call(bf16[304,640]{1,0:T(8,128)(2,1)S(1)} %shard_map.138.d_ref, bf16[592,768]{1,0:T(8,128)(2,1)} %get-tuple-element.62.h_far), custom_call_target="tpu_custom_call" | custom-call | flops 4294967296 | bytes 1048576 | tf_op jit(solution)/shard_map/pallas_call | solution.py:31
  86.8 3.0 %shard_map.140.e_ref = f32[592,640]{1,0:T(8,128)S(1)} custom-call(bf16[1152,128]{1,0:T(8,128)(2,1)} %get-tuple-element.38.w_ref, bf16[304,640]{1,0:T(8,128)(2,1)S(1)} %shard_map.138.d_ref, f32[224,128]{1,0:T(8,128)S(1)} %shard_map.139.after.gw_two), custom_call_target="tpu_custom_call" | custom-call | flops 4294967296 | bytes 1048576 | tf_op jit(solution)/shard_map/pallas_call | solution.py:31
  89.8 1.0 collective-permute-done.8.high_ref
  90.8 1.2 collective-permute-done.7.low_ref
  92.0 5.3 %shard_map.141 = (f32[592,640]{1,0:T(8,128)}, f32[32,15,128]{2,1,0:T(8,128)}) custom-call(bf16[1152,128]{1,0:T(8,128)(2,1)} %get-tuple-element.38.w_ref, f32[592,768]{1,0:T(8,128)S(1)} %get-tuple-element.50.c_ref, f32[32,1,128]{2,1,0:T(1,128)S(1)} %all-to-all-done.st_in, f32[8,128]{1,0:T(8,128)S(1)} %get-tuple-element.45.token_ref.p_ref, ...), custom_call_target="tpu_custom_call" | custom-call | flops 1073741824 | bytes 1048576 | tf_op jit(solution)/shard_map/pallas_call | solution.py:31
  97.3 14.8 %all_to_all.25.late_ref.st_in.sums_in = f32[32,15,128]{2,1,0:T(8,128)S(1)} all-to-all(f32[32,15,128]{2,1,0:T(8,128)} %get-tuple-element.63), channel_id=1, replica_groups=mesh['gx'=4,'gy'=4,'gz'=2] {'gx','gy','gz'}, dimensions={0} | all-to-all | bytes 491520 | tf_op jit(solution)/shard_map/all_to_all | solution.py:47
  112.0 1.5 %shard_map.142 = (bf16[32,16,128]{2,1,0:T(8,128)(2,1)}, f32[8,128]{1,0:T(8,128)S(1)}) custom-call(s32[9]{0:T(128)S(1)} %stack.39.bound, f32[32,1,128]{2,1,0:T(1,128)S(1)} %all-to-all-done.st_in, f32[8,128]{1,0:T(8,128)S(1)} %get-tuple-element.45.token_ref.p_ref, f32[32,3,128]{2,1,0:T(4,128)S(1)} %all-to-all-done.1.st_in.plain_ref, ...), custom_call_target="tpu_custom_call" | custom-call | bytes 1048576 | tf_op jit(solution)/shard_map/pallas_call | solution.py:31
  113.5 2.6 %all-to-all-start.4 = ((bf16[32,16,128]{2,1,0:T(8,128)(2,1)}), bf16[32,16,128]{2,1,0:T(8,128)(2,1)S(1)}, u32[]{:S(2)}, u32[]{:S(2)}) async-start(bf16[32,16,128]{2,1,0:T(8,128)(2,1)} %get-tuple-element.67), calls=%async_computation.4 | async-start | bytes 262144 | tf_op jit(solution)/shard_map/all_to_all | solution.py:47
  116.1 0.0 copy-start
  116.1 4.4 %shard_map.144 = bf16[32,2,16,128]{3,2,1,0:T(8,128)(2,1)} custom-call(s32[9]{0:T(128)S(1)} %stack.39.bound, f32[592,640]{1,0:T(8,128)} %get-tuple-element.66.s_far, f32[592,768]{1,0:T(8,128)S(1)} %get-tuple-element.50.c_ref, f32[32,1,128]{2,1,0:T(1,128)S(1)} %all-to-all-done.st_in, f32[8,128]{1,0:T(8,128)S(1)} %get-tuple-element.45.token_ref.p_ref, ...), custom_call_target="tpu_custom_call" | custom-call | flops 2147483648 | bytes 1048576 | tf_op jit(solution)/shard_map/pallas_call | solution.py:31
  120.5 0.0 copy-done
  120.5 1.5 %shard_map.143 = (bf16[32,2,16,128]{3,2,1,0:T(8,128)(2,1)}, f32[4,32]{1,0:T(4,128)}) custom-call(f32[304,512]{1,0:T(8,128)S(1)} %copy-done, f32[32,15,128]{2,1,0:T(8,128)S(1)} %all_to_all.25.late_ref.st_in.sums_in, f32[32,8,128]{2,1,0:T(8,128)S(1)} %all-to-all-done.2.sums_in.early_ref.st_two, f32[8,128]{1,0:T(8,128)S(1)} %get-tuple-element.45.token_ref.p_ref, ...), custom_call_target="tpu_custom_call" | custom-call | flops 2147483648 | bytes 1048576 | tf_op jit(solution)/shard_map/pallas_call | solution.py:31
  122.0 2.7 %all-to-all-done.4.got_ref = bf16[32,16,128]{2,1,0:T(8,128)(2,1)S(1)} async-done(((bf16[32,16,128]{2,1,0:T(8,128)(2,1)}), bf16[32,16,128]{2,1,0:T(8,128)(2,1)S(1)}, u32[]{:S(2)}, u32[]{:S(2)}) %all-to-all-start.4) | async-done | bytes 131104 | tf_op jit(solution)/shard_map/all_to_all | solution.py:47
  124.7 1.1 shard_map.145
Async XLA Ops:
  3.3 8.9 %collective-permute-start.2 = (bf16[96,640]{1,0:T(8,128)(2,1)S(1)}, bf16[96,640]{1,0:T(8,128)(2,1)S(1)}, u32[]{:S(2)}, u32[]{:S(2)}) collective-permute-start(bf16[96,640]{1,0:T(8,128)(2,1)S(1)} %bitcast.14), channel_id=1, source_target_pairs={{0,1},{1,0},{2,3},{3,2},{4,5},{5,4},{6,7},{7,6},{8,9},{9,8},{10,11... | collective-permute-start | bytes 368648 | tf_op jit(solution)/shard_map/ppermute | solution.py:360
  6.4 16.3 %collective-permute-start.1 = (bf16[512,512]{1,0:T(8,128)(2,1)S(1)}, bf16[512,512]{1,0:T(8,128)(2,1)S(1)}, u32[]{:S(2)}, u32[]{:S(2)}) collective-permute-start(bf16[512,512]{1,0:T(8,128)(2,1)S(1)} %get-tuple-element.39.t_ref.refs_1_), channel_id=1, source_target_pairs={{8,0},{16,8},{24,16},{9,1},{17,9},{25,17},{10,2},{18,10},{26,18},{... | collective-permute-start | bytes 1572872 | tf_op jit(solution)/shard_map/ppermute | solution.py:367
  7.7 15.2 %collective-permute-start = (bf16[512,512]{1,0:T(8,128)(2,1)S(1)}, bf16[512,512]{1,0:T(8,128)(2,1)S(1)}, u32[]{:S(2)}, u32[]{:S(2)}) collective-permute-start(bf16[512,512]{1,0:T(8,128)(2,1)S(1)} %get-tuple-element.39.t_ref.refs_1_), channel_id=1, source_target_pairs={{0,8},{8,16},{16,24},{1,9},{9,17},{17,25},{2,10},{10,18},{18,26},{... | collective-permute-start | bytes 1572872 | tf_op jit(solution)/shard_map/ppermute | solution.py:366
  12.9 3.1 %collective-permute-start.3 = (bf16[608,128]{1,0:T(8,128)(2,1)S(1)}, bf16[608,128]{1,0:T(8,128)(2,1)S(1)}, u32[]{:S(2)}, u32[]{:S(2)}) collective-permute-start(bf16[608,128]{1,0:T(8,128)(2,1)S(1)} %get-tuple-element.42), channel_id=1, source_target_pairs={{0,2},{2,0},{4,6},{6,4},{1,3},{3,1},{5,7},{7,5},{8,10},{10,8},{12,... | collective-permute-start | bytes 466952 | tf_op jit(solution)/shard_map/ppermute | solution.py:434
  13.0 3.0 %collective-permute-start.4 = (bf16[608,128]{1,0:T(8,128)(2,1)S(1)}, bf16[608,128]{1,0:T(8,128)(2,1)S(1)}, u32[]{:S(2)}, u32[]{:S(2)}) collective-permute-start(bf16[608,128]{1,0:T(8,128)(2,1)S(1)} %get-tuple-element.43), channel_id=1, source_target_pairs={{2,4},{4,2},{3,5},{5,3},{10,12},{12,10},{11,13},{13,11},{18,20},{2... | collective-permute-start | bytes 466952 | tf_op jit(solution)/shard_map/ppermute | solution.py:435
  16.8 8.7 %collective-permute-start.6 = (bf16[1168,128]{1,0:T(8,128)(2,1)S(1)}, bf16[1168,128]{1,0:T(8,128)(2,1)S(1)}, u32[]{:S(2)}, u32[]{:S(2)}) collective-permute-start(bf16[1168,128]{1,0:T(8,128)(2,1)S(1)} %get-tuple-element.46.refs_4_), channel_id=1, source_target_pairs={{8,0},{16,8},{24,16},{9,1},{17,9},{25,17},{10,2},{18,10},{26,18},{... | collective-permute-start | bytes 897032 | tf_op jit(solution)/shard_map/ppermute | solution.py:492
  18.1 9.0 %collective-permute-start.5 = (bf16[1168,128]{1,0:T(8,128)(2,1)S(1)}, bf16[1168,128]{1,0:T(8,128)(2,1)S(1)}, u32[]{:S(2)}, u32[]{:S(2)}) collective-permute-start(bf16[1168,128]{1,0:T(8,128)(2,1)S(1)} %get-tuple-element.46.refs_4_), channel_id=1, source_target_pairs={{0,8},{8,16},{16,24},{1,9},{9,17},{17,25},{2,10},{10,18},{18,26},{... | collective-permute-start | bytes 897032 | tf_op jit(solution)/shard_map/ppermute | solution.py:490
  32.5 16.3 %all-to-all-start = ((f32[32,1,128]{2,1,0:T(1,128)}), f32[32,1,128]{2,1,0:T(1,128)S(1)}, u32[]{:S(2)}, u32[]{:S(2)}) async-start(f32[32,1,128]{2,1,0:T(1,128)} %get-tuple-element.51), calls=%async_computation | async-start | bytes 32768 | tf_op jit(solution)/shard_map/all_to_all | solution.py:47
  53.1 11.4 %all-to-all-start.1 = ((f32[32,3,128]{2,1,0:T(4,128)}), f32[32,3,128]{2,1,0:T(4,128)S(1)}, u32[]{:S(2)}, u32[]{:S(2)}) async-start(f32[32,3,128]{2,1,0:T(4,128)} %get-tuple-element.53), calls=%async_computation.1 | async-start | bytes 131072 | tf_op jit(solution)/shard_map/all_to_all | solution.py:47
  65.9 11.2 %all-to-all-start.2 = ((f32[32,8,128]{2,1,0:T(8,128)}), f32[32,8,128]{2,1,0:T(8,128)S(1)}, u32[]{:S(2)}, u32[]{:S(2)}) async-start(f32[32,8,128]{2,1,0:T(8,128)} %get-tuple-element.61), calls=%async_computation.2 | async-start | bytes 262144 | tf_op jit(solution)/shard_map/all_to_all | solution.py:47
  78.4 12.4 %collective-permute-start.8 = (bf16[304,640]{1,0:T(8,128)(2,1)S(1)}, bf16[304,640]{1,0:T(8,128)(2,1)S(1)}, u32[]{:S(2)}, u32[]{:S(2)}) collective-permute-start(bf16[304,640]{1,0:T(8,128)(2,1)S(1)} %shard_map.138.d_ref), channel_id=1, source_target_pairs={{8,0},{16,8},{24,16},{9,1},{17,9},{25,17},{10,2},{18,10},{26,18},{... | collective-permute-start | bytes 1167368 | tf_op jit(solution)/shard_map/ppermute | solution.py:1033
  79.7 12.3 %collective-permute-start.7 = (bf16[304,640]{1,0:T(8,128)(2,1)S(1)}, bf16[304,640]{1,0:T(8,128)(2,1)S(1)}, u32[]{:S(2)}, u32[]{:S(2)}) collective-permute-start(bf16[304,640]{1,0:T(8,128)(2,1)S(1)} %shard_map.138.d_ref), channel_id=1, source_target_pairs={{0,8},{8,16},{16,24},{1,9},{9,17},{17,25},{2,10},{10,18},{18,26},{... | collective-permute-start | bytes 1167368 | tf_op jit(solution)/shard_map/ppermute | solution.py:1032
  113.5 11.2 %all-to-all-start.4 = ((bf16[32,16,128]{2,1,0:T(8,128)(2,1)}), bf16[32,16,128]{2,1,0:T(8,128)(2,1)S(1)}, u32[]{:S(2)}, u32[]{:S(2)}) async-start(bf16[32,16,128]{2,1,0:T(8,128)(2,1)} %get-tuple-element.67), calls=%async_computation.4 | async-start | bytes 262144 | tf_op jit(solution)/shard_map/all_to_all | solution.py:47
  116.1 4.4 %copy-start = (f32[304,512]{1,0:T(8,128)S(1)}, f32[304,512]{1,0:T(8,128)}, u32[]{:S(2)}) copy-start(f32[304,512]{1,0:T(8,128)} %get-tuple-element.59.c_ref) | copy-start | bytes 1867780
